TPU v7x, 16 devices: a 4x2x1 block of a 4x4x8 slice. The times are simulated.
16 devices in a mesh: rep: 2 (over y, z), dp: 8 (over x, core).
Axes of the slice: x: 4, y: 2, z: 1, core: 2. Of those that a mesh axis runs over, the one named last changes fastest.
The devices are a block of a 4x4x8 slice.
Arguments:
- g_w_gate: bfloat16 [16, 2, 1024, 3200], P(('rep', 'dp')), parts along dimension 0
- g_w_up: bfloat16 [16, 2, 1024, 3200], P(('rep', 'dp')), parts along dimension 0
- g_w_down: bfloat16 [16, 2, 3200, 1024], P(('rep', 'dp')), parts along dimension 0
- w_gate: bfloat16 [2, 1024, 3200], replicated
- w_up: bfloat16 [2, 1024, 3200], replicated
- w_down: bfloat16 [2, 3200, 1024], replicated
- m_w_gate: float32 [2, 1024, 3200], P(None, 'dp')
- m_w_up: float32 [2, 1024, 3200], P(None, 'dp')
- m_w_down: float32 [2, 3200, 1024], P(None, 'dp')
- v_w_gate: float32 [2, 1024, 3200], P(None, 'dp')
- v_w_up: float32 [2, 1024, 3200], P(None, 'dp')
- v_w_down: float32 [2, 3200, 1024], P(None, 'dp')
Outputs:
- output 1: bfloat16 [4, 1024, 3200], P('rep'), parts along dimension 0
- output 2: bfloat16 [4, 1024, 3200], P('rep'), parts along dimension 0
- output 3: bfloat16 [4, 3200, 1024], P('rep'), parts along dimension 0
- output 4: float32 [4, 1024, 3200], P('rep', 'dp'), parts along dimension 0
- output 5: float32 [4, 1024, 3200], P('rep', 'dp'), parts along dimension 0
- output 6: float32 [4, 3200, 1024], P('rep', 'dp'), parts along dimension 0
- output 7: float32 [4, 1024, 3200], P('rep', 'dp'), parts along dimension 0
- output 8: float32 [4, 1024, 3200], P('rep', 'dp'), parts along dimension 0
- output 9: float32 [4, 3200, 1024], P('rep', 'dp'), parts along dimension 0
There are 2 independent parts. A program takes and returns all parts, laid end to end along the dimension named above; an argument that names none is the same for every part.
All inputs are finite; a program needn't handle non-finite values.
Results may differ from a plain program's by a relative error of at most 0.022.
Values are sent between devices in bfloat16 or wider.
A program may use at most 768 MiB of HBM per device.

v0:
```python
import jax
import jax.numpy as jnp
from jax import lax
from jax.sharding import PartitionSpec as P


def adamw(w, m, v, g):
    m = 0.9 * m + 0.1 * g
    v = 0.95 * v + 0.05 * g * g
    step = m * lax.rsqrt(v + 1e-8) + 0.1 * w
    return (w - 0.02 * step).astype(jnp.bfloat16), m, v


def solution(mesh):
    def step(*arrays):
        terms, weights, m, v = (arrays[i : i + 3] for i in (0, 3, 6, 9))
        gradients = [lax.psum_scatter(t[0], "dp", scatter_dimension=1, tiled=True).astype(jnp.float32) for t in terms]
        me = lax.axis_index("dp")
        own = [lax.dynamic_slice_in_dim(w, me * one.shape[1], one.shape[1], 1).astype(jnp.float32) for w, one in zip(weights, m, strict=True)]
        new = [adamw(w, m, v, g) for w, m, v, g in zip(own, m, v, gradients, strict=True)]
        whole = [lax.all_gather(one[0], "dp", axis=1, tiled=True) for one in new]
        return (*whole, *(one[1] for one in new), *(one[2] for one in new))

    all_of, cut = P(None, None, None), P(None, "dp", None)
    return jax.shard_map(
        step,
        mesh=mesh,
        in_specs=(P(("rep", "dp"), None, None, None),) * 3 + (all_of,) * 3 + (cut,) * 6,
        out_specs=(P("rep", None, None),) * 3 + (P("rep", "dp", None),) * 6,
        check_vma=False,
    )
```

profile of v0, /device:TPU:113, one launch (start us, length us, event | category | flops | bytes accessed | tf_op | source)
XLA Modules:
  0.0 466.9 jit_solution(433090236659527310)
XLA Ops:
  7.2 0.1 reduce-scatter.8.cloned.1.call-start
  7.3 0.7 reduce-scatter.8.cloned.1.call-update
  8.0 0.1 reduce-scatter.6.cloned.1.call-start
  8.1 0.7 reduce-scatter.6.cloned.1.call-update
  8.8 0.1 reduce-scatter.4.cloned.1.call-start
  8.9 0.0 copy-start.1
  8.9 0.7 reduce-scatter.4.cloned.1.call-update
  9.6 0.1 all-gather.8.cloned.1.call-start
  9.7 74.0 %reduce-scatter.8.cloned.1.call-done = bf16[2,400,1024]{2,1,0:T(8,128)(2,1)} async-done(((bf16[2,3200,1024]{2,1,0:T(8,128)(2,1)}), bf16[2,400,1024]{2,1,0:T(8,128)(2,1)}) %reduce-scatter.8.cloned.1.call-update) | async-done | bytes 1638416 | tf_op jit(solution)/shard_map/reduce_scatter | solution.py:17
  83.7 0.0 copy-done.1
  83.7 5.7 %fusion.10 = (bf16[2,400,1024]{2,1,0:T(8,128)(2,1)}, f32[2,400,1024]{2,1,0:T(8,128)}, f32[2,400,1024]{2,1,0:T(8,128)}) fusion(bf16[2,3200,1024]{2,1,0:T(8,128)(2,1)} %param.17, s32[]{:T(128)S(6)} %select_n.8, bf16[2,400,1024]{2,1,0:T(8,128)(2,1)} %reduce-scatter.8.cloned.1.call-done, f32[2,400,1024]{2,1,0:T(8,128)S(1)} %copy-done.1, f32[2,400,1024]{2,1,0:T(8,128)} %param.20), kind=kLoop, calls=%fused_computation.22 | loop fusion | flops 13107200 | bytes 18022404 | tf_op jit(solution)/shard_map/convert_element_type | solution.py:11
  89.4 0.1 all-gather.8.cloned.1.call-update
  89.5 0.1 all-gather.6.cloned.1.call-start
  89.5 67.0 %reduce-scatter.6.cloned.1.call-done = bf16[2,128,3200]{2,1,0:T(8,128)(2,1)} async-done(((bf16[2,1024,3200]{2,1,0:T(8,128)(2,1)}), bf16[2,128,3200]{2,1,0:T(8,128)(2,1)}) %reduce-scatter.6.cloned.1.call-update) | async-done | bytes 1638416 | tf_op jit(solution)/shard_map/reduce_scatter | solution.py:17
  156.5 0.0 copy-start.2
  156.5 6.7 %fusion.6 = (bf16[2,128,3200]{2,1,0:T(8,128)(2,1)}, f32[2,128,3200]{2,1,0:T(8,128)}, f32[2,128,3200]{2,1,0:T(8,128)}) fusion(bf16[2,1024,3200]{2,1,0:T(8,128)(2,1)} %param.16, s32[]{:T(128)S(6)} %select_n.7, bf16[2,128,3200]{2,1,0:T(8,128)(2,1)} %reduce-scatter.6.cloned.1.call-done, f32[2,128,3200]{2,1,0:T(8,128)} %param.22, f32[2,128,3200]{2,1,0:T(8,128)} %param.19), kind=kLoop, calls=%fused_computation.18 | loop fusion | flops 13107200 | bytes 18022404 | tf_op jit(solution)/shard_map/convert_element_type | solution.py:11
  163.2 0.1 all-gather.6.cloned.1.call-update
  163.3 0.1 all-gather.4.cloned.1.call-start
  163.4 66.0 %reduce-scatter.4.cloned.1.call-done = bf16[2,128,3200]{2,1,0:T(8,128)(2,1)} async-done(((bf16[2,1024,3200]{2,1,0:T(8,128)(2,1)}), bf16[2,128,3200]{2,1,0:T(8,128)(2,1)}) %reduce-scatter.4.cloned.1.call-update) | async-done | bytes 1638416 | tf_op jit(solution)/shard_map/reduce_scatter | solution.py:17
  229.4 0.0 copy-done.2
  229.4 5.6 %fusion.2 = (bf16[2,128,3200]{2,1,0:T(8,128)(2,1)}, f32[2,128,3200]{2,1,0:T(8,128)}, f32[2,128,3200]{2,1,0:T(8,128)}) fusion(bf16[2,1024,3200]{2,1,0:T(8,128)(2,1)} %param.15, s32[]{:T(128)S(6)} %select_n.7, bf16[2,128,3200]{2,1,0:T(8,128)(2,1)} %reduce-scatter.4.cloned.1.call-done, f32[2,128,3200]{2,1,0:T(8,128)S(1)} %copy-done.2, f32[2,128,3200]{2,1,0:T(8,128)} %param.18), kind=kLoop, calls=%fused_computation.14 | loop fusion | flops 13107200 | bytes 18022404 | tf_op jit(solution)/shard_map/convert_element_type | solution.py:11
  235.0 0.1 all-gather.4.cloned.1.call-update
  235.1 62.4 %all-gather.8.cloned.1.call-done = bf16[2,3200,1024]{2,1,0:T(8,128)(2,1)} async-done(((bf16[2,400,1024]{2,1,0:T(8,128)(2,1)}), bf16[2,3200,1024]{2,1,0:T(8,128)(2,1)}) %all-gather.8.cloned.1.call-update) | async-done | bytes 13107216 | tf_op jit(solution)/shard_map/all_gather | solution.py:21
  297.4 67.9 %all-gather.6.cloned.1.call-done = bf16[2,1024,3200]{2,1,0:T(8,128)(2,1)} async-done(((bf16[2,128,3200]{2,1,0:T(8,128)(2,1)}), bf16[2,1024,3200]{2,1,0:T(8,128)(2,1)}) %all-gather.6.cloned.1.call-update) | async-done | bytes 13107216 | tf_op jit(solution)/shard_map/all_gather | solution.py:21
  365.3 67.9 %all-gather.4.cloned.1.call-done = bf16[2,1024,3200]{2,1,0:T(8,128)(2,1)} async-done(((bf16[2,128,3200]{2,1,0:T(8,128)(2,1)}), bf16[2,1024,3200]{2,1,0:T(8,128)(2,1)}) %all-gather.4.cloned.1.call-update) | async-done | bytes 13107216 | tf_op jit(solution)/shard_map/all_gather | solution.py:21
  433.3 0.0 copy-start
  433.3 0.0 slice-start
  433.3 0.0 slice-start.1
  433.3 0.0 slice-start.2
  433.3 12.7 %copy.24 = bf16[2,1024,3200]{2,1,0:T(8,128)(2,1)} copy(bf16[2,1024,3200]{2,1,0:T(8,128)(2,1)} %all-gather.4.cloned.1.call-done) | data formatting | bytes 26214400
  445.9 0.0 copy-done
  446.0 0.0 slice-start.3
  446.0 6.6 %copy.25 = bf16[2,1024,3200]{2,1,0:T(8,128)(2,1)} copy(bf16[2,1024,3200]{2,1,0:T(8,128)(2,1)S(1)} %copy-done) | data formatting | bytes 26214400
  452.6 0.0 slice-done
  452.6 1.2 slice-done.1
  453.8 1.2 slice-done.2
  455.0 0.1 slice-done.3
  455.1 4.9 %copy.26 = bf16[2,3200,1024]{2,1,0:T(8,128)(2,1)} copy(bf16[2,3200,1024]{2,1,0:T(8,128)(2,1)S(1)} %bitcast.7) | data formatting | bytes 26214400
  (1 shorter events, 0.0 us)
Async XLA Ops:
  7.2 76.5 %reduce-scatter.8.cloned.1.call-start = ((), (), s32[]{:S(2)}) async-start(), calls=%async_computation.7 | async-start | bytes 14745600 | tf_op jit(solution)/shard_map/reduce_scatter | solution.py:17
  8.0 148.5 %reduce-scatter.6.cloned.1.call-start = ((), (), s32[]{:S(2)}) async-start(), calls=%async_computation.5 | async-start | bytes 14745600 | tf_op jit(solution)/shard_map/reduce_scatter | solution.py:17
  8.8 220.6 %reduce-scatter.4.cloned.1.call-start = ((), (), s32[]{:S(2)}) async-start(), calls=%async_computation.3 | async-start | bytes 14745600 | tf_op jit(solution)/shard_map/reduce_scatter | solution.py:17
  8.9 74.8 %copy-start.1 = (f32[2,400,1024]{2,1,0:T(8,128)S(1)}, f32[2,400,1024]{2,1,0:T(8,128)}, u32[]{:S(2)}) copy-start(f32[2,400,1024]{2,1,0:T(8,128)} %param.23) | copy-start | bytes 9830404
  9.6 287.8 %all-gather.8.cloned.1.call-start = ((), (), s32[]{:S(2)}) async-start(), calls=%async_computation.8 | async-start | bytes 14745600 | tf_op jit(solution)/shard_map/all_gather | solution.py:21
  89.5 275.9 %all-gather.6.cloned.1.call-start = ((), (), s32[]{:S(2)}) async-start(), calls=%async_computation.6 | async-start | bytes 14745600 | tf_op jit(solution)/shard_map/all_gather | solution.py:21
  156.5 72.9 %copy-start.2 = (f32[2,128,3200]{2,1,0:T(8,128)S(1)}, f32[2,128,3200]{2,1,0:T(8,128)}, u32[]{:S(2)}) copy-start(f32[2,128,3200]{2,1,0:T(8,128)} %param.21) | copy-start | bytes 9830404
  163.3 270.0 %all-gather.4.cloned.1.call-start = ((), (), s32[]{:S(2)}) async-start(), calls=%async_computation.4 | async-start | bytes 14745600 | tf_op jit(solution)/shard_map/all_gather | solution.py:21
  433.3 12.7 %copy-start = (bf16[2,1024,3200]{2,1,0:T(8,128)(2,1)S(1)}, bf16[2,1024,3200]{2,1,0:T(8,128)(2,1)}, u32[]{:S(2)}) copy-start(bf16[2,1024,3200]{2,1,0:T(8,128)(2,1)} %all-gather.6.cloned.1.call-done) | copy-start | bytes 39321604
  433.3 19.4 %slice-start = ((s8[13107200]{0:T(1024)(128)(4,1)}), s8[4194304]{0:T(1024)(128)(4,1)S(1)}, s32[]{:S(2)}) async-start(s8[13107200]{0:T(1024)(128)(4,1)} %bitcast.6), calls=%async_computation.9 | async-start | bytes 8388608
  433.3 20.5 %slice-start.1 = ((s8[13107200]{0:T(1024)(128)(4,1)}), s8[4194304]{0:T(1024)(128)(4,1)S(1)}, s32[]{:S(2)}) async-start(s8[13107200]{0:T(1024)(128)(4,1)} %bitcast.6), calls=%async_computation.10 | async-start | bytes 8388608
  433.3 21.7 %slice-start.2 = ((s8[13107200]{0:T(1024)(128)(4,1)}), s8[4194304]{0:T(1024)(128)(4,1)S(1)}, s32[]{:S(2)}) async-start(s8[13107200]{0:T(1024)(128)(4,1)} %bitcast.6), calls=%async_computation.11 | async-start | bytes 8388608
  446.0 9.1 %slice-start.3 = ((s8[13107200]{0:T(1024)(128)(4,1)}), s8[524288]{0:T(1024)(128)(4,1)S(1)}, s32[]{:S(2)}) async-start(s8[13107200]{0:T(1024)(128)(4,1)} %bitcast.6), calls=%async_computation.12 | async-start | bytes 1048576
Sparse Core Ops, SparseCore 0:
  10.3 73.3 reduce-scatter.7
  86.0 70.5 reduce-scatter.5
  158.8 70.5 reduce-scatter.3
  231.4 65.9 all-gather.7
  299.4 65.8 all-gather.5
  367.3 65.8 all-gather.3
where the time goes:
time: 467 us
  waiting for transfers between devices  408 us (87%)
  local copies, waits for them, and re-layouts  26.8 us (6%)
  other arithmetic  18 us (4%)
  between operations  14.2 us (3%)
    reduce_scatter x3, waiting for transfers between devices, step(): lax.psum_scatter(t[0], 'dp', scatter_dimension=1, tiled=True)  207 us
    all_gather x3, waiting for transfers between devices, step(): whole = [lax.all_gather(one[0], 'dp', axis=1, tiled=True) for one in new]  198 us
    unnamed x17, local copies, waits for them, and re-layouts  26.8 us
    convert_element_type x3, other arithmetic, adamw(): return ((w - 0.02 * step).astype(jnp.bfloat16), m, v)  18 us
  transfers between devices with their start and end apart: 6, of which 6 were waited for; matrix products, arithmetic and copies ran while one was open for 4% of the time, Pallas kernels for 0%

commit v1 on v0

v1 whole, which is shorter than its diff:
```python
import functools

import jax
import jax.numpy as jnp
from jax import lax
from jax.experimental import pallas as pl
from jax.experimental.pallas import tpu as pltpu
from jax.sharding import PartitionSpec as P

MESH = pl.DeviceIdType.MESH
F32, BF16 = jnp.float32, jnp.bfloat16
CHIPS = 4
OPPOSITE, RIGHT, LEFT, OWN = range(4)
OFFSET = (2, 1, 3, 0)


def adamw(w, m, v, g):
    m = 0.9 * m + 0.1 * g
    v = 0.95 * v + 0.05 * g * g
    step = m * lax.rsqrt(v + 1e-8) + 0.1 * w
    return (w - 0.02 * step).astype(BF16), m, v


def rows_16(rows, cols, width, body):
    start, stop = rows

    @pl.loop(0, (stop - start) // 16)
    def _(t):
        r = pl.ds(pl.multiple_of(start + t * 16, 16), 16)
        for c in range(0, cols, width):
            body(r, pl.ds(c, width))


class Chunk:
    def __init__(self, number, which, layer, kind, place, block):
        self.number, self.which, self.layer = number, which, layer
        self.kind, self.place = kind, place
        self.block, self.cols = block
        half = self.block // 32 * 16
        if self.block - half != half and layer % 2 == 0:
            half = self.block - half
        self.half = half
        self.width = 640 if self.cols % 640 == 0 else 512

    def rows(self, part):
        return {"a": (0, self.half), "b": (self.half, self.block), "ab": (0, self.block)}[part]


def chunks_of(shapes):
    kinds, chunks, used = [], [], []
    for which, (layers, rows, cols) in enumerate(shapes):
        block = (rows // (2 * CHIPS), cols)
        if block not in kinds:
            kinds.append(block)
            used.append(0)
        kind = kinds.index(block)
        for layer in range(layers):
            chunks.append(Chunk(len(chunks), which, layer, kind, used[kind], block))
            used[kind] += 1
    return chunks, kinds, used


def exchange(chunks, kinds, tail, *refs):
    it = iter(refs)
    take = lambda n: [next(it) for _ in range(n)]
    g, w, m, v = take(3), take(3), take(3), take(3)
    out, new_m, new_v = take(3), take(3), take(3)
    nk = len(kinds)
    peer, pass_in, near_in, own, w_in, m_in, v_in = (take(nk) for _ in range(7))
    (x_send, x_recv, a_send, a_recv, b_send, b_recv, own_sem, in_sem, out_sem,
     g1_send, g1_recv, g2_send, g2_recv, gx_send, gx_recv) = it
    n = len(chunks)

    me = lax.axis_index("dp")
    chip, core = me // 2, me % 2
    right = lax.rem(chip + 1, CHIPS) * 2 + core
    left = lax.rem(chip + CHIPS - 1, CHIPS) * 2 + core
    other = chip * 2 + (1 - core)
    chip_at = [lax.rem(chip + OFFSET[r], CHIPS) for r in range(4)]

    barrier = pltpu.get_barrier_semaphore()
    for d in (right, left, other):
        pl.semaphore_signal(barrier, inc=1, device_id={"dp": d}, device_id_type=MESH)

    pending = []

    def remote(src, dst, send, recv, to):
        copy = pltpu.make_async_remote_copy(
            src_ref=src, dst_ref=dst, send_sem=send, recv_sem=recv, device_id={"dp": to}, device_id_type=MESH)
        copy.start()
        pending.append(copy)
        return copy

    def block_rows(c, block, part="ab"):
        start, stop = c.rows(part)
        return pl.ds(pl.multiple_of(block * c.block + start, 16), stop - start)

    order = [(OPPOSITE, c) for c in chunks]
    for c in chunks:
        order += [(RIGHT, c), (LEFT, c)]
    order += [(OWN, c) for c in chunks]
    slots, seen = {}, [0] * nk
    for r, c in order:
        slots[r, c.number] = seen[c.kind] % 3
        seen[c.kind] += 1

    def own_load(p):
        r, c = order[p]
        return pltpu.make_async_copy(
            g[c.which].at[c.layer, block_rows(c, chip_at[r] * 2 + core), :],
            own[c.kind].at[slots[r, c.number]], own_sem.at[r * n + c.number])

    def state_loads(c):
        s = c.place % 2
        return [
            pltpu.make_async_copy(w[c.which].at[c.layer, block_rows(c, me), :], w_in[c.kind].at[s], in_sem.at[c.number * 3]),
            pltpu.make_async_copy(m[c.which].at[c.layer], m_in[c.kind].at[s], in_sem.at[c.number * 3 + 1]),
            pltpu.make_async_copy(v[c.which].at[c.layer], v_in[c.kind].at[s], in_sem.at[c.number * 3 + 2]),
        ]

    own_load(0).start()
    own_load(1).start()
    pl.semaphore_wait(barrier, 3)

    x = {}

    def swap(r, c):
        x[r, c.number] = remote(
            g[c.which].at[c.layer, block_rows(c, chip_at[r] * 2 + (1 - core)), :], peer[c.kind].at[r, c.place],
            x_send.at[r * n + c.number], x_recv.at[r * n + c.number], other)

    for c in chunks:
        swap(OPPOSITE, c)

    position = [0]

    def take_own(r, c):
        p = position[0]
        position[0] += 1
        assert order[p] == (r, c)
        if p + 2 < len(order):
            own_load(p + 2).start()
        own_load(p).wait()
        x[r, c.number].wait_recv()
        return own[c.kind].at[slots[r, c.number]], peer[c.kind].at[r, c.place]

    def add(c, part, mine, theirs, *more):
        def tile(rows, cols):
            total = mine[rows, cols].astype(F32) + theirs[rows, cols].astype(F32)
            for ref in more:
                total += ref[rows, cols].astype(F32)
            theirs[rows, cols] = total.astype(BF16)

        rows_16(c.rows(part), c.cols, c.width, tile)

    def part_of(ref, c, part):
        start, stop = c.rows(part)
        return ref.at[pl.ds(start, stop - start), :]

    step0 = {}
    for c in chunks:
        mine, theirs = take_own(OPPOSITE, c)
        for part, to, side in (("a", right, 0), ("b", left, 1)):
            add(c, part, mine, theirs)
            step0[side, c.number] = remote(
                part_of(theirs, c, part), part_of(pass_in[c.kind].at[c.place], c, part),
                a_send.at[side * n + c.number], a_recv.at[side * n + c.number], to)
        swap(RIGHT, c)
        swap(LEFT, c)

    step1 = {}
    for c in chunks:
        for r, to, side, parts in ((RIGHT, right, 0, "ab"), (LEFT, left, 1, "ba")):
            mine, theirs = take_own(r, c)
            for k, part in enumerate(parts):
                if k == 0:
                    step0[side, c.number].wait_recv()
                    add(c, part, mine, theirs, pass_in[c.kind].at[c.place])
                else:
                    add(c, part, mine, theirs)
                s = (side * n + c.number) * 2 + k
                step1[side, c.number, k] = remote(
                    part_of(theirs, c, part), part_of(near_in[c.kind].at[side, c.place], c, part),
                    b_send.at[s], b_recv.at[s], to)
        swap(OWN, c)

    for c in chunks[:2]:
        for copy in state_loads(c):
            copy.start()
    hop1, crossing, stores = {}, [], {}

    def cross(ref_rows, c, s):
        crossing.append(remote(
            out[c.which].at[c.layer, ref_rows, :], out[c.which].at[c.layer, ref_rows, :], gx_send.at[s], gx_recv.at[s], other))

    for c in chunks:
        mine, theirs = take_own(OWN, c)
        for copy in state_loads(c):
            copy.wait()
        for side in (0, 1):
            for k in (0, 1):
                step1[side, c.number, k].wait_recv()
        s = c.place % 2
        from_left, from_right = near_in[c.kind].at[0, c.place], near_in[c.kind].at[1, c.place]
        w_ref, m_ref, v_ref = w_in[c.kind].at[s], m_in[c.kind].at[s], v_in[c.kind].at[s]

        def tile(rows, cols):
            total = mine[rows, cols].astype(F32) + theirs[rows, cols].astype(F32)
            total += from_left[rows, cols].astype(F32) + from_right[rows, cols].astype(F32)
            gradient = total.astype(BF16).astype(F32)
            new = adamw(w_ref[rows, cols].astype(F32), m_ref[rows, cols], v_ref[rows, cols], gradient)
            theirs[rows, cols], m_ref[rows, cols], v_ref[rows, cols] = new

        rows_16(c.rows("ab"), c.cols, c.width, tile)
        rows = block_rows(c, me)
        target = out[c.which].at[c.layer, rows, :]
        for side, to in ((0, right), (1, left)):
            hop1[side, c.number] = remote(theirs, target, g1_send.at[side * n + c.number], g1_recv.at[side * n + c.number], to)
        crossing.append(remote(theirs, target, gx_send.at[c.number], gx_recv.at[c.number], other))
        stores[c.number] = [
            pltpu.make_async_copy(theirs, target, out_sem.at[c.number * 3]),
            pltpu.make_async_copy(m_ref, new_m[c.which].at[c.layer], out_sem.at[c.number * 3 + 1]),
            pltpu.make_async_copy(v_ref, new_v[c.which].at[c.layer], out_sem.at[c.number * 3 + 2]),
        ]
        for copy in stores[c.number]:
            copy.start()
        if c.number + 1 < n and c.number >= 1:
            following = chunks[c.number + 1]
            for before in chunks[:c.number]:
                if before.kind == following.kind and before.place == following.place - 2:
                    for copy in stores.pop(before.number):
                        copy.wait()
            for copy in state_loads(following):
                copy.start()

    hop2 = {}
    for c in chunks:
        for side, source, to, part in ((0, LEFT, right, "a"), (1, RIGHT, left, "b")):
            s = side * n + c.number
            hop1[side, c.number].wait_recv()
            block = chip_at[source] * 2 + core
            if c.number not in tail:
                rows = block_rows(c, block, part)
                ref = out[c.which].at[c.layer, rows, :]
                hop2[side, c.number] = remote(ref, ref, g2_send.at[s], g2_recv.at[s], to)
            cross(block_rows(c, block), c, n + s)
    for c in chunks:
        if c.number in tail:
            continue
        for side, part in ((0, "a"), (1, "b")):
            s = side * n + c.number
            hop2[side, c.number].wait_recv()
            cross(block_rows(c, chip_at[OPPOSITE] * 2 + core, part), c, 3 * n + s)
    for copy in crossing:
        copy.wait_recv()
    for copies in stores.values():
        for copy in copies:
            copy.wait()
    for copy in pending:
        copy.wait_send()


def gather_step(tail, terms, weights, m, v):
    shapes = [w.shape for w in weights]
    chunks, kinds, used = chunks_of(shapes)
    n = len(chunks)
    hbm = pl.BlockSpec(memory_space=pl.ANY)
    slots = lambda lead, dtype: [pltpu.VMEM((*(u if x is None else x for x in lead), *k), dtype) for k, u in zip(kinds, used)]
    dma = lambda count: pltpu.SemaphoreType.DMA((count,))
    return pl.pallas_call(
        functools.partial(exchange, chunks, kinds, tail),
        out_shape=[jax.ShapeDtypeStruct(s, BF16) for s in shapes] + [jax.ShapeDtypeStruct(a.shape, F32) for a in (*m, *v)],
        in_specs=[hbm] * 12,
        out_specs=[hbm] * 9,
        scratch_shapes=[
            *slots((4, None), BF16), *slots((None,), BF16), *slots((2, None), BF16), *slots((3,), BF16),
            *slots((2,), BF16), *slots((2,), F32), *slots((2,), F32),
            dma(4 * n), dma(4 * n), dma(2 * n), dma(2 * n), dma(4 * n), dma(4 * n), dma(4 * n), dma(3 * n), dma(3 * n),
            dma(2 * n), dma(2 * n), dma(2 * n), dma(2 * n), dma(5 * n), dma(5 * n),
        ],
        compiler_params=pltpu.CompilerParams(collective_id=0, has_side_effects=True, vmem_limit_bytes=63 * 2**20),
    )(*terms, *weights, *m, *v)


def solution(mesh):
    assert mesh.shape["dp"] == 2 * CHIPS

    def step(*arrays):
        terms, weights, m, v = (arrays[i : i + 3] for i in (0, 3, 6, 9))
        return tuple(gather_step((), [t[0] for t in terms], weights, m, v))

    all_of, cut = P(None, None, None), P(None, "dp", None)
    return jax.shard_map(
        step,
        mesh=mesh,
        in_specs=(P(("rep", "dp"), None, None, None),) * 3 + (all_of,) * 3 + (cut,) * 6,
        out_specs=(P("rep", None, None),) * 3 + (P("rep", "dp", None),) * 6,
        check_vma=False,
    )
```

time: 467 us -> 375 us (0.80)
  waiting for transfers between devices: 408 us -> 0 us
  Pallas kernels: 0 us -> 329 us
  other arithmetic: 18 us -> 0.01 us
  local copies, waits for them, and re-layouts: 26.8 us -> 44.5 us
  between operations: 14.2 us -> 0.7 us
    pallas_call x0 -> x1, Pallas kernels: none -> 329 us  [gather_step(): pl.pallas_call(functools.partial(exchange, chunks, kinds, tail), out_shap...]
    reduce_scatter x3 -> x0, waiting for transfers between devices: 207 us -> none  [step(): lax.psum_scatter(t[0], 'dp', scatter_dimension=1, tiled=True)]
    all_gather x3 -> x0, waiting for transfers between devices: 198 us -> none  [step(): whole = [lax.all_gather(one[0], 'dp', axis=1, tiled=True) for one in new]]
    convert_element_type x3 -> x0, other arithmetic: 18 us -> none  [adamw(): return ((w - 0.02 * step).astype(jnp.bfloat16), m, v)]
    unnamed x17 -> x31, local copies, waits for them, and re-layouts: 26.8 us -> 44.5 us
  transfers between devices with their start and end apart: 6 -> 0, of which waited for: 6 -> 0; matrix products, arithmetic and copies ran while one was open for 4% -> 0% of each run, Pallas kernels for 0% -> 0%
where the time goes in v1:
time: 375 us; the launch traced here: 374 us
  Pallas kernels  329 us (88%)
  local copies, waits for them, and re-layouts  44.5 us (12%)
    pallas_call x1, Pallas kernels, gather_step(): pl.pallas_call(functools.partial(exchange, chunks, kinds, tail), out_shap...  329 us
    unnamed x31, local copies, waits for them, and re-layouts  44.5 us

profile of v1, /device:TPU:113, one launch (start us, length us, event | category | flops | bytes accessed | tf_op | source)
XLA Modules:
  0.0 374.4 jit_solution(545705586124773466)
XLA Ops:
  0.6 329.2 %shard_map.187 = (bf16[2,1024,3200]{2,1,0:T(8,128)(2,1)}, bf16[2,1024,3200]{2,1,0:T(8,128)(2,1)}, bf16[2,3200,1024]{2,1,0:T(8,128)(2,1)}, f32[2,128,3200]{2,1,0:...) custom-call(bf16[2,1024,3200]{2,1,0:T(8,128)(2,1)} %bitcast.3, ...), custom_call_target="tpu_custom_call" | custom-call | tf_op jit(solution)/shard_map/pallas_call | solution.py:270
  329.8 0.0 copy-start
  329.9 0.0 slice-start
  329.9 0.0 slice-start.1
  329.9 0.0 slice-start.2
  329.9 12.7 %copy.30 = bf16[2,1024,3200]{2,1,0:T(8,128)(2,1)} copy(bf16[2,1024,3200]{2,1,0:T(8,128)(2,1)} %get-tuple-element.18) | data formatting | bytes 26214400
  342.6 0.0 copy-done
  342.6 0.0 slice-start.3
  342.6 6.6 %copy.31 = bf16[2,1024,3200]{2,1,0:T(8,128)(2,1)} copy(bf16[2,1024,3200]{2,1,0:T(8,128)(2,1)S(1)} %copy-done) | data formatting | bytes 26214400
  349.2 0.0 slice-done
  349.2 1.1 slice-done.1
  350.4 1.2 slice-done.2
  351.6 0.1 slice-done.3
  351.7 0.0 copy-start.6
  351.7 5.5 %copy.32 = bf16[2,3200,1024]{2,1,0:T(8,128)(2,1)} copy(bf16[2,3200,1024]{2,1,0:T(8,128)(2,1)S(1)} %bitcast.7) | data formatting | bytes 26214400
  357.2 0.0 copy-done.6
  357.2 0.0 copy-start.5
  357.2 1.7 copy.33
  358.9 1.4 copy-done.5
  360.3 0.0 copy-start.4
  360.3 1.7 copy.34
  362.0 1.4 copy-done.4
  363.4 0.0 copy-start.3
  363.4 1.7 copy.35
  365.1 1.4 copy-done.3
  366.5 0.0 copy-start.2
  366.5 1.7 copy.36
  368.2 1.4 copy-done.2
  369.6 0.0 copy-start.1
  369.6 1.7 copy.37
  371.3 1.4 copy-done.1
  372.7 1.7 copy.38
  (1 shorter events, 0.0 us)
Async XLA Ops:
  329.8 12.7 %copy-start = (bf16[2,1024,3200]{2,1,0:T(8,128)(2,1)S(1)}, bf16[2,1024,3200]{2,1,0:T(8,128)(2,1)}, u32[]{:S(2)}) copy-start(bf16[2,1024,3200]{2,1,0:T(8,128)(2,1)} %get-tuple-element.19) | copy-start | bytes 39321604
  329.9 19.4 %slice-start = ((s8[13107200]{0:T(1024)(128)(4,1)}), s8[4194304]{0:T(1024)(128)(4,1)S(1)}, s32[]{:S(2)}) async-start(s8[13107200]{0:T(1024)(128)(4,1)} %bitcast.6), calls=%async_computation | async-start | bytes 8388608
  329.9 20.5 %slice-start.1 = ((s8[13107200]{0:T(1024)(128)(4,1)}), s8[4194304]{0:T(1024)(128)(4,1)S(1)}, s32[]{:S(2)}) async-start(s8[13107200]{0:T(1024)(128)(4,1)} %bitcast.6), calls=%async_computation.1 | async-start | bytes 8388608
  329.9 21.7 %slice-start.2 = ((s8[13107200]{0:T(1024)(128)(4,1)}), s8[4194304]{0:T(1024)(128)(4,1)S(1)}, s32[]{:S(2)}) async-start(s8[13107200]{0:T(1024)(128)(4,1)} %bitcast.6), calls=%async_computation.2 | async-start | bytes 8388608
  342.6 9.1 %slice-start.3 = ((s8[13107200]{0:T(1024)(128)(4,1)}), s8[524288]{0:T(1024)(128)(4,1)S(1)}, s32[]{:S(2)}) async-start(s8[13107200]{0:T(1024)(128)(4,1)} %bitcast.6), calls=%async_computation.3 | async-start | bytes 1048576
  351.7 5.5 %copy-start.6 = (f32[2,128,3200]{2,1,0:T(8,128)S(1)}, f32[2,128,3200]{2,1,0:T(8,128)}, u32[]{:S(2)}) copy-start(f32[2,128,3200]{2,1,0:T(8,128)} %get-tuple-element.21) | copy-start | bytes 9830404
  357.2 3.1 copy-start.5
  360.3 3.1 copy-start.4
  363.4 3.1 copy-start.3
  366.5 3.1 copy-start.2
  369.6 3.1 copy-start.1

commit v2 on v1

--- a/solution.py
+++ b/solution.py
@@ -6,6 +6,7 @@
 from jax.experimental import pallas as pl
 from jax.experimental.pallas import tpu as pltpu
 from jax.sharding import PartitionSpec as P
+
 
 MESH = pl.DeviceIdType.MESH
 F32, BF16 = jnp.float32, jnp.bfloat16
@@ -60,15 +61,16 @@
     return chunks, kinds, used
 
 
-def exchange(chunks, kinds, tail, *refs):
+def exchange(chunks, kinds, stages, *refs):
     it = iter(refs)
     take = lambda n: [next(it) for _ in range(n)]
     g, w, m, v = take(3), take(3), take(3), take(3)
     out, new_m, new_v = take(3), take(3), take(3)
+    for_right, for_left = take(len(stages)), take(len(stages))
     nk = len(kinds)
     peer, pass_in, near_in, own, w_in, m_in, v_in = (take(nk) for _ in range(7))
     (x_send, x_recv, a_send, a_recv, b_send, b_recv, own_sem, in_sem, out_sem,
-     g1_send, g1_recv, g2_send, g2_recv, gx_send, gx_recv) = it
+     g_send, g_recv, gx_send, gx_recv) = it
     n = len(chunks)
 
     me = lax.axis_index("dp")
@@ -187,11 +189,14 @@
     for c in chunks[:2]:
         for copy in state_loads(c):
             copy.start()
-    hop1, crossing, stores = {}, [], {}
-
-    def cross(ref_rows, c, s):
-        crossing.append(remote(
-            out[c.which].at[c.layer, ref_rows, :], out[c.which].at[c.layer, ref_rows, :], gx_send.at[s], gx_recv.at[s], other))
+    arrivals, crossing, stores = {}, [], {}
+
+    def passed_on(c, part):
+        stage, layer = c.stage
+        return (for_right if part == "a" else for_left)[stage].at[layer]
+
+    def kept(c, block, part="ab"):
+        return out[c.which].at[c.layer, block_rows(c, block, part), :]
 
     for c in chunks:
         mine, theirs = take_own(OWN, c)
@@ -212,10 +217,13 @@
             theirs[rows, cols], m_ref[rows, cols], v_ref[rows, cols] = new
 
         rows_16(c.rows("ab"), c.cols, c.width, tile)
-        rows = block_rows(c, me)
-        target = out[c.which].at[c.layer, rows, :]
+        target = kept(c, me)
         for side, to in ((0, right), (1, left)):
-            hop1[side, c.number] = remote(theirs, target, g1_send.at[side * n + c.number], g1_recv.at[side * n + c.number], to)
+            for k, part in enumerate("ab"):
+                s = (side * n + c.number) * 2 + k
+                arrivals[side, c.number, k] = remote(
+                    part_of(theirs, c, part), passed_on(c, part) if side == k else kept(c, me, part),
+                    g_send.at[s], g_recv.at[s], to)
         crossing.append(remote(theirs, target, gx_send.at[c.number], gx_recv.at[c.number], other))
         stores[c.number] = [
             pltpu.make_async_copy(theirs, target, out_sem.at[c.number * 3]),
@@ -233,24 +241,14 @@
             for copy in state_loads(following):
                 copy.start()
 
-    hop2 = {}
-    for c in chunks:
-        for side, source, to, part in ((0, LEFT, right, "a"), (1, RIGHT, left, "b")):
-            s = side * n + c.number
-            hop1[side, c.number].wait_recv()
-            block = chip_at[source] * 2 + core
-            if c.number not in tail:
-                rows = block_rows(c, block, part)
-                ref = out[c.which].at[c.layer, rows, :]
-                hop2[side, c.number] = remote(ref, ref, g2_send.at[s], g2_recv.at[s], to)
-            cross(block_rows(c, block), c, n + s)
-    for c in chunks:
-        if c.number in tail:
-            continue
-        for side, part in ((0, "a"), (1, "b")):
-            s = side * n + c.number
-            hop2[side, c.number].wait_recv()
-            cross(block_rows(c, chip_at[OPPOSITE] * 2 + core, part), c, 3 * n + s)
+    for c in chunks:
+        for k, part in enumerate("ab"):
+            for side, source in ((0, LEFT), (1, RIGHT)):
+                s = (side * n + c.number) * 2 + k
+                arrivals[side, c.number, k].wait_recv()
+                there = kept(c, chip_at[source] * 2 + core, part)
+                crossing.append(remote(
+                    passed_on(c, part) if side == k else there, there, gx_send.at[n + s], gx_recv.at[n + s], other))
     for copy in crossing:
         copy.wait_recv()
     for copies in stores.values():
@@ -260,34 +258,192 @@
         copy.wait_send()
 
 
-def gather_step(tail, terms, weights, m, v):
-    shapes = [w.shape for w in weights]
-    chunks, kinds, used = chunks_of(shapes)
+def gather_step(chunks, kinds, used, stages, terms, weights, m, v):
     n = len(chunks)
     hbm = pl.BlockSpec(memory_space=pl.ANY)
     slots = lambda lead, dtype: [pltpu.VMEM((*(u if x is None else x for x in lead), *k), dtype) for k, u in zip(kinds, used)]
     dma = lambda count: pltpu.SemaphoreType.DMA((count,))
+    part = lambda stage, part: jax.ShapeDtypeStruct(
+        (len(stage), stage[0].rows(part)[1] - stage[0].rows(part)[0], stage[0].cols), BF16)
+    results = [jax.ShapeDtypeStruct(w.shape, BF16) for w in weights]
+    results += [jax.ShapeDtypeStruct(a.shape, F32) for a in (*m, *v)]
+    results += [part(s, "a") for s in stages] + [part(s, "b") for s in stages]
     return pl.pallas_call(
-        functools.partial(exchange, chunks, kinds, tail),
-        out_shape=[jax.ShapeDtypeStruct(s, BF16) for s in shapes] + [jax.ShapeDtypeStruct(a.shape, F32) for a in (*m, *v)],
+        functools.partial(exchange, chunks, kinds, stages),
+        out_shape=results,
         in_specs=[hbm] * 12,
-        out_specs=[hbm] * 9,
+        out_specs=[hbm] * len(results),
         scratch_shapes=[
             *slots((4, None), BF16), *slots((None,), BF16), *slots((2, None), BF16), *slots((3,), BF16),
             *slots((2,), BF16), *slots((2,), F32), *slots((2,), F32),
             dma(4 * n), dma(4 * n), dma(2 * n), dma(2 * n), dma(4 * n), dma(4 * n), dma(4 * n), dma(3 * n), dma(3 * n),
-            dma(2 * n), dma(2 * n), dma(2 * n), dma(2 * n), dma(5 * n), dma(5 * n),
+            dma(4 * n), dma(4 * n), dma(5 * n), dma(5 * n),
         ],
         compiler_params=pltpu.CompilerParams(collective_id=0, has_side_effects=True, vmem_limit_bytes=63 * 2**20),
     )(*terms, *weights, *m, *v)
 
 
+class Move:
+    def __init__(self, source, source_at, target, target_at, rows):
+        self.source, self.source_at = source, source_at
+        self.target, self.target_at = target, target_at
+        self.rows = rows
+
+
+def move_body(moves, kinds, depth, n_in, n_out, *refs):
+    sources, targets = refs[:n_in], refs[n_in : n_in + n_out]
+    bufs, (in_sem, out_sem) = refs[n_in + n_out : -2], refs[-2:]
+    me = lax.axis_index("dp")
+    chip, core = me // 2, me % 2
+    seen, place = [0] * len(kinds), []
+    for u in moves:
+        place.append((u.kind, seen[u.kind] % depth[u.kind]))
+        seen[u.kind] += 1
+
+    def view(ref, at, rows):
+        layer, row = at(chip, core)
+        return ref.at[layer, pl.ds(row if isinstance(row, int) else pl.multiple_of(row, 8), rows), :]
+
+    def load(i):
+        u, (kind, slot) = moves[i], place[i]
+        return pltpu.make_async_copy(view(sources[u.source], u.source_at, u.rows), bufs[kind].at[slot], in_sem.at[i])
+
+    def store(i):
+        u, (kind, slot) = moves[i], place[i]
+        return pltpu.make_async_copy(bufs[kind].at[slot], view(targets[u.target], u.target_at, u.rows), out_sem.at[i])
+
+    waited, last = set(), {}
+
+    def start(i):
+        if place[i] in last:
+            store(last[place[i]]).wait()
+            waited.add(last[place[i]])
+        last[place[i]] = i
+        load(i).start()
+
+    ahead = 8
+    for i in range(min(ahead, len(moves))):
+        start(i)
+    for i in range(len(moves)):
+        load(i).wait()
+        store(i).start()
+        if i + ahead < len(moves):
+            start(i + ahead)
+    for i in range(len(moves)):
+        if i not in waited:
+            store(i).wait()
+
+
+def move(moves, sources, targets, *, into=()):
+    kinds, counts = [], []
+    for u in moves:
+        a = sources[u.source]
+        kind = (u.rows, a.shape[2], a.dtype)
+        if kind not in kinds:
+            kinds.append(kind)
+            counts.append(0)
+        u.kind = kinds.index(kind)
+        counts[u.kind] += 1
+    depth = [min(16, c) for c in counts]
+    nbytes = 2 * sum(k[0] * k[1] * k[2].itemsize * c for k, c in zip(kinds, counts))
+    hbm = pl.BlockSpec(memory_space=pl.ANY)
+    operands = (*sources, *into)
+    return pl.pallas_call(
+        functools.partial(move_body, moves, kinds, depth, len(operands), len(targets)),
+        out_shape=[jax.ShapeDtypeStruct(a.shape, a.dtype) for a in targets],
+        in_specs=[hbm] * len(operands),
+        out_specs=[hbm] * len(targets),
+        input_output_aliases={len(sources) + i: i for i in range(len(into))},
+        scratch_shapes=[pltpu.VMEM((d, *k[:2]), k[2]) for d, k in zip(depth, kinds)]
+        + [pltpu.SemaphoreType.DMA((len(moves),)), pltpu.SemaphoreType.DMA((len(moves),))],
+        compiler_params=pltpu.CompilerParams(vmem_limit_bytes=63 * 2**20),
+        cost_estimate=pl.CostEstimate(flops=2 * nbytes, bytes_accessed=nbytes, transcendentals=0),
+    )(*operands)
+
+
+def place_of(c, r, which, part, layer):
+    start = c.rows(part)[0]
+
+    def at(chip, core):
+        owner = lax.rem(chip + OFFSET[r], CHIPS) * 2 + (core if which == 0 else 1 - core)
+        return layer, owner * c.block + start
+
+    return at
+
+
+def fixed(layer, row=0):
+    return lambda chip, core: (layer, row)
+
+
 def solution(mesh):
-    assert mesh.shape["dp"] == 2 * CHIPS
+    size = mesh.shape["dp"]
+    assert size == 2 * CHIPS
+    to_right = [(d, (d + 2) % size) for d in range(size)]
+    to_left = [(d, (d - 2) % size) for d in range(size)]
+    to_other = [(d, d ^ 1) for d in range(size)]
 
     def step(*arrays):
         terms, weights, m, v = (arrays[i : i + 3] for i in (0, 3, 6, 9))
-        return tuple(gather_step((), [t[0] for t in terms], weights, m, v))
+        chunks, kinds, used = chunks_of([w.shape for w in weights])
+        stages = []
+        for c in chunks:
+            if stages and stages[-1][0].which == c.which and stages[-1][0].half == c.half:
+                stages[-1].append(c)
+            else:
+                stages.append([c])
+        for s, stage in enumerate(stages):
+            for layer, c in enumerate(stage):
+                c.stage = (s, layer)
+
+        results = gather_step(chunks, kinds, used, stages, [t[0] for t in terms], weights, m, v)
+        gathered, moments = results[:3], results[3:9]
+        for_right, for_left = results[9 : 9 + len(stages)], results[9 + len(stages) :]
+
+        passed, crossed = [], []
+        for s in range(len(stages)):
+            passed.append((lax.ppermute(for_right[s], "dp", to_right), lax.ppermute(for_left[s], "dp", to_left)))
+            crossed.append(tuple(lax.ppermute(p, "dp", to_other) for p in passed[s]))
+
+        whole = []
+        for which, g in enumerate(gathered):
+            sources, moves = [g], []
+            for c in (c for c in chunks if c.which == which):
+                stage, layer = c.stage
+                if layer == 0:
+                    sources += [for_right[stage], for_left[stage]]
+                for r in (OWN, LEFT, RIGHT):
+                    for core in (0, 1):
+                        if core == 0 and r != OWN:
+                            for part in "ab":
+                                start, stop = c.rows(part)
+                                at = place_of(c, r, core, part, c.layer)
+                                if (r, part) in ((LEFT, "a"), (RIGHT, "b")):
+                                    source = len(sources) - (2 if part == "a" else 1)
+                                    moves.append(Move(source, fixed(layer), 0, at, stop - start))
+                                else:
+                                    moves.append(Move(0, at, 0, at, stop - start))
+                        else:
+                            at = place_of(c, r, core, "ab", c.layer)
+                            moves.append(Move(0, at, 0, at, c.block))
+            whole += move(moves, sources, [g])
+
+        moves = []
+        for a, array in enumerate(moments):
+            layers, rows, _ = array.shape
+            for layer in range(layers):
+                for row in (0, rows // 2):
+                    moves.append(Move(a, fixed(layer, row), a, fixed(layer, row), rows // 2))
+        moments = move(moves, moments, moments)
+
+        for s, stage in enumerate(stages):
+            which, moves = stage[0].which, []
+            for layer, c in enumerate(stage):
+                for i in range(4):
+                    core, part = i // 2, "ab"[i % 2]
+                    start, stop = c.rows(part)
+                    moves.append(Move(i, fixed(layer), 0, place_of(c, OPPOSITE, core, part, c.layer), stop - start))
+            (whole[which],) = move(moves, [*passed[s], *crossed[s]], [whole[which]], into=[whole[which]])
+        return (*whole, *moments)
 
     all_of, cut = P(None, None, None), P(None, "dp", None)
     return jax.shard_map(

time: 375 us -> 390 us (1.040)
  waiting for transfers between devices: 0 us -> 48.7 us
  local copies, waits for them, and re-layouts: 44.5 us -> 0.77 us
  starting transfers between devices: 0 us -> 15.1 us
  Pallas kernels: 329 us -> 324 us
    ppermute x0 -> x16, waiting for transfers between devices: none -> 48.7 us  [the longest x4 47.3 us: step(): lax.ppermute(for_right[s], 'dp', to_right)]
    unnamed x31 -> x14, local copies, waits for them, and re-layouts: 44.5 us -> 0.77 us
    ppermute x0 -> x16, starting transfers between devices: none -> 15.1 us  [the longest x4 8.83 us: step(): lax.ppermute(for_left[s], 'dp', to_left)]
    pallas_call x1 -> x9, Pallas kernels: 329 us -> 324 us  [the longest x1 277 us: gather_step(): pl.pallas_call(functools.partial(exchange, chunks, kinds, stages), out_sh...]
  transfers between devices with their start and end apart: 0 -> 16, of which waited for: 0 -> 4; matrix products, arithmetic and copies ran while one was open for 0% -> 0% of each run, Pallas kernels for 0% -> 11%
where the time goes in v2:
time: 390 us; the launch traced here: 389 us
  Pallas kernels  324 us (83%)
  waiting for transfers between devices  48.7 us (12%)
  starting transfers between devices  15.1 us (4%)
    pallas_call x1, Pallas kernels, gather_step(): pl.pallas_call(functools.partial(exchange, chunks, kinds, stages), out_sh...  277 us
    ppermute x4, waiting for transfers between devices, step(): lax.ppermute(for_right[s], 'dp', to_right)  47.3 us
    pallas_call x8, Pallas kernels, move(): pl.pallas_call(functools.partial(move_body, moves, kinds, depth, len(oper...  46.8 us
    ppermute x4, starting transfers between devices, step(): lax.ppermute(for_left[s], 'dp', to_left)  8.83 us
  transfers between devices with their start and end apart: 16, of which 4 were waited for; matrix products, arithmetic and copies ran while one was open for 0% of the time, Pallas kernels for 11%

profile of v2, /device:TPU:113, one launch (start us, length us, event | category | flops | bytes accessed | tf_op | source)
XLA Modules:
  0.0 389.4 jit_solution(1392921504244842457)
XLA Ops:
  0.6 277.3 %shard_map.187 = (bf16[2,1024,3200]{2,1,0:T(8,128)(2,1)}, bf16[2,1024,3200]{2,1,0:T(8,128)(2,1)}, bf16[2,3200,1024]{2,1,0:T(8,128)(2,1)}, f32[2,128,3200]{2,1,0:...) custom-call(bf16[2,1024,3200]{2,1,0:T(8,128)(2,1)} %bitcast.3, ...), custom_call_target="tpu_custom_call" | custom-call | tf_op jit(solution)/shard_map/pallas_call | solution.py:271
  277.9 1.5 collective-permute-start.9
  279.4 0.1 collective-permute-start.12
  279.5 0.7 collective-permute-start.8
  280.1 2.0 collective-permute-start.13
  282.2 18.1 %collective-permute-done.8.refs_0_ = bf16[1,192,1024]{2,1,0:T(8,128)(2,1)S(1)} collective-permute-done((bf16[1,192,1024]{2,1,0:T(8,128)(2,1)}, bf16[1,192,1024]{2,1,0:T(8,128)(2,1)S(1)}, u32[]{:S(2)}, u32[]{:S(2)}) %collective-permute-start.8) | collective-permute-done | bytes 393248 | tf_op jit(solution)/shard_map/ppermute | solution.py:404
  300.2 1.3 collective-permute-start.10
  301.5 0.0 collective-permute-start
  301.5 0.0 collective-permute-done.13.refs_1_
  301.5 2.7 collective-permute-start.1
  304.2 0.0 collective-permute-done.9.refs_1_
  304.2 0.0 collective-permute-start.4
  304.2 0.0 collective-permute-done.12.refs_0_
  304.2 0.0 copy-start.1
  304.2 2.7 collective-permute-start.5
  306.9 0.0 collective-permute-done.10.refs_2_
  306.9 1.1 collective-permute-start.15
  308.0 0.0 copy-done.3
  308.0 0.0 copy-done.4
  308.0 1.3 collective-permute-done.15.refs_3_
  309.3 0.4 collective-permute-start.14
  309.7 13.0 %collective-permute-done.refs_0_ = bf16[2,64,3200]{2,1,0:T(8,128)(2,1)S(1)} collective-permute-done((bf16[2,64,3200]{2,1,0:T(8,128)(2,1)}, bf16[2,64,3200]{2,1,0:T(8,128)(2,1)S(1)}, u32[]{:S(2)}, u32[]{:S(2)}) %collective-permute-start) | collective-permute-done | bytes 819232 | tf_op jit(solution)/shard_map/ppermute | solution.py:404
  322.7 0.0 copy-done.1
  322.7 1.3 collective-permute-start.2
  324.0 0.0 collective-permute-done.1.refs_1_
  324.0 0.1 collective-permute-start.3
  324.1 16.2 %collective-permute-done.4.refs_0_ = bf16[2,64,3200]{2,1,0:T(8,128)(2,1)} collective-permute-done((bf16[2,64,3200]{2,1,0:T(8,128)(2,1)}, bf16[2,64,3200]{2,1,0:T(8,128)(2,1)}, u32[]{:S(2)}, u32[]{:S(2)}) %collective-permute-start.4) | collective-permute-done | bytes 819232 | tf_op jit(solution)/shard_map/ppermute | solution.py:404
  340.4 0.9 collective-permute-start.6
  341.2 0.0 collective-permute-done.5.refs_1_
  341.2 0.0 collective-permute-start.7
  341.2 0.0 collective-permute-done.14.refs_2_
  341.2 0.0 copy-start.2
  341.3 0.7 copy-done.2
  342.0 0.5 collective-permute-start.11
  342.5 0.0 copy-done.5
  342.5 7.6 %shard_map.188.refs_4_ = bf16[2,1024,3200]{2,1,0:T(8,128)(2,1)} custom-call(bf16[2,1024,3200]{2,1,0:T(8,128)(2,1)} %get-tuple-element.34.refs_0_, bf16[2,64,3200]{2,1,0:T(8,128)(2,1)} %get-tuple-element.32.refs_1_, bf16[2,64,3200]{2,1,0:T(8,128)(2,1)} %get-tuple-element.33.refs_2_), custom_call_target="tpu_custom_call" | custom-call | flops 39321600 | bytes 19660800 | tf_op jit(solution)/shard_map/pallas_call | solution.py:351
  350.1 7.6 %shard_map.190.refs_4_ = bf16[2,1024,3200]{2,1,0:T(8,128)(2,1)} custom-call(bf16[2,1024,3200]{2,1,0:T(8,128)(2,1)} %get-tuple-element.37.refs_0_, bf16[2,64,3200]{2,1,0:T(8,128)(2,1)} %get-tuple-element.35.refs_1_, bf16[2,64,3200]{2,1,0:T(8,128)(2,1)} %get-tuple-element.36.refs_2_), custom_call_target="tpu_custom_call" | custom-call | flops 39321600 | bytes 19660800 | tf_op jit(solution)/shard_map/pallas_call | solution.py:351
  357.7 7.6 %shard_map.192.refs_4_ = bf16[2,3200,1024]{2,1,0:T(8,128)(2,1)} custom-call(bf16[2,3200,1024]{2,1,0:T(8,128)(2,1)} %get-tuple-element.42.refs_0_, bf16[1,208,1024]{2,1,0:T(8,128)(2,1)} %get-tuple-element.40.refs_1_, bf16[1,192,1024]{2,1,0:T(8,128)(2,1)} %get-tuple-element.41.refs_2_, bf16[1,192,1024]{2,1,0:T(8,128)(2,1)} %get-tuple-element.38.refs_3_, ...), custom_call_target="tpu_custom_call" | custom-call | flops 39321600 | bytes 19660800 | tf_op jit(solution)/shard_map/pallas_call | solution.py:351
  365.3 13.9 %shard_map.195 = (f32[2,128,3200]{2,1,0:T(8,128)}, f32[2,128,3200]{2,1,0:T(8,128)}, f32[2,400,1024]{2,1,0:T(8,128)}, f32[2,128,3200]{2,1,0:T(8,128)}, f32[2,128,3200]{2,1,0:T(8,128)}, /*index=5*/f32[2,400,1024]{2,1,0:T(8,128)}) custom-call(f32[2,128,3200]{2,1,0:T(8,128)} %get-tuple-element.43.refs_0_, f32[2,128,3200]{2,1,0:T(8,128)} %get-tuple-element.44.refs_1_, ...), custom_call_target="tpu_custom_call" | custom-call | flops 78643200 | bytes 39321600 | tf_op jit(solution)/shard_map/pallas_call | solution.py:351
  379.2 2.2 shard_map.193.refs_4_
  381.4 0.0 collective-permute-done.11.refs_3_
  381.4 2.2 shard_map.194
  383.7 0.0 collective-permute-done.2.refs_2_
  383.7 0.0 collective-permute-done.3.refs_3_
  383.7 2.8 shard_map.189
  386.5 0.0 collective-permute-done.6.refs_2_
  386.5 0.0 collective-permute-done.7.refs_3_
  386.5 2.8 shard_map.191
  (7 shorter events, 0.0 us)
Async XLA Ops:
  277.9 26.2 %collective-permute-start.9 = (bf16[1,208,1024]{2,1,0:T(8,128)(2,1)}, bf16[1,208,1024]{2,1,0:T(8,128)(2,1)}, u32[]{:S(2)}, u32[]{:S(2)}) collective-permute-start(bf16[1,208,1024]{2,1,0:T(8,128)(2,1)} %get-tuple-element.39.refs_4_), channel_id=1, source_target_pairs={{0,6},{1,7},{2,0},{3,1},{4,2},{5,3},{6,4},{7,5},{8,14},{9,15},{10,... | collective-permute-start | bytes 1277960 | tf_op jit(solution)/shard_map/ppermute | solution.py:404
  279.4 24.8 %collective-permute-start.12 = (bf16[1,208,1024]{2,1,0:T(8,128)(2,1)}, bf16[1,208,1024]{2,1,0:T(8,128)(2,1)S(1)}, u32[]{:S(2)}, u32[]{:S(2)}) collective-permute-start(bf16[1,208,1024]{2,1,0:T(8,128)(2,1)} %get-tuple-element.40.refs_1_), channel_id=1, source_target_pairs={{0,2},{1,3},{2,4},{3,5},{4,6},{5,7},{6,0},{7,1},{8,10},{9,11},{10,... | collective-permute-start | bytes 1277960 | tf_op jit(solution)/shard_map/ppermute | solution.py:404
  279.5 20.8 %collective-permute-start.8 = (bf16[1,192,1024]{2,1,0:T(8,128)(2,1)}, bf16[1,192,1024]{2,1,0:T(8,128)(2,1)S(1)}, u32[]{:S(2)}, u32[]{:S(2)}) collective-permute-start(bf16[1,192,1024]{2,1,0:T(8,128)(2,1)} %get-tuple-element.38.refs_3_), channel_id=1, source_target_pairs={{0,2},{1,3},{2,4},{3,5},{4,6},{5,7},{6,0},{7,1},{8,10},{9,11},{10,... | collective-permute-start | bytes 1179656 | tf_op jit(solution)/shard_map/ppermute | solution.py:404
  280.1 21.4 %collective-permute-start.13 = (bf16[1,192,1024]{2,1,0:T(8,128)(2,1)}, bf16[1,192,1024]{2,1,0:T(8,128)(2,1)S(1)}, u32[]{:S(2)}, u32[]{:S(2)}) collective-permute-start(bf16[1,192,1024]{2,1,0:T(8,128)(2,1)} %get-tuple-element.41.refs_2_), channel_id=1, source_target_pairs={{0,6},{1,7},{2,0},{3,1},{4,2},{5,3},{6,4},{7,5},{8,14},{9,15},{10,... | collective-permute-start | bytes 1179656 | tf_op jit(solution)/shard_map/ppermute | solution.py:404
  300.2 7.8 %copy-start.3 = (bf16[1,192,1024]{2,1,0:T(8,128)(2,1)}, bf16[1,192,1024]{2,1,0:T(8,128)(2,1)S(1)}, u32[]{:S(2)}) copy-start(bf16[1,192,1024]{2,1,0:T(8,128)(2,1)S(1)} %collective-permute-done.8.refs_0_) | copy-start | bytes 1179652
  300.2 6.6 %collective-permute-start.10 = (bf16[1,192,1024]{2,1,0:T(8,128)(2,1)S(1)}, bf16[1,192,1024]{2,1,0:T(8,128)(2,1)S(1)}, u32[]{:S(2)}, u32[]{:S(2)}) collective-permute-start(bf16[1,192,1024]{2,1,0:T(8,128)(2,1)S(1)} %collective-permute-done.8.refs_0_), channel_id=1, source_target_pairs={{0,1},{1,0},{2,3},{3,2},{4,5},{5,4},{6,7},{7,6},{8,9},{9,8},{10,11... | collective-permute-start | bytes 1179656 | tf_op jit(solution)/shard_map/ppermute | solution.py:405
  301.5 21.2 %collective-permute-start = (bf16[2,64,3200]{2,1,0:T(8,128)(2,1)}, bf16[2,64,3200]{2,1,0:T(8,128)(2,1)S(1)}, u32[]{:S(2)}, u32[]{:S(2)}) collective-permute-start(bf16[2,64,3200]{2,1,0:T(8,128)(2,1)} %get-tuple-element.32.refs_1_), channel_id=1, source_target_pairs={{0,2},{1,3},{2,4},{3,5},{4,6},{5,7},{6,0},{7,1},{8,10},{9,11},{10,... | collective-permute-start | bytes 2457608 | tf_op jit(solution)/shard_map/ppermute | solution.py:404
  301.5 41.0 %copy-start.5 = (bf16[1,192,1024]{2,1,0:T(8,128)(2,1)}, bf16[1,192,1024]{2,1,0:T(8,128)(2,1)S(1)}, u32[]{:S(2)}) copy-start(bf16[1,192,1024]{2,1,0:T(8,128)(2,1)S(1)} %collective-permute-done.13.refs_1_) | copy-start | bytes 1179652
  301.5 22.5 %collective-permute-start.1 = (bf16[2,64,3200]{2,1,0:T(8,128)(2,1)}, bf16[2,64,3200]{2,1,0:T(8,128)(2,1)}, u32[]{:S(2)}, u32[]{:S(2)}) collective-permute-start(bf16[2,64,3200]{2,1,0:T(8,128)(2,1)} %get-tuple-element.33.refs_2_), channel_id=1, source_target_pairs={{0,6},{1,7},{2,0},{3,1},{4,2},{5,3},{6,4},{7,5},{8,14},{9,15},{10,... | collective-permute-start | bytes 2457608 | tf_op jit(solution)/shard_map/ppermute | solution.py:404
  304.2 36.2 %collective-permute-start.4 = (bf16[2,64,3200]{2,1,0:T(8,128)(2,1)}, bf16[2,64,3200]{2,1,0:T(8,128)(2,1)}, u32[]{:S(2)}, u32[]{:S(2)}) collective-permute-start(bf16[2,64,3200]{2,1,0:T(8,128)(2,1)} %get-tuple-element.35.refs_1_), channel_id=1, source_target_pairs={{0,2},{1,3},{2,4},{3,5},{4,6},{5,7},{6,0},{7,1},{8,10},{9,11},{10,... | collective-permute-start | bytes 2457608 | tf_op jit(solution)/shard_map/ppermute | solution.py:404
  304.2 18.5 %copy-start.1 = (bf16[1,208,1024]{2,1,0:T(8,128)(2,1)}, bf16[1,208,1024]{2,1,0:T(8,128)(2,1)S(1)}, u32[]{:S(2)}) copy-start(bf16[1,208,1024]{2,1,0:T(8,128)(2,1)S(1)} %collective-permute-done.12.refs_0_) | copy-start | bytes 1277956
  304.2 37.0 %collective-permute-start.5 = (bf16[2,64,3200]{2,1,0:T(8,128)(2,1)}, bf16[2,64,3200]{2,1,0:T(8,128)(2,1)}, u32[]{:S(2)}, u32[]{:S(2)}) collective-permute-start(bf16[2,64,3200]{2,1,0:T(8,128)(2,1)} %get-tuple-element.36.refs_2_), channel_id=1, source_target_pairs={{0,6},{1,7},{2,0},{3,1},{4,2},{5,3},{6,4},{7,5},{8,14},{9,15},{10,... | collective-permute-start | bytes 2457608 | tf_op jit(solution)/shard_map/ppermute | solution.py:404
  306.9 1.1 copy-start.4
  306.9 2.5 collective-permute-start.15
  309.3 33.2 %copy-start.6 = (bf16[1,192,1024]{2,1,0:T(8,128)(2,1)}, bf16[1,192,1024]{2,1,0:T(8,128)(2,1)S(1)}, u32[]{:S(2)}) copy-start(bf16[1,192,1024]{2,1,0:T(8,128)(2,1)S(1)} %collective-permute-done.15.refs_3_) | copy-start | bytes 1179652
  309.3 31.9 %collective-permute-start.14 = (bf16[1,208,1024]{2,1,0:T(8,128)(2,1)S(1)}, bf16[1,208,1024]{2,1,0:T(8,128)(2,1)S(1)}, u32[]{:S(2)}, u32[]{:S(2)}) collective-permute-start(bf16[1,208,1024]{2,1,0:T(8,128)(2,1)S(1)} %collective-permute-done.12.refs_0_), channel_id=1, source_target_pairs={{0,1},{1,0},{2,3},{3,2},{4,5},{5,4},{6,7},{7,6},{8,9},{9,8},{10,11... | collective-permute-start | bytes 1277960 | tf_op jit(solution)/shard_map/ppermute | solution.py:405
  322.7 27.4 %copy-start = (bf16[2,64,3200]{2,1,0:T(8,128)(2,1)}, bf16[2,64,3200]{2,1,0:T(8,128)(2,1)S(1)}, u32[]{:S(2)}) copy-start(bf16[2,64,3200]{2,1,0:T(8,128)(2,1)S(1)} %collective-permute-done.refs_0_) | copy-start | bytes 2457604
  322.7 60.9 %collective-permute-start.2 = (bf16[2,64,3200]{2,1,0:T(8,128)(2,1)S(1)}, bf16[2,64,3200]{2,1,0:T(8,128)(2,1)}, u32[]{:S(2)}, u32[]{:S(2)}) collective-permute-start(bf16[2,64,3200]{2,1,0:T(8,128)(2,1)S(1)} %collective-permute-done.refs_0_), channel_id=1, source_target_pairs={{0,1},{1,0},{2,3},{3,2},{4,5},{5,4},{6,7},{7,6},{8,9},{9,8},{10,11... | collective-permute-start | bytes 2457608 | tf_op jit(solution)/shard_map/ppermute | solution.py:405
  324.0 59.6 %collective-permute-start.3 = (bf16[2,64,3200]{2,1,0:T(8,128)(2,1)}, bf16[2,64,3200]{2,1,0:T(8,128)(2,1)}, u32[]{:S(2)}, u32[]{:S(2)}) collective-permute-start(bf16[2,64,3200]{2,1,0:T(8,128)(2,1)} %collective-permute-done.1.refs_1_), channel_id=1, source_target_pairs={{0,1},{1,0},{2,3},{3,2},{4,5},{5,4},{6,7},{7,6},{8,9},{9,8},{10,11... | collective-permute-start | bytes 2457608 | tf_op jit(solution)/shard_map/ppermute | solution.py:405
  340.4 46.2 %collective-permute-start.6 = (bf16[2,64,3200]{2,1,0:T(8,128)(2,1)}, bf16[2,64,3200]{2,1,0:T(8,128)(2,1)}, u32[]{:S(2)}, u32[]{:S(2)}) collective-permute-start(bf16[2,64,3200]{2,1,0:T(8,128)(2,1)} %collective-permute-done.4.refs_0_), channel_id=1, source_target_pairs={{0,1},{1,0},{2,3},{3,2},{4,5},{5,4},{6,7},{7,6},{8,9},{9,8},{10,11... | collective-permute-start | bytes 2457608 | tf_op jit(solution)/shard_map/ppermute | solution.py:405
  341.2 45.3 %collective-permute-start.7 = (bf16[2,64,3200]{2,1,0:T(8,128)(2,1)}, bf16[2,64,3200]{2,1,0:T(8,128)(2,1)}, u32[]{:S(2)}, u32[]{:S(2)}) collective-permute-start(bf16[2,64,3200]{2,1,0:T(8,128)(2,1)} %collective-permute-done.5.refs_1_), channel_id=1, source_target_pairs={{0,1},{1,0},{2,3},{3,2},{4,5},{5,4},{6,7},{7,6},{8,9},{9,8},{10,11... | collective-permute-start | bytes 2457608 | tf_op jit(solution)/shard_map/ppermute | solution.py:405
  341.2 0.8 copy-start.2
  342.0 39.4 %collective-permute-start.11 = (bf16[1,208,1024]{2,1,0:T(8,128)(2,1)}, bf16[1,208,1024]{2,1,0:T(8,128)(2,1)}, u32[]{:S(2)}, u32[]{:S(2)}) collective-permute-start(bf16[1,208,1024]{2,1,0:T(8,128)(2,1)} %collective-permute-done.9.refs_1_), channel_id=1, source_target_pairs={{0,1},{1,0},{2,3},{3,2},{4,5},{5,4},{6,7},{7,6},{8,9},{9,8},{10,11... | collective-permute-start | bytes 1277960 | tf_op jit(solution)/shard_map/ppermute | solution.py:405

commit v3 on v1

v3 whole, which is shorter than its diff:
```python
import functools

import jax
import jax.numpy as jnp
from jax import lax
from jax.experimental import pallas as pl
from jax.experimental.pallas import tpu as pltpu
from jax.sharding import PartitionSpec as P


MESH = pl.DeviceIdType.MESH
F32, BF16 = jnp.float32, jnp.bfloat16
VMEM_LIMIT = 63 * 2**20
CHIPS = 4
OPPOSITE, RIGHT, LEFT, OWN = range(4)
OFFSET = (2, 1, 3, 0)
FIRST_ROWS = 16
LAST_ROWS = 56


def adamw(w, m, v, g):
    m = 0.9 * m + 0.1 * g
    v = 0.95 * v + 0.05 * g * g
    step = m * lax.rsqrt(v + 1e-8) + 0.1 * w
    return (w - 0.02 * step).astype(BF16), m, v


class Chunk:
    def __init__(self, number, which, layer, kind, place, rows, cols):
        self.number, self.which, self.layer = number, which, layer
        self.kind, self.place = kind, place
        self.rows, self.cols = rows, cols
        self.width = 640 if cols % 640 == 0 else 512
        self.segments = []


def plan(shapes):
    kinds, chunks, used = [], [], []
    for which, (layers, _, rows, cols) in enumerate(shapes):
        if (rows, cols) not in kinds:
            kinds.append((rows, cols))
            used.append(0)
        kind = kinds.index((rows, cols))
        for layer in range(layers):
            chunks.append(Chunk(len(chunks), which, layer, kind, used[kind], rows, cols))
            used[kind] += 1
    stages, count = [], 0
    for c in chunks:
        last = c.which == chunks[-1].which
        cuts = [0, c.rows - LAST_ROWS, c.rows] if c is chunks[-1] else [0, c.rows]
        for start, stop in zip(cuts, cuts[1:]):
            if last or not stages or stages[-1][0][0].which != c.which:
                stages.append([])
            stages[-1].append((c, start, stop - start))
            c.segments.append((count, len(stages) - 1, len(stages[-1]) - 1, start, stop - start))
            count += 1
    return chunks, kinds, used, stages, count


def exchange(chunks, kinds, stages, *refs):
    it = iter(refs)
    take = lambda n: [next(it) for _ in range(n)]
    g, w, m, v = take(3), take(3), take(3), take(3)
    out, new_m, new_v, onward = take(3), take(3), take(3), take(len(stages))
    nk = len(kinds)
    peer, pass_in, near_in, own, w_in, m_in, v_in = (take(nk) for _ in range(7))
    (x_send, x_recv, a_send, a_recv, b_send, b_recv, own_sem, in_sem, out_sem, g_send, g_recv, gx_send, gx_recv) = it
    n = len(chunks)

    me = lax.axis_index("dp")
    chip, core = me // 2, me % 2
    right = lax.rem(chip + 1, CHIPS) * 2 + core
    left = lax.rem(chip + CHIPS - 1, CHIPS) * 2 + core
    other = chip * 2 + (1 - core)
    chip_at = [lax.rem(chip + OFFSET[r], CHIPS) for r in range(4)]
    ahead_chip, behind_chip = (lax.rem(chip + 1 + 2 * (core if s else 1 - core), CHIPS) for s in (1, 0))
    ahead, behind = ahead_chip * 2 + core, behind_chip * 2 + core

    barrier = pltpu.get_barrier_semaphore()
    for d in (right, left, other):
        pl.semaphore_signal(barrier, inc=1, device_id={"dp": d}, device_id_type=MESH)

    pending = []

    def remote(src, dst, send, recv, to):
        copy = pltpu.make_async_remote_copy(
            src_ref=src, dst_ref=dst, send_sem=send, recv_sem=recv, device_id={"dp": to}, device_id_type=MESH)
        copy.start()
        pending.append(copy)
        return copy

    order = [(OPPOSITE, c) for c in chunks]
    for c in chunks:
        order += [(RIGHT, c), (LEFT, c)]
    order += [(OWN, c) for c in chunks]
    slots, seen = {}, [0] * nk
    for r, c in order:
        slots[r, c.number] = seen[c.kind] % 3
        seen[c.kind] += 1

    def own_load(p):
        r, c = order[p]
        return pltpu.make_async_copy(
            g[c.which].at[c.layer, pl.ds((chip_at[r] * 2 + core) * 2, 2)],
            own[c.kind].at[slots[r, c.number]], own_sem.at[r * n + c.number])

    def state_loads(c):
        s = c.place % 2
        return [
            pltpu.make_async_copy(w[c.which].at[c.layer, pl.ds(me * 2, 2)], w_in[c.kind].at[s], in_sem.at[c.number * 3]),
            pltpu.make_async_copy(m[c.which].at[c.layer], m_in[c.kind].at[s], in_sem.at[c.number * 3 + 1]),
            pltpu.make_async_copy(v[c.which].at[c.layer], v_in[c.kind].at[s], in_sem.at[c.number * 3 + 2]),
        ]

    own_load(0).start()
    own_load(1).start()
    pl.semaphore_wait(barrier, 3)

    x = {}

    def swap(r, c):
        x[r, c.number] = remote(
            g[c.which].at[c.layer, pl.ds((chip_at[r] * 2 + (1 - core)) * 2, 2)], peer[c.kind].at[r, c.place],
            x_send.at[r * n + c.number], x_recv.at[r * n + c.number], other)

    first = chunks[0]
    pieces = [(h, rows) for rows in ((0, FIRST_ROWS), (FIRST_ROWS, first.rows)) for h in (0, 1)]
    for k, (h, (start, stop)) in enumerate(pieces):
        s = 4 * n + k
        x[OPPOSITE, h, start] = remote(
            g[first.which].at[first.layer, (chip_at[OPPOSITE] * 2 + (1 - core)) * 2 + h, pl.ds(start, stop - start)],
            peer[first.kind].at[OPPOSITE, first.place, h, pl.ds(start, stop - start)], x_send.at[s], x_recv.at[s], other)
    for c in chunks[1:]:
        swap(OPPOSITE, c)

    position = [0]

    def take_own(r, c):
        p = position[0]
        position[0] += 1
        assert order[p] == (r, c)
        if p + 2 < len(order):
            own_load(p + 2).start()
        own_load(p).wait()
        if (r, c.number) in x:
            x[r, c.number].wait_recv()
        return own[c.kind].at[slots[r, c.number]], peer[c.kind].at[r, c.place]

    def tiles(c, start, stop, body):
        whole = (stop - start) // 16
        cols = [pl.ds(k, c.width) for k in range(0, c.cols, c.width)]

        @pl.loop(0, whole)
        def _(t):
            for k in cols:
                body(pl.ds(pl.multiple_of(start + t * 16, 16), 16), k)

        if start + whole * 16 < stop:
            for k in cols:
                body(pl.ds(start + whole * 16, stop - start - whole * 16), k)

    def add(c, h, mine, theirs, *more, rows=None):
        def tile(r, k):
            total = mine[h, r, k].astype(F32) + theirs[h, r, k].astype(F32)
            for ref in more:
                total += ref[h, r, k].astype(F32)
            theirs[h, r, k] = total.astype(BF16)

        tiles(c, *(rows or (0, c.rows)), tile)

    step0 = {}
    for c in chunks:
        mine, theirs = take_own(OPPOSITE, c)
        for h, (start, stop) in pieces if c is first else [(0, (0, c.rows)), (1, (0, c.rows))]:
            if c is first:
                x[OPPOSITE, h, start].wait_recv()
            add(c, h, mine, theirs, rows=(start, stop))
            s = h * n + c.number if start == 0 else 2 * n + h
            step0.setdefault((h, c.number), []).append(remote(
                theirs.at[h, pl.ds(start, stop - start)], pass_in[c.kind].at[c.place, h, pl.ds(start, stop - start)],
                a_send.at[s], a_recv.at[s], (right, left)[h]))
        swap(RIGHT, c)
        swap(LEFT, c)

    step1 = {}
    for c in chunks:
        for r, to, side in ((RIGHT, right, 0), (LEFT, left, 1)):
            mine, theirs = take_own(r, c)
            for h in (side, 1 - side):
                if h == side:
                    for copy in step0[h, c.number]:
                        copy.wait_recv()
                    add(c, h, mine, theirs, pass_in[c.kind].at[c.place])
                else:
                    add(c, h, mine, theirs)
                s = (side * n + c.number) * 2 + h
                step1[side, c.number, h] = remote(
                    theirs.at[h], near_in[c.kind].at[side, c.place, h], b_send.at[s], b_recv.at[s], to)
        swap(OWN, c)

    for c in chunks[:2]:
        for copy in state_loads(c):
            copy.start()
    arrivals, crossing, stores = {}, [], {}
    for c in chunks:
        mine, theirs = take_own(OWN, c)
        for copy in state_loads(c):
            copy.wait()
        s = c.place % 2
        from_left, from_right = near_in[c.kind].at[0, c.place], near_in[c.kind].at[1, c.place]
        w_ref, m_ref, v_ref = w_in[c.kind].at[s], m_in[c.kind].at[s], v_in[c.kind].at[s]
        for h in (0, 1):
            step1[0, c.number, h].wait_recv()
            step1[1, c.number, h].wait_recv()

            def tile(r, k):
                total = mine[h, r, k].astype(F32) + theirs[h, r, k].astype(F32)
                total += from_left[h, r, k].astype(F32) + from_right[h, r, k].astype(F32)
                gradient = total.astype(BF16).astype(F32)
                new = adamw(w_ref[h, r, k].astype(F32), m_ref[h, r, k], v_ref[h, r, k], gradient)
                theirs[h, r, k], m_ref[h, r, k], v_ref[h, r, k] = new

            tiles(c, 0, c.rows, tile)
        for number, stage, index, start, size in c.segments:
            rows = pl.ds(start, size)
            for k, (h, to) in enumerate(((core, ahead), (1 - core, ahead), (1 - core, behind), (core, behind))):
                dst = onward[stage].at[index, core] if k == 0 else out[c.which].at[c.layer, me * 2 + h, rows]
                arrivals[number, k] = remote(
                    theirs.at[h, rows], dst, g_send.at[number * 4 + k], g_recv.at[number * 4 + k], to)
        target = out[c.which].at[c.layer, pl.ds(me * 2, 2)]
        crossing.append(remote(theirs, target, gx_send.at[c.number], gx_recv.at[c.number], other))
        stores[c.number] = [
            pltpu.make_async_copy(theirs, target, out_sem.at[c.number * 3]),
            pltpu.make_async_copy(m_ref, new_m[c.which].at[c.layer], out_sem.at[c.number * 3 + 1]),
            pltpu.make_async_copy(v_ref, new_v[c.which].at[c.layer], out_sem.at[c.number * 3 + 2]),
        ]
        for copy in stores[c.number]:
            copy.start()
        if c.number + 1 < n and c.number >= 1:
            following = chunks[c.number + 1]
            for before in chunks[: c.number]:
                if before.kind == following.kind and before.place == following.place - 2:
                    for copy in stores.pop(before.number):
                        copy.wait()
            for copy in state_loads(following):
                copy.start()

    for c in chunks:
        for number, stage, index, start, size in c.segments:
            rows = pl.ds(start, size)
            for k, (h, owner) in enumerate(
                ((core, behind_chip), (1 - core, behind_chip), (1 - core, ahead_chip), (core, ahead_chip))):
                s = n + number * 4 + k
                arrivals[number, k].wait_recv()
                there = out[c.which].at[c.layer, (owner * 2 + core) * 2 + h, rows]
                crossing.append(remote(
                    onward[stage].at[index, core] if k == 0 else there,
                    onward[stage].at[index, core] if k == 2 else there, gx_send.at[s], gx_recv.at[s], other))
    for copy in crossing:
        copy.wait_recv()
    for copies in stores.values():
        for copy in copies:
            copy.wait()
    for copy in pending:
        copy.wait_send()


def gather_step(chunks, kinds, used, stages, segments, terms, weights, m, v):
    n = len(chunks)
    hbm = pl.BlockSpec(memory_space=pltpu.HBM)
    slots = lambda lead, dtype: [
        pltpu.VMEM((*(u if x is None else x for x in lead), 2, *k), dtype) for k, u in zip(kinds, used)]
    dma = lambda count: pltpu.SemaphoreType.DMA((count,))
    results = [jax.ShapeDtypeStruct(w.shape, BF16) for w in weights]
    results += [jax.ShapeDtypeStruct(a.shape, F32) for a in (*m, *v)]
    results += [jax.ShapeDtypeStruct((len(s), 2, s[0][2], s[0][0].cols), BF16) for s in stages]
    return pl.pallas_call(
        functools.partial(exchange, chunks, kinds, stages),
        out_shape=results,
        in_specs=[hbm] * 12,
        out_specs=[hbm] * len(results),
        scratch_shapes=[
            *slots((4, None), BF16), *slots((None,), BF16), *slots((2, None), BF16), *slots((3,), BF16),
            *slots((2,), BF16), *slots((2,), F32), *slots((2,), F32),
            dma(4 * n + 4), dma(4 * n + 4), dma(2 * n + 2), dma(2 * n + 2), dma(4 * n), dma(4 * n), dma(4 * n), dma(3 * n),
            dma(3 * n), dma(4 * segments), dma(4 * segments), dma(n + 4 * segments), dma(n + 4 * segments),
        ],
        compiler_params=pltpu.CompilerParams(collective_id=0, has_side_effects=True, vmem_limit_bytes=VMEM_LIMIT),
    )(*terms, *weights, *m, *v)


class Move:
    def __init__(self, source, source_at, target, target_at, shape):
        self.source, self.source_at = source, source_at
        self.target, self.target_at = target, target_at
        self.shape = shape


def move_body(moves, kinds, depth, n_in, n_out, *refs):
    sources, targets = refs[:n_in], refs[n_in : n_in + n_out]
    bufs, (in_sem, out_sem) = refs[n_in + n_out : -2], refs[-2:]
    me = lax.axis_index("dp")
    chip, core = me // 2, me % 2
    seen, place = [0] * len(kinds), []
    for u in moves:
        place.append((u.kind, seen[u.kind] % depth[u.kind]))
        seen[u.kind] += 1

    def load(i):
        u, (kind, slot) = moves[i], place[i]
        return pltpu.make_async_copy(sources[u.source].at[u.source_at(chip, core)], bufs[kind].at[slot], in_sem.at[i])

    def store(i):
        u, (kind, slot) = moves[i], place[i]
        return pltpu.make_async_copy(bufs[kind].at[slot], targets[u.target].at[u.target_at(chip, core)], out_sem.at[i])

    waited, last = set(), {}

    def start(i):
        if place[i] in last:
            store(last[place[i]]).wait()
            waited.add(last[place[i]])
        last[place[i]] = i
        load(i).start()

    ahead = 8
    for i in range(min(ahead, len(moves))):
        start(i)
    for i in range(len(moves)):
        load(i).wait()
        store(i).start()
        if i + ahead < len(moves):
            start(i + ahead)
    for i in range(len(moves)):
        if i not in waited:
            store(i).wait()


def move(moves, sources, targets):
    kinds, counts = [], []
    for u in moves:
        kind = (u.shape, sources[u.source].dtype)
        if kind not in kinds:
            kinds.append(kind)
            counts.append(0)
        u.kind = kinds.index(kind)
        counts[u.kind] += 1
    depth = [min(14, c) for c in counts]
    size = lambda shape: functools.reduce(lambda a, b: a * b, shape)
    nbytes = 2 * sum(size(shape) * dtype.itemsize * c for (shape, dtype), c in zip(kinds, counts))
    hbm = pl.BlockSpec(memory_space=pltpu.HBM)
    return pl.pallas_call(
        functools.partial(move_body, moves, kinds, depth, len(sources), len(targets)),
        out_shape=[jax.ShapeDtypeStruct(a.shape, a.dtype) for a in targets],
        in_specs=[hbm] * len(sources),
        out_specs=[hbm] * len(targets),
        scratch_shapes=[pltpu.VMEM((d, *shape), dtype) for d, (shape, dtype) in zip(depth, kinds)]
        + [pltpu.SemaphoreType.DMA((len(moves),)), pltpu.SemaphoreType.DMA((len(moves),))],
        compiler_params=pltpu.CompilerParams(vmem_limit_bytes=48 * 2**20),
        cost_estimate=pl.CostEstimate(flops=2 * nbytes, bytes_accessed=nbytes, transcendentals=0),
    )(*sources)


def put_body(moves, n_in, *refs):
    sources, target, sem = refs[:n_in], refs[-2], refs[-1]
    me = lax.axis_index("dp")
    chip, core = me // 2, me % 2
    copies = [
        pltpu.make_async_copy(
            sources[u.source].at[u.source_at(chip, core)], target.at[u.target_at(chip, core)], sem.at[i])
        for i, u in enumerate(moves)
    ]
    for copy in copies:
        copy.start()
    for copy in copies:
        copy.wait()


def put(moves, sources, into):
    nbytes = 2 * sum(a.size * a.dtype.itemsize for a in sources)
    hbm = pl.BlockSpec(memory_space=pltpu.HBM)
    return pl.pallas_call(
        functools.partial(put_body, moves, len(sources) + 1),
        out_shape=jax.ShapeDtypeStruct(into.shape, into.dtype),
        in_specs=[pl.BlockSpec(memory_space=pltpu.VMEM)] * len(sources) + [hbm],
        out_specs=hbm,
        input_output_aliases={len(sources): 0},
        scratch_shapes=[pltpu.SemaphoreType.DMA((len(moves),))],
        compiler_params=pltpu.CompilerParams(vmem_limit_bytes=16 * 2**20),
        cost_estimate=pl.CostEstimate(flops=2 * nbytes, bytes_accessed=nbytes, transcendentals=0),
    )(*sources, into)


def known_moves(chunks, which, source, onward, target):
    def block(c, r, parity):
        def at(chip, core):
            owner = lax.rem(chip + (0 if r == OWN else 1 + 2 * core), CHIPS) * 2 + parity
            return c.layer, pl.ds(owner * 2, 2)

        return at

    def behind(c, parity, passed, start, size):
        def at(chip, core):
            owner = lax.rem(chip + 3 - 2 * core, CHIPS) * 2 + parity
            return c.layer, owner * 2 + (core if passed else 1 - core), pl.ds(start, size)

        return at

    moves = []
    for c in (c for c in chunks if c.which == which):
        for parity in (0, 1):
            for r in (OWN, RIGHT):
                at = block(c, r, parity)
                moves.append(Move(source, at, target, at, (2, c.rows, c.cols)))
            at = behind(c, parity, False, 0, c.rows)
            moves.append(Move(source, at, target, at, (c.rows, c.cols)))
            for _, stage, index, start, size in c.segments:
                at = lambda chip, core, index=index, parity=parity: (index, parity)
                moves.append(Move(onward[stage], at, target, behind(c, parity, True, start, size), (size, c.cols)))
    return moves


def last_moves(stage, sources, target):
    moves = []
    for index, (c, start, size) in enumerate(stage):
        for k, source in enumerate(sources):
            for parity in (0, 1):
                def to(chip, core, c=c, start=start, size=size, k=k, parity=parity):
                    owner = lax.rem(chip + 2, CHIPS) * 2 + parity
                    return c.layer, owner * 2 + (core if k == 0 else 1 - core), pl.ds(start, size)

                at = lambda chip, core, index=index, parity=parity: (index, parity)
                moves.append(Move(source, at, target, to, (size, c.cols)))
    return moves


def solution(mesh):
    devices = mesh.shape["dp"]
    assert devices == 2 * CHIPS
    onward_to = [(d, (d + 2 - 4 * (d % 2)) % devices) for d in range(devices)]
    across = [(d, d ^ 1) for d in range(devices)]

    def halves(a, count):
        return a.reshape(a.shape[0], count, a.shape[1] // count, a.shape[2])

    def step(*arrays):
        shapes = [a.shape for a in arrays]
        terms = [halves(t[0], 2 * devices) for t in arrays[:3]]
        weights = [halves(w, 2 * devices) for w in arrays[3:6]]
        m, v = ([halves(a, 2) for a in arrays[i : i + 3]] for i in (6, 9))
        chunks, kinds, used, stages, segments = plan([w.shape for w in weights])
        results = gather_step(chunks, kinds, used, stages, segments, terms, weights, m, v)
        gathered, moments, onward = results[:3], results[3:9], results[9:]

        passed, crossed = [], []
        for s, piece in enumerate(onward):
            passed.append(lax.ppermute(piece, "dp", onward_to))
            crossed.append(lax.ppermute(passed[s], "dp", across))

        whole = [None] * 3
        sources = [*gathered[:2], *onward[:2]]
        moves = [u for i in (0, 1) for u in known_moves(chunks, i, i, [2, 3], i)]
        whole[:2] = move(moves, sources, gathered[:2])
        sources = [gathered[2], *onward[2:], *moments]
        moves = known_moves(chunks, 2, 0, [None, None, *range(1, len(stages) - 1)], 0)
        for a, array in enumerate(moments):
            for layer in range(array.shape[0]):
                for h in (0, 1):
                    at = lambda chip, core, layer=layer, h=h: (layer, h)
                    moves.append(Move(len(stages) - 1 + a, at, 1 + a, at, array.shape[2:]))
        whole[2], *moments = move(moves, sources, [gathered[2], *moments])

        for group in ([0], [1], [2], range(3, len(stages))):
            which = stages[group[0]][0][0].which
            sources, moves = [], []
            for s in group:
                moves += last_moves(stages[s], (len(sources), len(sources) + 1), 0)
                sources += [passed[s], crossed[s]]
            whole[which] = put(moves, sources, whole[which])
        return tuple(a.reshape(s) for a, s in zip((*whole, *moments), shapes[3:]))

    all_of, cut = P(None, None, None), P(None, "dp", None)
    return jax.shard_map(
        step,
        mesh=mesh,
        in_specs=(P(("rep", "dp"), None, None, None),) * 3 + (all_of,) * 3 + (cut,) * 6,
        out_specs=(P("rep", None, None),) * 3 + (P("rep", "dp", None),) * 6,
        check_vma=False,
    )
```

time: 375 us -> 384 us (1.024)
  waiting for transfers between devices: 0 us -> 47.9 us
  local copies, waits for them, and re-layouts: 44.5 us -> 2.87 us
  starting transfers between devices: 0 us -> 14.8 us
  Pallas kernels: 329 us -> 317 us
    ppermute x0 -> x10, waiting for transfers between devices: none -> 47.9 us  [the longest x5 47.9 us: step(): passed.append(lax.ppermute(piece, 'dp', onward_to))]
    unnamed x31 -> x12, local copies, waits for them, and re-layouts: 44.5 us -> 2.87 us
    ppermute x0 -> x10, starting transfers between devices: none -> 14.8 us  [the longest x5 10 us: step(): crossed.append(lax.ppermute(passed[s], 'dp', across))]
    pallas_call x1 -> x7, Pallas kernels: 329 us -> 317 us  [the longest x1 276 us: gather_step(): pl.pallas_call(functools.partial(exchange, chunks, kinds, stages), out_sh...]
  transfers between devices with their start and end apart: 0 -> 10, of which waited for: 0 -> 5; matrix products, arithmetic and copies ran while one was open for 0% -> 0% of each run, Pallas kernels for 0% -> 10%
where the time goes in v3:
time: 384 us
  Pallas kernels  317 us (83%)
  waiting for transfers between devices  47.9 us (12%)
  starting transfers between devices  14.8 us (4%)
    pallas_call x1, Pallas kernels, gather_step(): pl.pallas_call(functools.partial(exchange, chunks, kinds, stages), out_sh...  276 us
    ppermute x5, waiting for transfers between devices, step(): passed.append(lax.ppermute(piece, 'dp', onward_to))  47.9 us
    pallas_call x2, Pallas kernels, move(): pl.pallas_call(functools.partial(move_body, moves, kinds, depth, len(sour...  34.4 us
    ppermute x5, starting transfers between devices, step(): crossed.append(lax.ppermute(passed[s], 'dp', across))  10 us
  transfers between devices with their start and end apart: 10, of which 5 were waited for; matrix products, arithmetic and copies ran while one was open for 0% of the time, Pallas kernels for 10%

profile of v3, /device:TPU:113, one launch (start us, length us, event | category | flops | bytes accessed | tf_op | source)
XLA Modules:
  0.0 383.8 jit_solution(4867169553398904898)
XLA Ops:
  0.6 275.7 %shard_map.187 = (bf16[2,16,64,3200]{3,2,1,0:T(8,128)(2,1)}, bf16[2,16,64,3200]{3,2,1,0:T(8,128)(2,1)}, bf16[2,16,200,1024]{3,2,1,0:T(8,128)(2,1)}, f32[2,2,64,3...) custom-call(bf16[2,16,64,3200]{3,2,1,0:T(8,128)(2,1)} %bitcast.22, ...), custom_call_target="tpu_custom_call" | custom-call | tf_op jit(solution)/shard_map/pallas_call | solution.py:277
  276.4 1.8 collective-permute-start
  278.1 0.1 collective-permute-start.2
  278.2 0.9 collective-permute-start.8
  279.2 17.7 %collective-permute-done.refs_0_ = bf16[2,2,64,3200]{3,2,1,0:T(8,128)(2,1)S(1)} collective-permute-done((bf16[2,2,64,3200]{3,2,1,0:T(8,128)(2,1)}, bf16[2,2,64,3200]{3,2,1,0:T(8,128)(2,1)S(1)}, u32[]{:S(2)}, u32[]{:S(2)}) %collective-permute-start) | collective-permute-done | bytes 1638432 | tf_op jit(solution)/shard_map/ppermute | solution.py:457
  296.9 2.0 collective-permute-start.1
  298.9 15.6 %collective-permute-done.2.refs_0_ = bf16[2,2,64,3200]{3,2,1,0:T(8,128)(2,1)S(1)} collective-permute-done((bf16[2,2,64,3200]{3,2,1,0:T(8,128)(2,1)}, bf16[2,2,64,3200]{3,2,1,0:T(8,128)(2,1)S(1)}, u32[]{:S(2)}, u32[]{:S(2)}) %collective-permute-start.2) | collective-permute-done | bytes 1638432 | tf_op jit(solution)/shard_map/ppermute | solution.py:457
  314.5 2.0 collective-permute-start.3
  316.5 1.0 collective-permute-start.4
  317.5 5.8 %collective-permute-done.8.refs_0_ = bf16[1,2,200,1024]{3,2,1,0:T(8,128)(2,1)S(1)} collective-permute-done((bf16[1,2,200,1024]{3,2,1,0:T(8,128)(2,1)}, bf16[1,2,200,1024]{3,2,1,0:T(8,128)(2,1)S(1)}, u32[]{:S(2)}, u32[]{:S(2)}) %collective-permute-start.8) | collective-permute-done | bytes 819232 | tf_op jit(solution)/shard_map/ppermute | solution.py:457
  323.2 2.0 collective-permute-start.9
  325.2 4.4 %collective-permute-done.4.refs_0_ = bf16[1,2,144,1024]{3,2,1,0:T(8,128)(2,1)} collective-permute-done((bf16[1,2,144,1024]{3,2,1,0:T(8,128)(2,1)}, bf16[1,2,144,1024]{3,2,1,0:T(8,128)(2,1)}, u32[]{:S(2)}, u32[]{:S(2)}) %collective-permute-start.4) | collective-permute-done | bytes 589856 | tf_op jit(solution)/shard_map/ppermute | solution.py:457
  329.7 2.0 collective-permute-start.5
  331.7 1.0 collective-permute-start.6
  332.7 4.4 %collective-permute-done.6.refs_2_ = bf16[1,2,56,1024]{3,2,1,0:T(8,128)(2,1)S(1)} collective-permute-done((bf16[1,2,56,1024]{3,2,1,0:T(8,128)(2,1)}, bf16[1,2,56,1024]{3,2,1,0:T(8,128)(2,1)S(1)}, u32[]{:S(2)}, u32[]{:S(2)}) %collective-permute-start.6) | collective-permute-done | bytes 229408 | tf_op jit(solution)/shard_map/ppermute | solution.py:457
  337.0 2.1 collective-permute-start.7
  339.1 0.0 copy-start.1
  339.1 1.4 copy-done.1
  340.5 0.0 copy-start.2
  340.5 1.4 copy-done.2
  342.0 0.0 copy-start
  342.0 0.0 copy-start.3
  342.0 0.0 copy-start.4
  342.0 0.0 copy-start.5
  342.0 15.1 %shard_map.188 = (bf16[2,16,64,3200]{3,2,1,0:T(8,128)(2,1)}, bf16[2,16,64,3200]{3,2,1,0:T(8,128)(2,1)}) custom-call(bf16[2,16,64,3200]{3,2,1,0:T(8,128)(2,1)} %get-tuple-element.33.refs_0_, bf16[2,16,64,3200]{3,2,1,0:T(8,128)(2,1)} %get-tuple-element.34.refs_1_, bf16[2,2,64,3200]{3,2,1,0:T(8,128)(2,1)S(1)} %copy-done.1, bf16[2,2,64,3200]{3,2,1,0:T(8,128)(2,1)S(1)} %copy-done.2), custom_call_target="tpu_custom_call" | custom-call | flops 78643200 | bytes 39321600 | tf_op jit(solution)/shard_map/pallas_call | solution.py:352
  357.1 0.0 copy-done
  357.1 0.0 copy-done.3
  357.1 0.0 copy-done.4
  357.1 0.0 copy-done.5
  357.2 19.3 %shard_map.191 = (bf16[2,16,200,1024]{3,2,1,0:T(8,128)(2,1)}, f32[2,2,64,3200]{3,2,1,0:T(8,128)}, f32[2,2,64,3200]{3,2,1,0:T(8,128)}, f32[2,2,200,1024]{3,2,1,0:...) custom-call(bf16[2,16,200,1024]{3,2,1,0:T(8,128)(2,1)} %get-tuple-element.41.refs_0_, ...), custom_call_target="tpu_custom_call" | custom-call | flops 117964800 | bytes 58982400 | tf_op jit(solution)/shard_map/pallas_call | solution.py:352
  376.5 0.0 collective-permute-done.9.refs_1_
  376.5 1.2 shard_map.192.refs_4_
  377.7 0.0 collective-permute-done.7.refs_3_
  377.7 0.0 collective-permute-done.5.refs_1_
  377.7 2.5 shard_map.193
  380.2 0.0 collective-permute-done.1.refs_1_
  380.3 1.8 shard_map.189
  382.0 0.0 collective-permute-done.3.refs_1_
  382.1 1.8 shard_map.190
Async XLA Ops:
  276.4 20.6 %collective-permute-start = (bf16[2,2,64,3200]{3,2,1,0:T(8,128)(2,1)}, bf16[2,2,64,3200]{3,2,1,0:T(8,128)(2,1)S(1)}, u32[]{:S(2)}, u32[]{:S(2)}) collective-permute-start(bf16[2,2,64,3200]{3,2,1,0:T(8,128)(2,1)} %get-tuple-element.32.refs_2_), channel_id=1, source_target_pairs={{0,2},{1,7},{2,4},{3,1},{4,6},{5,3},{6,0},{7,5},{8,10},{9,15},{10,... | collective-permute-start | bytes 4915208 | tf_op jit(solution)/shard_map/ppermute | solution.py:457
  278.1 36.3 %collective-permute-start.2 = (bf16[2,2,64,3200]{3,2,1,0:T(8,128)(2,1)}, bf16[2,2,64,3200]{3,2,1,0:T(8,128)(2,1)S(1)}, u32[]{:S(2)}, u32[]{:S(2)}) collective-permute-start(bf16[2,2,64,3200]{3,2,1,0:T(8,128)(2,1)} %get-tuple-element.35.refs_3_), channel_id=1, source_target_pairs={{0,2},{1,7},{2,4},{3,1},{4,6},{5,3},{6,0},{7,5},{8,10},{9,15},{10,... | collective-permute-start | bytes 4915208 | tf_op jit(solution)/shard_map/ppermute | solution.py:457
  278.2 45.0 %collective-permute-start.8 = (bf16[1,2,200,1024]{3,2,1,0:T(8,128)(2,1)}, bf16[1,2,200,1024]{3,2,1,0:T(8,128)(2,1)S(1)}, u32[]{:S(2)}, u32[]{:S(2)}) collective-permute-start(bf16[1,2,200,1024]{3,2,1,0:T(8,128)(2,1)} %get-tuple-element.40.refs_1_), channel_id=1, source_target_pairs={{0,2},{1,7},{2,4},{3,1},{4,6},{5,3},{6,0},{7,5},{8,10},{9,15},{10,... | collective-permute-start | bytes 2457608 | tf_op jit(solution)/shard_map/ppermute | solution.py:457
  296.9 83.3 %collective-permute-start.1 = (bf16[2,2,64,3200]{3,2,1,0:T(8,128)(2,1)S(1)}, bf16[2,2,64,3200]{3,2,1,0:T(8,128)(2,1)S(1)}, u32[]{:S(2)}, u32[]{:S(2)}) collective-permute-start(bf16[2,2,64,3200]{3,2,1,0:T(8,128)(2,1)S(1)} %collective-permute-done.refs_0_), channel_id=1, source_target_pairs={{0,1},{1,0},{2,3},{3,2},{4,5},{5,4},{6,7},{7,6},{8,9},{9,8},{10,11... | collective-permute-start | bytes 4915208 | tf_op jit(solution)/shard_map/ppermute | solution.py:458
  314.5 67.6 %collective-permute-start.3 = (bf16[2,2,64,3200]{3,2,1,0:T(8,128)(2,1)S(1)}, bf16[2,2,64,3200]{3,2,1,0:T(8,128)(2,1)S(1)}, u32[]{:S(2)}, u32[]{:S(2)}) collective-permute-start(bf16[2,2,64,3200]{3,2,1,0:T(8,128)(2,1)S(1)} %collective-permute-done.2.refs_0_), channel_id=1, source_target_pairs={{0,1},{1,0},{2,3},{3,2},{4,5},{5,4},{6,7},{7,6},{8,9},{9,8},{10,11... | collective-permute-start | bytes 4915208 | tf_op jit(solution)/shard_map/ppermute | solution.py:458
  316.5 13.2 %collective-permute-start.4 = (bf16[1,2,144,1024]{3,2,1,0:T(8,128)(2,1)}, bf16[1,2,144,1024]{3,2,1,0:T(8,128)(2,1)}, u32[]{:S(2)}, u32[]{:S(2)}) collective-permute-start(bf16[1,2,144,1024]{3,2,1,0:T(8,128)(2,1)} %get-tuple-element.38.refs_2_), channel_id=1, source_target_pairs={{0,2},{1,7},{2,4},{3,1},{4,6},{5,3},{6,0},{7,5},{8,10},{9,15},{10,... | collective-permute-start | bytes 1769480 | tf_op jit(solution)/shard_map/ppermute | solution.py:457
  323.2 53.2 %collective-permute-start.9 = (bf16[1,2,200,1024]{3,2,1,0:T(8,128)(2,1)S(1)}, bf16[1,2,200,1024]{3,2,1,0:T(8,128)(2,1)S(1)}, u32[]{:S(2)}, u32[]{:S(2)}) collective-permute-start(bf16[1,2,200,1024]{3,2,1,0:T(8,128)(2,1)S(1)} %collective-permute-done.8.refs_0_), channel_id=1, source_target_pairs={{0,1},{1,0},{2,3},{3,2},{4,5},{5,4},{6,7},{7,6},{8,9},{9,8},{10,11... | collective-permute-start | bytes 2457608 | tf_op jit(solution)/shard_map/ppermute | solution.py:458
  329.7 48.0 %collective-permute-start.5 = (bf16[1,2,144,1024]{3,2,1,0:T(8,128)(2,1)}, bf16[1,2,144,1024]{3,2,1,0:T(8,128)(2,1)}, u32[]{:S(2)}, u32[]{:S(2)}) collective-permute-start(bf16[1,2,144,1024]{3,2,1,0:T(8,128)(2,1)} %collective-permute-done.4.refs_0_), channel_id=1, source_target_pairs={{0,1},{1,0},{2,3},{3,2},{4,5},{5,4},{6,7},{7,6},{8,9},{9,8},{10,11... | collective-permute-start | bytes 1769480 | tf_op jit(solution)/shard_map/ppermute | solution.py:458
  331.7 5.4 %collective-permute-start.6 = (bf16[1,2,56,1024]{3,2,1,0:T(8,128)(2,1)}, bf16[1,2,56,1024]{3,2,1,0:T(8,128)(2,1)S(1)}, u32[]{:S(2)}, u32[]{:S(2)}) collective-permute-start(bf16[1,2,56,1024]{3,2,1,0:T(8,128)(2,1)} %get-tuple-element.39.refs_3_), channel_id=1, source_target_pairs={{0,2},{1,7},{2,4},{3,1},{4,6},{5,3},{6,0},{7,5},{8,10},{9,15},{10,... | collective-permute-start | bytes 688136 | tf_op jit(solution)/shard_map/ppermute | solution.py:457
  337.0 40.7 %collective-permute-start.7 = (bf16[1,2,56,1024]{3,2,1,0:T(8,128)(2,1)S(1)}, bf16[1,2,56,1024]{3,2,1,0:T(8,128)(2,1)}, u32[]{:S(2)}, u32[]{:S(2)}) collective-permute-start(bf16[1,2,56,1024]{3,2,1,0:T(8,128)(2,1)S(1)} %collective-permute-done.6.refs_2_), channel_id=1, source_target_pairs={{0,1},{1,0},{2,3},{3,2},{4,5},{5,4},{6,7},{7,6},{8,9},{9,8},{10,11... | collective-permute-start | bytes 688136 | tf_op jit(solution)/shard_map/ppermute | solution.py:458
  339.1 1.4 copy-start.1
  340.5 1.4 copy-start.2
  342.0 15.2 %copy-start = (f32[2,2,64,3200]{3,2,1,0:T(8,128)S(1)}, f32[2,2,64,3200]{3,2,1,0:T(8,128)}, u32[]{:S(2)}) copy-start(f32[2,2,64,3200]{3,2,1,0:T(8,128)} %get-tuple-element.42.refs_4_) | copy-start | bytes 9830404
  342.0 15.2 %copy-start.3 = (bf16[1,2,200,1024]{3,2,1,0:T(8,128)(2,1)S(1)}, bf16[1,2,200,1024]{3,2,1,0:T(8,128)(2,1)}, u32[]{:S(2)}) copy-start(bf16[1,2,200,1024]{3,2,1,0:T(8,128)(2,1)} %get-tuple-element.40.refs_1_) | copy-start | bytes 2457604
  342.0 15.2 %copy-start.4 = (bf16[1,2,144,1024]{3,2,1,0:T(8,128)(2,1)S(1)}, bf16[1,2,144,1024]{3,2,1,0:T(8,128)(2,1)}, u32[]{:S(2)}) copy-start(bf16[1,2,144,1024]{3,2,1,0:T(8,128)(2,1)} %get-tuple-element.38.refs_2_) | copy-start | bytes 1769476
  342.0 15.2 %copy-start.5 = (bf16[1,2,56,1024]{3,2,1,0:T(8,128)(2,1)S(1)}, bf16[1,2,56,1024]{3,2,1,0:T(8,128)(2,1)}, u32[]{:S(2)}) copy-start(bf16[1,2,56,1024]{3,2,1,0:T(8,128)(2,1)} %get-tuple-element.39.refs_3_) | copy-start | bytes 688132

commit v4 on v3

--- a/solution.py
+++ b/solution.py
@@ -57,14 +57,15 @@
     return chunks, kinds, used, stages, count
 
 
-def exchange(chunks, kinds, stages, *refs):
+def exchange(chunks, kinds, stages, segments, *refs):
     it = iter(refs)
     take = lambda n: [next(it) for _ in range(n)]
     g, w, m, v = take(3), take(3), take(3), take(3)
     out, new_m, new_v, onward = take(3), take(3), take(3), take(len(stages))
     nk = len(kinds)
     peer, pass_in, near_in, own, w_in, m_in, v_in = (take(nk) for _ in range(7))
-    (x_send, x_recv, a_send, a_recv, b_send, b_recv, own_sem, in_sem, out_sem, g_send, g_recv, gx_send, gx_recv) = it
+    (first_in, first_sem, x_send, x_recv, a_send, a_recv, b_send, b_recv, own_sem, in_sem, out_sem, kept_sem, g_send, g_recv,
+     gx_send, gx_recv) = it
     n = len(chunks)
 
     me = lax.axis_index("dp")
@@ -80,14 +81,12 @@
     for d in (right, left, other):
         pl.semaphore_signal(barrier, inc=1, device_id={"dp": d}, device_id_type=MESH)
 
-    pending = []
-
     def remote(src, dst, send, recv, to):
-        copy = pltpu.make_async_remote_copy(
-            src_ref=src, dst_ref=dst, send_sem=send, recv_sem=recv, device_id={"dp": to}, device_id_type=MESH)
-        copy.start()
-        pending.append(copy)
-        return copy
+        pltpu.make_async_remote_copy(
+            src_ref=src, dst_ref=dst, send_sem=send, recv_sem=recv, device_id={"dp": to}, device_id_type=MESH).start()
+
+    def await_bytes(ref, sem):
+        pltpu.make_async_copy(ref, ref, sem).wait()
 
     order = [(OPPOSITE, c) for c in chunks]
     for c in chunks:
@@ -100,36 +99,42 @@
 
     def own_load(p):
         r, c = order[p]
+        slot = slots[r, c.number]
         return pltpu.make_async_copy(
-            g[c.which].at[c.layer, pl.ds((chip_at[r] * 2 + core) * 2, 2)],
-            own[c.kind].at[slots[r, c.number]], own_sem.at[r * n + c.number])
-
-    def state_loads(c):
+            g[c.which].at[c.layer, pl.ds((chip_at[r] * 2 + core) * 2, 2)], own[c.kind].at[slot], own_sem.at[c.kind * 3 + slot])
+
+    def load_state(c):
         s = c.place % 2
-        return [
-            pltpu.make_async_copy(w[c.which].at[c.layer, pl.ds(me * 2, 2)], w_in[c.kind].at[s], in_sem.at[c.number * 3]),
-            pltpu.make_async_copy(m[c.which].at[c.layer], m_in[c.kind].at[s], in_sem.at[c.number * 3 + 1]),
-            pltpu.make_async_copy(v[c.which].at[c.layer], v_in[c.kind].at[s], in_sem.at[c.number * 3 + 2]),
-        ]
-
+        sem = (c.kind * 2 + s) * 2
+        pltpu.make_async_copy(w[c.which].at[c.layer, pl.ds(me * 2, 2)], w_in[c.kind].at[s], in_sem.at[sem]).start()
+        pltpu.make_async_copy(m[c.which].at[c.layer], m_in[c.kind].at[s], in_sem.at[sem + 1]).start()
+        pltpu.make_async_copy(v[c.which].at[c.layer], v_in[c.kind].at[s], in_sem.at[sem + 1]).start()
+
+    first = chunks[0]
+    pieces = [(h, rows) for rows in ((0, FIRST_ROWS), (FIRST_ROWS, first.rows)) for h in (0, 1)]
+
+    def given(h, start, stop):
+        return g[first.which].at[first.layer, (chip_at[OPPOSITE] * 2 + (1 - core)) * 2 + h, pl.ds(start, stop - start)]
+
+    for h in (0, 1):
+        pltpu.make_async_copy(given(h, 0, FIRST_ROWS), first_in.at[h], first_sem.at[0]).start()
     own_load(0).start()
     own_load(1).start()
+    await_bytes(first_in, first_sem.at[0])
     pl.semaphore_wait(barrier, 3)
 
-    x = {}
-
     def swap(r, c):
-        x[r, c.number] = remote(
+        remote(
             g[c.which].at[c.layer, pl.ds((chip_at[r] * 2 + (1 - core)) * 2, 2)], peer[c.kind].at[r, c.place],
-            x_send.at[r * n + c.number], x_recv.at[r * n + c.number], other)
-
-    first = chunks[0]
-    pieces = [(h, rows) for rows in ((0, FIRST_ROWS), (FIRST_ROWS, first.rows)) for h in (0, 1)]
+            x_send.at[c.kind], x_recv.at[{OPPOSITE: 0, RIGHT: n, LEFT: n, OWN: 2 * n}[r] + c.number], other)
+
+    def first_piece(h, start, stop):
+        return peer[first.kind].at[OPPOSITE, first.place, h, pl.ds(start, stop - start)]
+
     for k, (h, (start, stop)) in enumerate(pieces):
-        s = 4 * n + k
-        x[OPPOSITE, h, start] = remote(
-            g[first.which].at[first.layer, (chip_at[OPPOSITE] * 2 + (1 - core)) * 2 + h, pl.ds(start, stop - start)],
-            peer[first.kind].at[OPPOSITE, first.place, h, pl.ds(start, stop - start)], x_send.at[s], x_recv.at[s], other)
+        remote(
+            first_in.at[h] if start == 0 else given(h, start, stop), first_piece(h, start, stop),
+            x_send.at[first.kind], x_recv.at[3 * n + k], other)
     for c in chunks[1:]:
         swap(OPPOSITE, c)
 
@@ -142,8 +147,10 @@
         if p + 2 < len(order):
             own_load(p + 2).start()
         own_load(p).wait()
-        if (r, c.number) in x:
-            x[r, c.number].wait_recv()
+        if r == RIGHT:
+            await_bytes(peer[c.kind].at[pl.ds(RIGHT, 2), c.place], x_recv.at[n + c.number])
+        elif r == OWN or r == OPPOSITE and c is not first:
+            await_bytes(peer[c.kind].at[r, c.place], x_recv.at[(0 if r == OPPOSITE else 2 * n) + c.number])
         return own[c.kind].at[slots[r, c.number]], peer[c.kind].at[r, c.place]
 
     def tiles(c, start, stop, body):
@@ -168,50 +175,44 @@
 
         tiles(c, *(rows or (0, c.rows)), tile)
 
-    step0 = {}
     for c in chunks:
         mine, theirs = take_own(OPPOSITE, c)
-        for h, (start, stop) in pieces if c is first else [(0, (0, c.rows)), (1, (0, c.rows))]:
+        for k, (h, (start, stop)) in enumerate(pieces if c is first else [(0, (0, c.rows)), (1, (0, c.rows))]):
             if c is first:
-                x[OPPOSITE, h, start].wait_recv()
+                await_bytes(first_piece(h, start, stop), x_recv.at[3 * n + k])
             add(c, h, mine, theirs, rows=(start, stop))
-            s = h * n + c.number if start == 0 else 2 * n + h
-            step0.setdefault((h, c.number), []).append(remote(
+            remote(
                 theirs.at[h, pl.ds(start, stop - start)], pass_in[c.kind].at[c.place, h, pl.ds(start, stop - start)],
-                a_send.at[s], a_recv.at[s], (right, left)[h]))
+                a_send.at[c.kind], a_recv.at[c.number], (right, left)[h])
         swap(RIGHT, c)
         swap(LEFT, c)
 
-    step1 = {}
     for c in chunks:
         for r, to, side in ((RIGHT, right, 0), (LEFT, left, 1)):
             mine, theirs = take_own(r, c)
+            if r == RIGHT:
+                await_bytes(pass_in[c.kind].at[c.place], a_recv.at[c.number])
             for h in (side, 1 - side):
-                if h == side:
-                    for copy in step0[h, c.number]:
-                        copy.wait_recv()
-                    add(c, h, mine, theirs, pass_in[c.kind].at[c.place])
-                else:
-                    add(c, h, mine, theirs)
-                s = (side * n + c.number) * 2 + h
-                step1[side, c.number, h] = remote(
-                    theirs.at[h], near_in[c.kind].at[side, c.place, h], b_send.at[s], b_recv.at[s], to)
+                add(c, h, mine, theirs, *([pass_in[c.kind].at[c.place]] if h == side else []))
+                remote(theirs.at[h], near_in[c.kind].at[side, c.place, h], b_send.at[c.kind], b_recv.at[c.number], to)
         swap(OWN, c)
 
     for c in chunks[:2]:
-        for copy in state_loads(c):
-            copy.start()
-    arrivals, crossing, stores = {}, [], {}
+        load_state(c)
+    storing = []
+
+    def await_moments(c):
+        await_bytes(m_in[c.kind], out_sem.at[c.kind * 2 + c.place % 2])
+
     for c in chunks:
         mine, theirs = take_own(OWN, c)
-        for copy in state_loads(c):
-            copy.wait()
         s = c.place % 2
+        await_bytes(w_in[c.kind].at[s], in_sem.at[(c.kind * 2 + s) * 2])
+        await_bytes(m_in[c.kind], in_sem.at[(c.kind * 2 + s) * 2 + 1])
+        await_bytes(near_in[c.kind].at[:, c.place], b_recv.at[c.number])
         from_left, from_right = near_in[c.kind].at[0, c.place], near_in[c.kind].at[1, c.place]
         w_ref, m_ref, v_ref = w_in[c.kind].at[s], m_in[c.kind].at[s], v_in[c.kind].at[s]
         for h in (0, 1):
-            step1[0, c.number, h].wait_recv()
-            step1[1, c.number, h].wait_recv()
 
             def tile(r, k):
                 total = mine[h, r, k].astype(F32) + theirs[h, r, k].astype(F32)
@@ -225,65 +226,75 @@
             rows = pl.ds(start, size)
             for k, (h, to) in enumerate(((core, ahead), (1 - core, ahead), (1 - core, behind), (core, behind))):
                 dst = onward[stage].at[index, core] if k == 0 else out[c.which].at[c.layer, me * 2 + h, rows]
-                arrivals[number, k] = remote(
-                    theirs.at[h, rows], dst, g_send.at[number * 4 + k], g_recv.at[number * 4 + k], to)
+                if number == segments - 1:
+                    dst = onward[stage].at[k]
+                remote(theirs.at[h, rows], dst, g_send.at[c.kind], g_recv.at[number], to)
         target = out[c.which].at[c.layer, pl.ds(me * 2, 2)]
-        crossing.append(remote(theirs, target, gx_send.at[c.number], gx_recv.at[c.number], other))
-        stores[c.number] = [
-            pltpu.make_async_copy(theirs, target, out_sem.at[c.number * 3]),
-            pltpu.make_async_copy(m_ref, new_m[c.which].at[c.layer], out_sem.at[c.number * 3 + 1]),
-            pltpu.make_async_copy(v_ref, new_v[c.which].at[c.layer], out_sem.at[c.number * 3 + 2]),
-        ]
-        for copy in stores[c.number]:
-            copy.start()
-        if c.number + 1 < n and c.number >= 1:
+        remote(theirs, target, gx_send.at[c.kind], gx_recv.at[c.kind], other)
+        pltpu.make_async_copy(theirs, target, kept_sem.at[c.kind]).start()
+        pltpu.make_async_copy(m_ref, new_m[c.which].at[c.layer], out_sem.at[c.kind * 2 + s]).start()
+        pltpu.make_async_copy(v_ref, new_v[c.which].at[c.layer], out_sem.at[c.kind * 2 + s]).start()
+        storing.append(c)
+        if 1 <= c.number < n - 1:
             following = chunks[c.number + 1]
-            for before in chunks[: c.number]:
+            for before in storing[:-1]:
                 if before.kind == following.kind and before.place == following.place - 2:
-                    for copy in stores.pop(before.number):
-                        copy.wait()
-            for copy in state_loads(following):
-                copy.start()
-
+                    await_moments(before)
+                    storing.remove(before)
+            load_state(following)
+
+    several = {}
     for c in chunks:
         for number, stage, index, start, size in c.segments:
             rows = pl.ds(start, size)
+            await_bytes(near_in[c.kind].at[:, c.place, :, rows], g_recv.at[number])
+            if number == segments - 1:
+                continue
+            sem = nk + (c.kind if size == c.rows else nk)
+            several.setdefault(sem, []).append((c, rows))
             for k, (h, owner) in enumerate(
                 ((core, behind_chip), (1 - core, behind_chip), (1 - core, ahead_chip), (core, ahead_chip))):
-                s = n + number * 4 + k
-                arrivals[number, k].wait_recv()
                 there = out[c.which].at[c.layer, (owner * 2 + core) * 2 + h, rows]
-                crossing.append(remote(
+                remote(
                     onward[stage].at[index, core] if k == 0 else there,
-                    onward[stage].at[index, core] if k == 2 else there, gx_send.at[s], gx_recv.at[s], other))
-    for copy in crossing:
-        copy.wait_recv()
-    for copies in stores.values():
-        for copy in copies:
-            copy.wait()
-    for copy in pending:
-        copy.wait_send()
+                    onward[stage].at[index, core] if k == 2 else there, gx_send.at[sem], gx_recv.at[sem], other)
+    for c in storing:
+        await_moments(c)
+    for kind in range(nk):
+        await_bytes(peer[kind], x_send.at[kind])
+        await_bytes(peer[kind].at[0], a_send.at[kind])
+        await_bytes(peer[kind].at[pl.ds(1, 2)], b_send.at[kind])
+        await_bytes(peer[kind].at[pl.ds(0, 2)], g_send.at[kind])
+        await_bytes(peer[kind].at[0], gx_send.at[kind])
+        await_bytes(peer[kind].at[0], gx_recv.at[kind])
+        await_bytes(peer[kind].at[0], kept_sem.at[kind])
+    for sem, parts in several.items():
+        c, rows = parts[0]
+        for sems in (gx_send, gx_recv):
+            await_bytes(near_in[c.kind].at[:, pl.ds(0, len(parts)), :, rows], sems.at[sem])
 
 
 def gather_step(chunks, kinds, used, stages, segments, terms, weights, m, v):
-    n = len(chunks)
+    n, nk = len(chunks), len(kinds)
     hbm = pl.BlockSpec(memory_space=pltpu.HBM)
     slots = lambda lead, dtype: [
         pltpu.VMEM((*(u if x is None else x for x in lead), 2, *k), dtype) for k, u in zip(kinds, used)]
     dma = lambda count: pltpu.SemaphoreType.DMA((count,))
     results = [jax.ShapeDtypeStruct(w.shape, BF16) for w in weights]
     results += [jax.ShapeDtypeStruct(a.shape, F32) for a in (*m, *v)]
-    results += [jax.ShapeDtypeStruct((len(s), 2, s[0][2], s[0][0].cols), BF16) for s in stages]
+    results += [jax.ShapeDtypeStruct((len(s), 2, s[0][2], s[0][0].cols), BF16) for s in stages[:-1]]
+    results += [jax.ShapeDtypeStruct((4, s[0][2], s[0][0].cols), BF16) for s in stages[-1:]]
     return pl.pallas_call(
-        functools.partial(exchange, chunks, kinds, stages),
+        functools.partial(exchange, chunks, kinds, stages, segments),
         out_shape=results,
         in_specs=[hbm] * 12,
         out_specs=[hbm] * len(results),
         scratch_shapes=[
             *slots((4, None), BF16), *slots((None,), BF16), *slots((2, None), BF16), *slots((3,), BF16),
             *slots((2,), BF16), *slots((2,), F32), *slots((2,), F32),
-            dma(4 * n + 4), dma(4 * n + 4), dma(2 * n + 2), dma(2 * n + 2), dma(4 * n), dma(4 * n), dma(4 * n), dma(3 * n),
-            dma(3 * n), dma(4 * segments), dma(4 * segments), dma(n + 4 * segments), dma(n + 4 * segments),
+            pltpu.VMEM((2, FIRST_ROWS, chunks[0].cols), BF16), dma(1),
+            dma(nk), dma(3 * n + 4), dma(nk), dma(n), dma(nk), dma(n), dma(3 * nk), dma(4 * nk), dma(2 * nk), dma(nk),
+            dma(nk), dma(segments), dma(2 * nk + 1), dma(2 * nk + 1),
         ],
         compiler_params=pltpu.CompilerParams(collective_id=0, has_side_effects=True, vmem_limit_bytes=VMEM_LIMIT),
     )(*terms, *weights, *m, *v)
@@ -392,10 +403,10 @@
 
 
 def known_moves(chunks, which, source, onward, target):
-    def block(c, r, parity):
+    def block(c, r, parity, size):
         def at(chip, core):
             owner = lax.rem(chip + (0 if r == OWN else 1 + 2 * core), CHIPS) * 2 + parity
-            return c.layer, pl.ds(owner * 2, 2)
+            return c.layer, pl.ds(owner * 2, 2), pl.ds(0, size)
 
         return at
 
@@ -408,26 +419,42 @@
 
     moves = []
     for c in (c for c in chunks if c.which == which):
+        segments = [segment for segment in c.segments if onward[segment[1]] is not None]
+        known = sum(segment[-1] for segment in segments)
         for parity in (0, 1):
-            for r in (OWN, RIGHT):
-                at = block(c, r, parity)
-                moves.append(Move(source, at, target, at, (2, c.rows, c.cols)))
-            at = behind(c, parity, False, 0, c.rows)
-            moves.append(Move(source, at, target, at, (c.rows, c.cols)))
-            for _, stage, index, start, size in c.segments:
+            for r, size in ((OWN, c.rows), (RIGHT, known)):
+                at = block(c, r, parity, size)
+                moves.append(Move(source, at, target, at, (2, size, c.cols)))
+            at = behind(c, parity, False, 0, known)
+            moves.append(Move(source, at, target, at, (known, c.cols)))
+            for _, stage, index, start, size in segments:
                 at = lambda chip, core, index=index, parity=parity: (index, parity)
                 moves.append(Move(onward[stage], at, target, behind(c, parity, True, start, size), (size, c.cols)))
     return moves
 
 
-def last_moves(stage, sources, target):
+def late_moves(stage, sources, target):
+    (c, start, size), moves = stage[0], []
+    for k, source in enumerate(sources):
+        for i in range(4):
+            def to(chip, core, k=k, i=i):
+                there = core if k == 0 else 1 - core
+                owner = lax.rem(chip + (3 - 2 * there if i < 2 else 1 + 2 * there), CHIPS) * 2 + there
+                return c.layer, owner * 2 + (there if i in (0, 3) else 1 - there), pl.ds(start, size)
+
+            moves.append(Move(source, lambda chip, core, i=i: (i,), target, to, (size, c.cols)))
+    return moves
+
+
+def last_moves(stage, sources, target, joined=False):
     moves = []
     for index, (c, start, size) in enumerate(stage):
         for k, source in enumerate(sources):
             for parity in (0, 1):
                 def to(chip, core, c=c, start=start, size=size, k=k, parity=parity):
-                    owner = lax.rem(chip + 2, CHIPS) * 2 + parity
-                    return c.layer, owner * 2 + (core if k == 0 else 1 - core), pl.ds(start, size)
+                    half = core if k == 0 else 1 - core
+                    owner = lax.rem(chip + 2, CHIPS) * 2 + ((half if parity == 0 else 1 - half) if joined else parity)
+                    return c.layer, owner * 2 + half, pl.ds(start, size)
 
                 at = lambda chip, core, index=index, parity=parity: (index, parity)
                 moves.append(Move(source, at, target, to, (size, c.cols)))
@@ -450,8 +477,10 @@
         m, v = ([halves(a, 2) for a in arrays[i : i + 3]] for i in (6, 9))
         chunks, kinds, used, stages, segments = plan([w.shape for w in weights])
         results = gather_step(chunks, kinds, used, stages, segments, terms, weights, m, v)
-        gathered, moments, onward = results[:3], results[3:9], results[9:]
-
+        gathered, moments, onward = results[:3], results[3:9], list(results[9:])
+
+        late = onward[-1], lax.ppermute(onward[-1], "dp", across)
+        onward[-1] = jnp.stack([late[0][0], late[1][2]])[None]
         passed, crossed = [], []
         for s, piece in enumerate(onward):
             passed.append(lax.ppermute(piece, "dp", onward_to))
@@ -461,21 +490,25 @@
         sources = [*gathered[:2], *onward[:2]]
         moves = [u for i in (0, 1) for u in known_moves(chunks, i, i, [2, 3], i)]
         whole[:2] = move(moves, sources, gathered[:2])
-        sources = [gathered[2], *onward[2:], *moments]
-        moves = known_moves(chunks, 2, 0, [None, None, *range(1, len(stages) - 1)], 0)
+        sources = [gathered[2], *onward[2:-1], *moments]
+        first = len(sources) - len(moments)
+        moves = known_moves(chunks, 2, 0, [None, None, *range(1, first), None], 0)
         for a, array in enumerate(moments):
             for layer in range(array.shape[0]):
                 for h in (0, 1):
                     at = lambda chip, core, layer=layer, h=h: (layer, h)
-                    moves.append(Move(len(stages) - 1 + a, at, 1 + a, at, array.shape[2:]))
+                    moves.append(Move(first + a, at, 1 + a, at, array.shape[2:]))
         whole[2], *moments = move(moves, sources, [gathered[2], *moments])
 
-        for group in ([0], [1], [2], range(3, len(stages))):
+        for place, group in enumerate(([0], [1], [2], range(3, len(stages)))):
             which = stages[group[0]][0][0].which
             sources, moves = [], []
             for s in group:
-                moves += last_moves(stages[s], (len(sources), len(sources) + 1), 0)
+                moves += last_moves(stages[s], (len(sources), len(sources) + 1), 0, joined=s == len(stages) - 1)
                 sources += [passed[s], crossed[s]]
+            if place == 2:
+                moves += late_moves(stages[-1], (2, 3), 0)
+                sources += late
             whole[which] = put(moves, sources, whole[which])
         return tuple(a.reshape(s) for a, s in zip((*whole, *moments), shapes[3:]))
 

time: 384 us -> 382 us (level)
    pallas_call x1, Pallas kernels: 276 us -> 272 us  [gather_step(): pl.pallas_call(functools.partial(exchange, chunks, kinds, stages, segment...]
  transfers between devices with their start and end apart: 10 -> 11, of which waited for: 5 -> 5; matrix products, arithmetic and copies ran while one was open for 0% -> 0% of each run, Pallas kernels for 10% -> 11%
where the time goes in v4:
time: 382 us
  Pallas kernels  314 us (82%)
  waiting for transfers between devices  48.1 us (13%)
  starting transfers between devices  15.2 us (4%)
    pallas_call x1, Pallas kernels, gather_step(): pl.pallas_call(functools.partial(exchange, chunks, kinds, stages, segment...  272 us
    ppermute x5, waiting for transfers between devices, step(): passed.append(lax.ppermute(piece, 'dp', onward_to))  48.1 us
    pallas_call x2, Pallas kernels, move(): pl.pallas_call(functools.partial(move_body, moves, kinds, depth, len(sour...  34.1 us
    ppermute x5, starting transfers between devices, step(): crossed.append(lax.ppermute(passed[s], 'dp', across))  12.3 us
    pallas_call x4, Pallas kernels, put(): pl.pallas_call(functools.partial(put_body, moves, len(sources) + 1), out_...  7.74 us
  transfers between devices with their start and end apart: 11, of which 5 were waited for; matrix products, arithmetic and copies ran while one was open for 0% of the time, Pallas kernels for 11%

profile of v4, /device:TPU:113, one launch (start us, length us, event | category | flops | bytes accessed | tf_op | source)
XLA Modules:
  0.0 381.6 jit_solution(8193174219859095256)
XLA Ops:
  0.6 271.8 %shard_map.187 = (bf16[2,16,64,3200]{3,2,1,0:T(8,128)(2,1)}, bf16[2,16,64,3200]{3,2,1,0:T(8,128)(2,1)}, bf16[2,16,200,1024]{3,2,1,0:T(8,128)(2,1)}, f32[2,2,64,3...) custom-call(bf16[2,16,64,3200]{3,2,1,0:T(8,128)(2,1)} %bitcast.24, ...), custom_call_target="tpu_custom_call" | custom-call | tf_op jit(solution)/shard_map/pallas_call | solution.py:287
  272.4 1.6 collective-permute-start.2
  274.1 0.1 collective-permute-start
  274.2 0.6 collective-permute-start.9
  274.8 18.2 %collective-permute-done.2.refs_0_ = bf16[2,2,64,3200]{3,2,1,0:T(8,128)(2,1)S(1)} collective-permute-done((bf16[2,2,64,3200]{3,2,1,0:T(8,128)(2,1)}, bf16[2,2,64,3200]{3,2,1,0:T(8,128)(2,1)S(1)}, u32[]{:S(2)}, u32[]{:S(2)}) %collective-permute-start.2) | collective-permute-done | bytes 1638432 | tf_op jit(solution)/shard_map/ppermute | solution.py:486
  293.0 2.5 collective-permute-start.3
  295.5 15.0 %collective-permute-done.refs_0_ = bf16[2,2,64,3200]{3,2,1,0:T(8,128)(2,1)S(1)} collective-permute-done((bf16[2,2,64,3200]{3,2,1,0:T(8,128)(2,1)}, bf16[2,2,64,3200]{3,2,1,0:T(8,128)(2,1)S(1)}, u32[]{:S(2)}, u32[]{:S(2)}) %collective-permute-start) | collective-permute-done | bytes 1638432 | tf_op jit(solution)/shard_map/ppermute | solution.py:486
  310.6 2.5 collective-permute-start.1
  313.1 0.3 collective-permute-start.4
  313.4 0.0 collective-permute-start.6
  313.4 6.0 %collective-permute-done.9.refs_0_ = bf16[1,2,200,1024]{3,2,1,0:T(8,128)(2,1)S(1)} collective-permute-done((bf16[1,2,200,1024]{3,2,1,0:T(8,128)(2,1)}, bf16[1,2,200,1024]{3,2,1,0:T(8,128)(2,1)S(1)}, u32[]{:S(2)}, u32[]{:S(2)}) %collective-permute-start.9) | collective-permute-done | bytes 819232 | tf_op jit(solution)/shard_map/ppermute | solution.py:486
  319.3 2.5 collective-permute-start.10
  321.9 3.9 %collective-permute-done.4.refs_0_ = bf16[1,2,144,1024]{3,2,1,0:T(8,128)(2,1)} collective-permute-done((bf16[1,2,144,1024]{3,2,1,0:T(8,128)(2,1)}, bf16[1,2,144,1024]{3,2,1,0:T(8,128)(2,1)}, u32[]{:S(2)}, u32[]{:S(2)}) %collective-permute-start.4) | collective-permute-done | bytes 589856 | tf_op jit(solution)/shard_map/ppermute | solution.py:486
  325.8 2.5 collective-permute-start.5
  328.3 0.9 slice.6
  329.2 0.0 collective-permute-done.6.refs_3_
  329.3 0.3 collective-permute-start.7
  329.6 5.0 %collective-permute-done.7.refs_2_ = bf16[1,2,56,1024]{3,2,1,0:T(8,128)(2,1)} collective-permute-done((bf16[1,2,56,1024]{3,2,1,0:T(8,128)(2,1)S(1)}, bf16[1,2,56,1024]{3,2,1,0:T(8,128)(2,1)}, u32[]{:S(2)}, u32[]{:S(2)}) %collective-permute-start.7) | collective-permute-done | bytes 229408 | tf_op jit(solution)/shard_map/ppermute | solution.py:486
  334.6 2.1 collective-permute-start.8
  336.7 0.0 copy-start.1
  336.7 1.4 copy-done.1
  338.1 0.0 copy-start.2
  338.1 1.4 copy-done.2
  339.5 0.0 copy-start
  339.5 0.0 copy-start.3
  339.5 0.0 copy-start.5
  339.6 15.1 %shard_map.188 = (bf16[2,16,64,3200]{3,2,1,0:T(8,128)(2,1)}, bf16[2,16,64,3200]{3,2,1,0:T(8,128)(2,1)}) custom-call(bf16[2,16,64,3200]{3,2,1,0:T(8,128)(2,1)} %get-tuple-element.33.refs_0_, bf16[2,16,64,3200]{3,2,1,0:T(8,128)(2,1)} %get-tuple-element.34.refs_1_, bf16[2,2,64,3200]{3,2,1,0:T(8,128)(2,1)S(1)} %copy-done.1, bf16[2,2,64,3200]{3,2,1,0:T(8,128)(2,1)S(1)} %copy-done.2), custom_call_target="tpu_custom_call" | custom-call | flops 78643200 | bytes 39321600 | tf_op jit(solution)/shard_map/pallas_call | solution.py:363
  354.6 0.0 copy-done
  354.6 0.0 copy-done.3
  354.7 0.0 copy-done.5
  354.7 0.0 copy-start.4
  354.7 19.1 %shard_map.191 = (bf16[2,16,200,1024]{3,2,1,0:T(8,128)(2,1)}, f32[2,2,64,3200]{3,2,1,0:T(8,128)}, f32[2,2,64,3200]{3,2,1,0:T(8,128)}, f32[2,2,200,1024]{3,2,1,0:...) custom-call(bf16[2,16,200,1024]{3,2,1,0:T(8,128)(2,1)} %get-tuple-element.41.refs_0_, ...), custom_call_target="tpu_custom_call" | custom-call | flops 114294784 | bytes 57147392 | tf_op jit(solution)/shard_map/pallas_call | solution.py:363
  373.7 0.0 collective-permute-done.10.refs_1_
  373.8 0.0 copy-done.4
  373.8 1.6 shard_map.192.refs_4_
  375.3 0.0 collective-permute-done.8.refs_3_
  375.4 0.0 collective-permute-done.5.refs_1_
  375.4 2.6 shard_map.193
  378.0 0.0 collective-permute-done.3.refs_1_
  378.0 1.8 shard_map.190
  379.8 0.0 collective-permute-done.1.refs_1_
  379.8 1.8 shard_map.189
  (2 shorter events, 0.0 us)
Async XLA Ops:
  272.4 20.6 %collective-permute-start.2 = (bf16[2,2,64,3200]{3,2,1,0:T(8,128)(2,1)}, bf16[2,2,64,3200]{3,2,1,0:T(8,128)(2,1)S(1)}, u32[]{:S(2)}, u32[]{:S(2)}) collective-permute-start(bf16[2,2,64,3200]{3,2,1,0:T(8,128)(2,1)} %get-tuple-element.35.refs_3_), channel_id=1, source_target_pairs={{0,2},{1,7},{2,4},{3,1},{4,6},{5,3},{6,0},{7,5},{8,10},{9,15},{10,... | collective-permute-start | bytes 4915208 | tf_op jit(solution)/shard_map/ppermute | solution.py:486
  274.1 36.5 %collective-permute-start = (bf16[2,2,64,3200]{3,2,1,0:T(8,128)(2,1)}, bf16[2,2,64,3200]{3,2,1,0:T(8,128)(2,1)S(1)}, u32[]{:S(2)}, u32[]{:S(2)}) collective-permute-start(bf16[2,2,64,3200]{3,2,1,0:T(8,128)(2,1)} %get-tuple-element.32.refs_2_), channel_id=1, source_target_pairs={{0,2},{1,7},{2,4},{3,1},{4,6},{5,3},{6,0},{7,5},{8,10},{9,15},{10,... | collective-permute-start | bytes 4915208 | tf_op jit(solution)/shard_map/ppermute | solution.py:486
  274.2 45.1 %collective-permute-start.9 = (bf16[1,2,200,1024]{3,2,1,0:T(8,128)(2,1)}, bf16[1,2,200,1024]{3,2,1,0:T(8,128)(2,1)S(1)}, u32[]{:S(2)}, u32[]{:S(2)}) collective-permute-start(bf16[1,2,200,1024]{3,2,1,0:T(8,128)(2,1)} %get-tuple-element.40.refs_1_), channel_id=1, source_target_pairs={{0,2},{1,7},{2,4},{3,1},{4,6},{5,3},{6,0},{7,5},{8,10},{9,15},{10,... | collective-permute-start | bytes 2457608 | tf_op jit(solution)/shard_map/ppermute | solution.py:486
  293.0 85.0 %collective-permute-start.3 = (bf16[2,2,64,3200]{3,2,1,0:T(8,128)(2,1)S(1)}, bf16[2,2,64,3200]{3,2,1,0:T(8,128)(2,1)S(1)}, u32[]{:S(2)}, u32[]{:S(2)}) collective-permute-start(bf16[2,2,64,3200]{3,2,1,0:T(8,128)(2,1)S(1)} %collective-permute-done.2.refs_0_), channel_id=1, source_target_pairs={{0,1},{1,0},{2,3},{3,2},{4,5},{5,4},{6,7},{7,6},{8,9},{9,8},{10,11... | collective-permute-start | bytes 4915208 | tf_op jit(solution)/shard_map/ppermute | solution.py:487
  310.6 69.2 %collective-permute-start.1 = (bf16[2,2,64,3200]{3,2,1,0:T(8,128)(2,1)S(1)}, bf16[2,2,64,3200]{3,2,1,0:T(8,128)(2,1)S(1)}, u32[]{:S(2)}, u32[]{:S(2)}) collective-permute-start(bf16[2,2,64,3200]{3,2,1,0:T(8,128)(2,1)S(1)} %collective-permute-done.refs_0_), channel_id=1, source_target_pairs={{0,1},{1,0},{2,3},{3,2},{4,5},{5,4},{6,7},{7,6},{8,9},{9,8},{10,11... | collective-permute-start | bytes 4915208 | tf_op jit(solution)/shard_map/ppermute | solution.py:487
  313.1 12.7 %collective-permute-start.4 = (bf16[1,2,144,1024]{3,2,1,0:T(8,128)(2,1)}, bf16[1,2,144,1024]{3,2,1,0:T(8,128)(2,1)}, u32[]{:S(2)}, u32[]{:S(2)}) collective-permute-start(bf16[1,2,144,1024]{3,2,1,0:T(8,128)(2,1)} %get-tuple-element.38.refs_2_), channel_id=1, source_target_pairs={{0,2},{1,7},{2,4},{3,1},{4,6},{5,3},{6,0},{7,5},{8,10},{9,15},{10,... | collective-permute-start | bytes 1769480 | tf_op jit(solution)/shard_map/ppermute | solution.py:486
  313.4 15.8 %collective-permute-start.6 = (bf16[4,56,1024]{2,1,0:T(8,128)(2,1)}, bf16[4,56,1024]{2,1,0:T(8,128)(2,1)S(1)}, u32[]{:S(2)}, u32[]{:S(2)}) collective-permute-start(bf16[4,56,1024]{2,1,0:T(8,128)(2,1)} %get-tuple-element.39.refs_2_), channel_id=1, source_target_pairs={{0,1},{1,0},{2,3},{3,2},{4,5},{5,4},{6,7},{7,6},{8,9},{9,8},{10,11... | collective-permute-start | bytes 1376264 | tf_op jit(solution)/shard_map/ppermute | solution.py:482
  319.3 54.4 %collective-permute-start.10 = (bf16[1,2,200,1024]{3,2,1,0:T(8,128)(2,1)S(1)}, bf16[1,2,200,1024]{3,2,1,0:T(8,128)(2,1)S(1)}, u32[]{:S(2)}, u32[]{:S(2)}) collective-permute-start(bf16[1,2,200,1024]{3,2,1,0:T(8,128)(2,1)S(1)} %collective-permute-done.9.refs_0_), channel_id=1, source_target_pairs={{0,1},{1,0},{2,3},{3,2},{4,5},{5,4},{6,7},{7,6},{8,9},{9,8},{10,11... | collective-permute-start | bytes 2457608 | tf_op jit(solution)/shard_map/ppermute | solution.py:487
  325.8 49.6 %collective-permute-start.5 = (bf16[1,2,144,1024]{3,2,1,0:T(8,128)(2,1)}, bf16[1,2,144,1024]{3,2,1,0:T(8,128)(2,1)}, u32[]{:S(2)}, u32[]{:S(2)}) collective-permute-start(bf16[1,2,144,1024]{3,2,1,0:T(8,128)(2,1)} %collective-permute-done.4.refs_0_), channel_id=1, source_target_pairs={{0,1},{1,0},{2,3},{3,2},{4,5},{5,4},{6,7},{7,6},{8,9},{9,8},{10,11... | collective-permute-start | bytes 1769480 | tf_op jit(solution)/shard_map/ppermute | solution.py:487
  329.3 5.3 %collective-permute-start.7 = (bf16[1,2,56,1024]{3,2,1,0:T(8,128)(2,1)S(1)}, bf16[1,2,56,1024]{3,2,1,0:T(8,128)(2,1)}, u32[]{:S(2)}, u32[]{:S(2)}) collective-permute-start(bf16[1,2,56,1024]{3,2,1,0:T(8,128)(2,1)S(1)} %maximum_bitcast_fusion), channel_id=1, source_target_pairs={{0,2},{1,7},{2,4},{3,1},{4,6},{5,3},{6,0},{7,5},{8,10},{9,15},{10,... | collective-permute-start | bytes 688136 | tf_op jit(solution)/shard_map/ppermute | solution.py:486
  334.6 40.7 %collective-permute-start.8 = (bf16[1,2,56,1024]{3,2,1,0:T(8,128)(2,1)}, bf16[1,2,56,1024]{3,2,1,0:T(8,128)(2,1)}, u32[]{:S(2)}, u32[]{:S(2)}) collective-permute-start(bf16[1,2,56,1024]{3,2,1,0:T(8,128)(2,1)} %collective-permute-done.7.refs_2_), channel_id=1, source_target_pairs={{0,1},{1,0},{2,3},{3,2},{4,5},{5,4},{6,7},{7,6},{8,9},{9,8},{10,11... | collective-permute-start | bytes 688136 | tf_op jit(solution)/shard_map/ppermute | solution.py:487
  336.7 1.4 copy-start.1
  338.1 1.4 copy-start.2
  339.5 15.1 %copy-start = (f32[2,2,64,3200]{3,2,1,0:T(8,128)S(1)}, f32[2,2,64,3200]{3,2,1,0:T(8,128)}, u32[]{:S(2)}) copy-start(f32[2,2,64,3200]{3,2,1,0:T(8,128)} %get-tuple-element.42.refs_3_) | copy-start | bytes 9830404
  339.5 15.1 %copy-start.3 = (bf16[1,2,200,1024]{3,2,1,0:T(8,128)(2,1)S(1)}, bf16[1,2,200,1024]{3,2,1,0:T(8,128)(2,1)}, u32[]{:S(2)}) copy-start(bf16[1,2,200,1024]{3,2,1,0:T(8,128)(2,1)} %get-tuple-element.40.refs_1_) | copy-start | bytes 2457604
  339.5 15.1 %copy-start.5 = (bf16[1,2,144,1024]{3,2,1,0:T(8,128)(2,1)S(1)}, bf16[1,2,144,1024]{3,2,1,0:T(8,128)(2,1)}, u32[]{:S(2)}) copy-start(bf16[1,2,144,1024]{3,2,1,0:T(8,128)(2,1)} %get-tuple-element.38.refs_2_) | copy-start | bytes 1769476
  354.7 19.1 %copy-start.4 = (bf16[4,56,1024]{2,1,0:T(8,128)(2,1)S(1)}, bf16[4,56,1024]{2,1,0:T(8,128)(2,1)}, u32[]{:S(2)}) copy-start(bf16[4,56,1024]{2,1,0:T(8,128)(2,1)} %get-tuple-element.39.refs_2_) | copy-start | bytes 1376260

commit v5 on v4

--- a/solution.py
+++ b/solution.py
@@ -57,14 +57,16 @@
     return chunks, kinds, used, stages, count
 
 
-def exchange(chunks, kinds, stages, segments, *refs):
+def exchange(chunks, kinds, used, stages, *refs):
     it = iter(refs)
     take = lambda n: [next(it) for _ in range(n)]
     g, w, m, v = take(3), take(3), take(3), take(3)
-    out, new_m, new_v, onward = take(3), take(3), take(3), take(len(stages))
+    out, new_m, new_v = take(3), take(3), take(3)
+    to_go_right, to_go_left, *onward = take(len(stages) + 1)
+    onward = [None, *onward]
     nk = len(kinds)
     peer, pass_in, near_in, own, w_in, m_in, v_in = (take(nk) for _ in range(7))
-    (first_in, first_sem, x_send, x_recv, a_send, a_recv, b_send, b_recv, own_sem, in_sem, out_sem, kept_sem, g_send, g_recv,
+    (first_in, lead_sem, first_sem, lead_send, x_send, x_recv, a_send, a_recv, b_send, b_recv, own_sem, in_sem, out_sem, kept_sem, g_send, g_recv,
      gx_send, gx_recv) = it
     n = len(chunks)
 
@@ -181,11 +183,23 @@
             if c is first:
                 await_bytes(first_piece(h, start, stop), x_recv.at[3 * n + k])
             add(c, h, mine, theirs, rows=(start, stop))
+            if c is first and k == 0:
+
+                @pl.when(core == 1)
+                def _():
+                    pl.semaphore_wait(lead_sem, 1)
+
             remote(
                 theirs.at[h, pl.ds(start, stop - start)], pass_in[c.kind].at[c.place, h, pl.ds(start, stop - start)],
-                a_send.at[c.kind], a_recv.at[c.number], (right, left)[h])
+                lead_send.at[0] if c is first else a_send.at[c.kind], a_recv.at[c.number], (right, left)[h])
         swap(RIGHT, c)
         swap(LEFT, c)
+        if c.number == 1:
+
+            @pl.when(core == 0)
+            def _():
+                await_bytes(pass_in[first.kind].at[first.place], lead_send.at[0])
+                pl.semaphore_signal(lead_sem, inc=1, device_id={"dp": other}, device_id_type=MESH)
 
     for c in chunks:
         for r, to, side in ((RIGHT, right, 0), (LEFT, left, 1)):
@@ -224,10 +238,19 @@
             tiles(c, 0, c.rows, tile)
         for number, stage, index, start, size in c.segments:
             rows = pl.ds(start, size)
-            for k, (h, to) in enumerate(((core, ahead), (1 - core, ahead), (1 - core, behind), (core, behind))):
-                dst = onward[stage].at[index, core] if k == 0 else out[c.which].at[c.layer, me * 2 + h, rows]
-                if number == segments - 1:
-                    dst = onward[stage].at[k]
+            here = lambda h: out[c.which].at[c.layer, me * 2 + h, rows]
+            if stage == 0:
+                sends = (
+                    (0, right, to_go_right.at[index]), (1, right, here(1)), (1, left, to_go_left.at[index]), (0, left, here(0)))
+            elif c is chunks[-1]:
+                e = onward[stage]
+                sends = (
+                    (core, ahead, e.at[0]), (1 - core, ahead, e.at[1]), (1 - core, behind, e.at[2]), (core, behind, e.at[3]))
+            else:
+                sends = (
+                    (core, ahead, onward[stage].at[index, core]), (1 - core, ahead, here(1 - core)),
+                    (1 - core, behind, here(1 - core)), (core, behind, here(core)))
+            for h, to, dst in sends:
                 remote(theirs.at[h, rows], dst, g_send.at[c.kind], g_recv.at[number], to)
         target = out[c.which].at[c.layer, pl.ds(me * 2, 2)]
         remote(theirs, target, gx_send.at[c.kind], gx_recv.at[c.kind], other)
@@ -243,35 +266,45 @@
                     storing.remove(before)
             load_state(following)
 
-    several = {}
+    full = [sum(c.kind == kind for c in chunks[:-1]) for kind in range(nk)]
     for c in chunks:
         for number, stage, index, start, size in c.segments:
             rows = pl.ds(start, size)
             await_bytes(near_in[c.kind].at[:, c.place, :, rows], g_recv.at[number])
-            if number == segments - 1:
+            if c is chunks[-1]:
                 continue
-            sem = nk + (c.kind if size == c.rows else nk)
-            several.setdefault(sem, []).append((c, rows))
-            for k, (h, owner) in enumerate(
-                ((core, behind_chip), (1 - core, behind_chip), (1 - core, ahead_chip), (core, ahead_chip))):
-                there = out[c.which].at[c.layer, (owner * 2 + core) * 2 + h, rows]
-                remote(
-                    onward[stage].at[index, core] if k == 0 else there,
-                    onward[stage].at[index, core] if k == 2 else there, gx_send.at[sem], gx_recv.at[sem], other)
+            there = lambda owner, h: out[c.which].at[c.layer, (owner * 2 + core) * 2 + h]
+            if stage == 0:
+                moves = (
+                    (to_go_right.at[index], there(chip_at[LEFT], 0)), (there(chip_at[LEFT], 1),) * 2,
+                    (to_go_left.at[index], there(chip_at[RIGHT], 1)), (there(chip_at[RIGHT], 0),) * 2)
+            else:
+                mine = onward[stage].at[index, core]
+                moves = (
+                    (mine, there(behind_chip, core)), (there(behind_chip, 1 - core),) * 2,
+                    (there(ahead_chip, 1 - core), mine), (there(ahead_chip, core),) * 2)
+            for src, dst in moves:
+                remote(src, dst, gx_send.at[nk + c.kind], gx_recv.at[nk + c.kind], other)
     for c in storing:
         await_moments(c)
     for kind in range(nk):
         await_bytes(peer[kind], x_send.at[kind])
-        await_bytes(peer[kind].at[0], a_send.at[kind])
+        if kind == first.kind:
+            await_bytes(pass_in[kind].at[pl.ds(1, used[kind] - 1)], a_send.at[kind])
+        else:
+            await_bytes(pass_in[kind], a_send.at[kind])
         await_bytes(peer[kind].at[pl.ds(1, 2)], b_send.at[kind])
         await_bytes(peer[kind].at[pl.ds(0, 2)], g_send.at[kind])
         await_bytes(peer[kind].at[0], gx_send.at[kind])
         await_bytes(peer[kind].at[0], gx_recv.at[kind])
         await_bytes(peer[kind].at[0], kept_sem.at[kind])
-    for sem, parts in several.items():
-        c, rows = parts[0]
-        for sems in (gx_send, gx_recv):
-            await_bytes(near_in[c.kind].at[:, pl.ds(0, len(parts)), :, rows], sems.at[sem])
+        if full[kind]:
+            await_bytes(near_in[kind].at[:, pl.ds(0, full[kind])], gx_send.at[nk + kind])
+            await_bytes(near_in[kind].at[:, pl.ds(0, full[kind])], gx_recv.at[nk + kind])
+
+    @pl.when(core == 1)
+    def _():
+        await_bytes(pass_in[first.kind].at[first.place], lead_send.at[0])
 
 
 def gather_step(chunks, kinds, used, stages, segments, terms, weights, m, v):
@@ -282,19 +315,21 @@
     dma = lambda count: pltpu.SemaphoreType.DMA((count,))
     results = [jax.ShapeDtypeStruct(w.shape, BF16) for w in weights]
     results += [jax.ShapeDtypeStruct(a.shape, F32) for a in (*m, *v)]
-    results += [jax.ShapeDtypeStruct((len(s), 2, s[0][2], s[0][0].cols), BF16) for s in stages[:-1]]
-    results += [jax.ShapeDtypeStruct((4, s[0][2], s[0][0].cols), BF16) for s in stages[-1:]]
+    results += [jax.ShapeDtypeStruct((len(stages[0]), *kinds[stages[0][0][0].kind]), BF16)] * 2
+    for s in stages[1:]:
+        lead = (4,) if s[0][0] is chunks[-1] else (len(s), 2)
+        results.append(jax.ShapeDtypeStruct((*lead, s[0][2], s[0][0].cols), BF16))
     return pl.pallas_call(
-        functools.partial(exchange, chunks, kinds, stages, segments),
+        functools.partial(exchange, chunks, kinds, used, stages),
         out_shape=results,
         in_specs=[hbm] * 12,
         out_specs=[hbm] * len(results),
         scratch_shapes=[
             *slots((4, None), BF16), *slots((None,), BF16), *slots((2, None), BF16), *slots((3,), BF16),
             *slots((2,), BF16), *slots((2,), F32), *slots((2,), F32),
-            pltpu.VMEM((2, FIRST_ROWS, chunks[0].cols), BF16), dma(1),
+            pltpu.VMEM((2, FIRST_ROWS, chunks[0].cols), BF16), pltpu.SemaphoreType.REGULAR, dma(1), dma(1),
             dma(nk), dma(3 * n + 4), dma(nk), dma(n), dma(nk), dma(n), dma(3 * nk), dma(4 * nk), dma(2 * nk), dma(nk),
-            dma(nk), dma(segments), dma(2 * nk + 1), dma(2 * nk + 1),
+            dma(nk), dma(segments), dma(2 * nk), dma(2 * nk),
         ],
         compiler_params=pltpu.CompilerParams(collective_id=0, has_side_effects=True, vmem_limit_bytes=VMEM_LIMIT),
     )(*terms, *weights, *m, *v)
@@ -316,14 +351,17 @@
     for u in moves:
         place.append((u.kind, seen[u.kind] % depth[u.kind]))
         seen[u.kind] += 1
+    sem = {slot: k for k, slot in enumerate(sorted(set(place)))}
 
     def load(i):
         u, (kind, slot) = moves[i], place[i]
-        return pltpu.make_async_copy(sources[u.source].at[u.source_at(chip, core)], bufs[kind].at[slot], in_sem.at[i])
+        return pltpu.make_async_copy(
+            sources[u.source].at[u.source_at(chip, core)], bufs[kind].at[slot], in_sem.at[sem[place[i]]])
 
     def store(i):
         u, (kind, slot) = moves[i], place[i]
-        return pltpu.make_async_copy(bufs[kind].at[slot], targets[u.target].at[u.target_at(chip, core)], out_sem.at[i])
+        return pltpu.make_async_copy(
+            bufs[kind].at[slot], targets[u.target].at[u.target_at(chip, core)], out_sem.at[sem[place[i]]])
 
     waited, last = set(), {}
 
@@ -356,7 +394,7 @@
             counts.append(0)
         u.kind = kinds.index(kind)
         counts[u.kind] += 1
-    depth = [min(14, c) for c in counts]
+    depth = [min(12, c) for c in counts]
     size = lambda shape: functools.reduce(lambda a, b: a * b, shape)
     nbytes = 2 * sum(size(shape) * dtype.itemsize * c for (shape, dtype), c in zip(kinds, counts))
     hbm = pl.BlockSpec(memory_space=pltpu.HBM)
@@ -366,8 +404,8 @@
         in_specs=[hbm] * len(sources),
         out_specs=[hbm] * len(targets),
         scratch_shapes=[pltpu.VMEM((d, *shape), dtype) for d, (shape, dtype) in zip(depth, kinds)]
-        + [pltpu.SemaphoreType.DMA((len(moves),)), pltpu.SemaphoreType.DMA((len(moves),))],
-        compiler_params=pltpu.CompilerParams(vmem_limit_bytes=48 * 2**20),
+        + [pltpu.SemaphoreType.DMA((sum(depth),)), pltpu.SemaphoreType.DMA((sum(depth),))],
+        compiler_params=pltpu.CompilerParams(vmem_limit_bytes=56 * 2**20),
         cost_estimate=pl.CostEstimate(flops=2 * nbytes, bytes_accessed=nbytes, transcendentals=0),
     )(*sources)
 
@@ -403,33 +441,44 @@
 
 
 def known_moves(chunks, which, source, onward, target):
-    def block(c, r, parity, size):
-        def at(chip, core):
-            owner = lax.rem(chip + (0 if r == OWN else 1 + 2 * core), CHIPS) * 2 + parity
-            return c.layer, pl.ds(owner * 2, 2), pl.ds(0, size)
-
-        return at
-
-    def behind(c, parity, passed, start, size):
-        def at(chip, core):
-            owner = lax.rem(chip + 3 - 2 * core, CHIPS) * 2 + parity
-            return c.layer, owner * 2 + (core if passed else 1 - core), pl.ds(start, size)
-
-        return at
-
-    moves = []
+    def blocks(c, steps, block):
+        return lambda chip, core: (c.layer, pl.ds((lax.rem(chip + steps * (1 + 2 * core), CHIPS) * 2 + block(core)) * 2, 2))
+
+    def behind(c, parity, h):
+        return lambda chip, core: (c.layer, (lax.rem(chip + 3 - 2 * core, CHIPS) * 2 + parity) * 2 + h(core))
+
+    def beside(c, r, h):
+        return lambda chip, core: (c.layer, (lax.rem(chip + OFFSET[r], CHIPS) * 2 + core) * 2 + h)
+
+    def at(*index):
+        return lambda chip, core: index
+
+    def add(source, source_at, place, shape):
+        moves.append(Move(source, source_at, target, place, shape))
+
+    mine, its, moves = (lambda core: core), (lambda core: 1 - core), []
     for c in (c for c in chunks if c.which == which):
-        segments = [segment for segment in c.segments if onward[segment[1]] is not None]
-        known = sum(segment[-1] for segment in segments)
-        for parity in (0, 1):
-            for r, size in ((OWN, c.rows), (RIGHT, known)):
-                at = block(c, r, parity, size)
-                moves.append(Move(source, at, target, at, (2, size, c.cols)))
-            at = behind(c, parity, False, 0, known)
-            moves.append(Move(source, at, target, at, (known, c.cols)))
-            for _, stage, index, start, size in segments:
-                at = lambda chip, core, index=index, parity=parity: (index, parity)
-                moves.append(Move(onward[stage], at, target, behind(c, parity, True, start, size), (size, c.cols)))
+        block, piece = (2, c.rows, c.cols), (c.rows, c.cols)
+        for place in (blocks(c, 0, mine), blocks(c, 0, its)):
+            add(source, place, place, block)
+        if c is chunks[-1]:
+            continue
+        ((_, stage, index, _, _),) = c.segments
+        if stage == 0:
+            for steps in (1, 3):
+                place = blocks(c, steps, its)
+                add(source, place, place, block)
+            for passed, r in enumerate((LEFT, RIGHT)):
+                add(onward[0][passed], at(index), beside(c, r, passed), piece)
+                place = beside(c, r, 1 - passed)
+                add(source, place, place, piece)
+        else:
+            for parity in (0, 1):
+                place = blocks(c, 1, lambda core, parity=parity: parity)
+                add(source, place, place, block)
+                place = behind(c, parity, its)
+                add(source, place, place, piece)
+                add(onward[stage], at(index, parity), behind(c, parity, mine), piece)
     return moves
 
 
@@ -443,6 +492,18 @@
                 return c.layer, owner * 2 + (there if i in (0, 3) else 1 - there), pl.ds(start, size)
 
             moves.append(Move(source, lambda chip, core, i=i: (i,), target, to, (size, c.cols)))
+    return moves
+
+
+def first_moves(stage, sources, target):
+    moves = []
+    for index, (c, _, _) in enumerate(stage):
+        for k, source in enumerate(sources):
+            def to(chip, core, c=c, k=k):
+                owner = lax.rem(chip + 2, CHIPS) * 2 + (core if k < 2 else 1 - core)
+                return c.layer, owner * 2 + k % 2
+
+            moves.append(Move(source, lambda chip, core, index=index: (index,), target, to, (c.rows, c.cols)))
     return moves
 
 
@@ -466,6 +527,8 @@
     assert devices == 2 * CHIPS
     onward_to = [(d, (d + 2 - 4 * (d % 2)) % devices) for d in range(devices)]
     across = [(d, d ^ 1) for d in range(devices)]
+    to_right = [(d, (d + 2) % devices) for d in range(devices)]
+    to_left = [(d, (d - 2) % devices) for d in range(devices)]
 
     def halves(a, count):
         return a.reshape(a.shape[0], count, a.shape[1] // count, a.shape[2])
@@ -477,38 +540,48 @@
         m, v = ([halves(a, 2) for a in arrays[i : i + 3]] for i in (6, 9))
         chunks, kinds, used, stages, segments = plan([w.shape for w in weights])
         results = gather_step(chunks, kinds, used, stages, segments, terms, weights, m, v)
-        gathered, moments, onward = results[:3], results[3:9], list(results[9:])
-
-        late = onward[-1], lax.ppermute(onward[-1], "dp", across)
-        onward[-1] = jnp.stack([late[0][0], late[1][2]])[None]
-        passed, crossed = [], []
-        for s, piece in enumerate(onward):
-            passed.append(lax.ppermute(piece, "dp", onward_to))
-            crossed.append(lax.ppermute(passed[s], "dp", across))
+        gathered, moments, first_stage, onward = results[:3], results[3:9], results[9:11], list(results[11:])
+        late = range(len(stages) - len(chunks[-1].segments), len(stages))
+
+        passed, crossed = {}, {}
+
+        def hop(s, piece, to):
+            passed.setdefault(s, []).append(lax.ppermute(piece, "dp", to))
+            crossed.setdefault(s, []).append(lax.ppermute(passed[s][-1], "dp", across))
+
+        hop(0, first_stage[0], to_right)
+        hop(0, first_stage[1], to_left)
+        onward = dict(enumerate(onward, 1))
+        for s in range(1, late.start):
+            hop(s, onward[s], onward_to)
+        after = {s: lax.ppermute(onward[s], "dp", across) for s in late}
+        for s in late:
+            hop(s, jnp.stack([onward[s][0], after[s][2]])[None], onward_to)
 
         whole = [None] * 3
-        sources = [*gathered[:2], *onward[:2]]
-        moves = [u for i in (0, 1) for u in known_moves(chunks, i, i, [2, 3], i)]
+        sources = [*gathered[:2], *first_stage, onward[1]]
+        moves = [u for i in (0, 1) for u in known_moves(chunks, i, i, [(2, 3), 4], i)]
         whole[:2] = move(moves, sources, gathered[:2])
-        sources = [gathered[2], *onward[2:-1], *moments]
-        first = len(sources) - len(moments)
-        moves = known_moves(chunks, 2, 0, [None, None, *range(1, first), None], 0)
+        sources = [gathered[2], onward[2], *moments]
+        moves = known_moves(chunks, 2, 0, [None, None, 1], 0)
         for a, array in enumerate(moments):
             for layer in range(array.shape[0]):
                 for h in (0, 1):
                     at = lambda chip, core, layer=layer, h=h: (layer, h)
-                    moves.append(Move(first + a, at, 1 + a, at, array.shape[2:]))
+                    moves.append(Move(2 + a, at, 1 + a, at, array.shape[2:]))
         whole[2], *moments = move(moves, sources, [gathered[2], *moments])
 
-        for place, group in enumerate(([0], [1], [2], range(3, len(stages)))):
+        whole[0] = put(first_moves(stages[0], range(4), 0), [*passed[0], *crossed[0]], whole[0])
+        for place, group in enumerate(([1], [2], late), 1):
             which = stages[group[0]][0][0].which
             sources, moves = [], []
             for s in group:
-                moves += last_moves(stages[s], (len(sources), len(sources) + 1), 0, joined=s == len(stages) - 1)
-                sources += [passed[s], crossed[s]]
+                moves += last_moves(stages[s], (len(sources), len(sources) + 1), 0, joined=s in late)
+                sources += [*passed[s], *crossed[s]]
             if place == 2:
-                moves += late_moves(stages[-1], (2, 3), 0)
-                sources += late
+                for s in late:
+                    moves += late_moves(stages[s], (len(sources), len(sources) + 1), 0)
+                    sources += [onward[s], after[s]]
             whole[which] = put(moves, sources, whole[which])
         return tuple(a.reshape(s) for a, s in zip((*whole, *moments), shapes[3:]))
 

time: 382 us -> 375 us (0.982)
    ppermute x11 -> x14, starting transfers between devices: 15.2 us -> 11.5 us  [the longest x6 9.91 us: hop(): passed.setdefault(s, []).append(lax.ppermute(piece, 'dp', to))]
    ppermute x11 -> x14, waiting for transfers between devices: 48.1 us -> 45.7 us  [the longest x6 45.2 us: hop(): passed.setdefault(s, []).append(lax.ppermute(piece, 'dp', to))]
  transfers between devices with their start and end apart: 11 -> 14, of which waited for: 5 -> 4; matrix products, arithmetic and copies ran while one was open for 0% -> 1% of each run, Pallas kernels for 11% -> 11%
where the time goes in v5:
time: 375 us
  Pallas kernels  314 us (84%)
  waiting for transfers between devices  45.7 us (12%)
  starting transfers between devices  11.5 us (3%)
    pallas_call x1, Pallas kernels, gather_step(): pl.pallas_call(functools.partial(exchange, chunks, kinds, used, stages),...  272 us
    ppermute x6, waiting for transfers between devices, hop(): passed.setdefault(s, []).append(lax.ppermute(piece, 'dp', to))  45.2 us
    pallas_call x2, Pallas kernels, move(): pl.pallas_call(functools.partial(move_body, moves, kinds, depth, len(sour...  32.3 us
    pallas_call x4, Pallas kernels, put(): pl.pallas_call(functools.partial(put_body, moves, len(sources) + 1), out_...  9.93 us
    ppermute x6, starting transfers between devices, hop(): passed.setdefault(s, []).append(lax.ppermute(piece, 'dp', to))  9.91 us
  transfers between devices with their start and end apart: 14, of which 4 were waited for; matrix products, arithmetic and copies ran while one was open for 1% of the time, Pallas kernels for 11%

profile of v5, /device:TPU:113, one launch (start us, length us, event | category | flops | bytes accessed | tf_op | source)
XLA Modules:
  0.0 374.6 jit_solution(9844919164590298607)
XLA Ops:
  0.6 271.7 %shard_map.187 = (bf16[2,16,64,3200]{3,2,1,0:T(8,128)(2,1)}, bf16[2,16,64,3200]{3,2,1,0:T(8,128)(2,1)}, bf16[2,16,200,1024]{3,2,1,0:T(8,128)(2,1)}, f32[2,2,64,3...) custom-call(bf16[2,16,64,3200]{3,2,1,0:T(8,128)(2,1)} %bitcast.26, ...), custom_call_target="tpu_custom_call" | custom-call | tf_op jit(solution)/shard_map/pallas_call | solution.py:322
  272.3 1.7 collective-permute-start.4
  274.0 0.0 collective-permute-start.6
  274.0 0.5 collective-permute-start.9
  274.5 0.0 collective-permute-start
  274.5 2.7 collective-permute-start.1
  277.2 0.5 collective-permute-done.9.refs_5_
  277.7 0.2 collective-permute-start.12
  277.9 23.7 %collective-permute-done.4.refs_0_ = bf16[2,2,64,3200]{3,2,1,0:T(8,128)(2,1)S(1)} collective-permute-done((bf16[2,2,64,3200]{3,2,1,0:T(8,128)(2,1)}, bf16[2,2,64,3200]{3,2,1,0:T(8,128)(2,1)S(1)}, u32[]{:S(2)}, u32[]{:S(2)}) %collective-permute-start.4) | collective-permute-done | bytes 1638432 | tf_op jit(solution)/shard_map/ppermute | solution.py:549
  301.7 0.0 collective-permute-start.5
  301.7 0.9 slice.14
  302.6 0.0 collective-permute-done.6.refs_3_
  302.6 2.6 collective-permute-start.10
  305.2 1.0 slice.12
  306.2 0.1 maximum_bitcast_fusion
  306.3 15.2 %collective-permute-done.10.refs_2_ = bf16[1,2,56,1024]{3,2,1,0:T(8,128)(2,1)} collective-permute-done((bf16[1,2,56,1024]{3,2,1,0:T(8,128)(2,1)S(1)}, bf16[1,2,56,1024]{3,2,1,0:T(8,128)(2,1)}, u32[]{:S(2)}, u32[]{:S(2)}) %collective-permute-start.10) | collective-permute-done | bytes 229408 | tf_op jit(solution)/shard_map/ppermute | solution.py:549
  321.5 2.8 collective-permute-start.7
  324.3 0.0 collective-permute-done.refs_0_
  324.3 0.0 collective-permute-start.2
  324.3 0.0 collective-permute-done.1.refs_1_
  324.3 0.5 collective-permute-start.3
  324.8 0.0 collective-permute-done.12.refs_0_
  324.8 0.1 collective-permute-start.13
  324.9 6.2 %collective-permute-done.7.refs_0_ = bf16[1,2,144,1024]{3,2,1,0:T(8,128)(2,1)} collective-permute-done((bf16[1,2,144,1024]{3,2,1,0:T(8,128)(2,1)S(1)}, bf16[1,2,144,1024]{3,2,1,0:T(8,128)(2,1)}, u32[]{:S(2)}, u32[]{:S(2)}) %collective-permute-start.7) | collective-permute-done | bytes 589856 | tf_op jit(solution)/shard_map/ppermute | solution.py:549
  331.1 0.0 collective-permute-start.8
  331.1 0.0 collective-permute-done.2.refs_2_
  331.1 0.5 collective-permute-start.11
  331.6 14.0 %shard_map.188 = (bf16[2,16,64,3200]{3,2,1,0:T(8,128)(2,1)}, bf16[2,16,64,3200]{3,2,1,0:T(8,128)(2,1)}) custom-call(bf16[2,16,64,3200]{3,2,1,0:T(8,128)(2,1)} %get-tuple-element.35.refs_0_, bf16[2,16,64,3200]{3,2,1,0:T(8,128)(2,1)} %get-tuple-element.36.refs_1_, bf16[2,64,3200]{2,1,0:T(8,128)(2,1)} %get-tuple-element.33.refs_2_, ...), custom_call_target="tpu_custom_call" | custom-call | flops 78643200 | bytes 39321600 | tf_op jit(solution)/shard_map/pallas_call | solution.py:401
  345.7 18.3 %shard_map.191 = (bf16[2,16,200,1024]{3,2,1,0:T(8,128)(2,1)}, f32[2,2,64,3200]{3,2,1,0:T(8,128)}, f32[2,2,64,3200]{3,2,1,0:T(8,128)}, f32[2,2,200,1024]{3,2,1,0:...) custom-call(bf16[2,16,200,1024]{3,2,1,0:T(8,128)(2,1)} %get-tuple-element.43.refs_0_, ...), custom_call_target="tpu_custom_call" | custom-call | flops 104857600 | bytes 52428800 | tf_op jit(solution)/shard_map/pallas_call | solution.py:401
  363.9 0.0 collective-permute-done.3.refs_3_
  363.9 0.0 copy-start
  363.9 0.0 copy-start.1
  364.0 1.8 shard_map.189
  365.8 0.0 collective-permute-done.13.refs_1_
  365.8 0.2 copy-done
  365.9 0.5 copy-done.1
  366.4 3.8 %shard_map.192.refs_4_ = bf16[2,16,200,1024]{3,2,1,0:T(8,128)(2,1)} custom-call(bf16[1,2,200,1024]{3,2,1,0:T(8,128)(2,1)} %collective-permute-done.12.refs_0_, bf16[1,2,200,1024]{3,2,1,0:T(8,128)(2,1)} %collective-permute-done.13.refs_1_, bf16[4,144,1024]{2,1,0:T(8,128)(2,1)S(1)} %copy-done, ...), custom_call_target="tpu_custom_call", output_to_operand_aliasing={{}: (6, {})} | custom-call | flops 19660800 | bytes 9830400 | tf_op jit(solution)/shard_map/pallas_call | solution.py:431
  370.2 0.0 collective-permute-done.11.refs_3_
  370.2 0.0 collective-permute-done.8.refs_1_
  370.2 2.6 shard_map.193
  372.8 0.0 collective-permute-done.5.refs_1_
  372.8 1.8 shard_map.190
  (3 shorter events, 0.1 us)
Async XLA Ops:
  272.3 29.3 %collective-permute-start.4 = (bf16[2,2,64,3200]{3,2,1,0:T(8,128)(2,1)}, bf16[2,2,64,3200]{3,2,1,0:T(8,128)(2,1)S(1)}, u32[]{:S(2)}, u32[]{:S(2)}) collective-permute-start(bf16[2,2,64,3200]{3,2,1,0:T(8,128)(2,1)} %get-tuple-element.37.refs_4_), channel_id=1, source_target_pairs={{0,2},{1,7},{2,4},{3,1},{4,6},{5,3},{6,0},{7,5},{8,10},{9,15},{10,... | collective-permute-start | bytes 4915208 | tf_op jit(solution)/shard_map/ppermute | solution.py:549
  274.0 28.6 %collective-permute-start.6 = (bf16[4,144,1024]{2,1,0:T(8,128)(2,1)}, bf16[4,144,1024]{2,1,0:T(8,128)(2,1)S(1)}, u32[]{:S(2)}, u32[]{:S(2)}) collective-permute-start(bf16[4,144,1024]{2,1,0:T(8,128)(2,1)} %get-tuple-element.40.refs_2_), channel_id=1, source_target_pairs={{0,1},{1,0},{2,3},{3,2},{4,5},{5,4},{6,7},{7,6},{8,9},{9,8},{10,11... | collective-permute-start | bytes 3538952 | tf_op jit(solution)/shard_map/ppermute | solution.py:557
  274.0 3.7 collective-permute-start.9
  274.5 49.8 %collective-permute-start = (bf16[2,64,3200]{2,1,0:T(8,128)(2,1)}, bf16[2,64,3200]{2,1,0:T(8,128)(2,1)S(1)}, u32[]{:S(2)}, u32[]{:S(2)}) collective-permute-start(bf16[2,64,3200]{2,1,0:T(8,128)(2,1)} %get-tuple-element.33.refs_2_), channel_id=1, source_target_pairs={{0,2},{1,3},{2,4},{3,5},{4,6},{5,7},{6,0},{7,1},{8,10},{9,11},{10,... | collective-permute-start | bytes 2457608 | tf_op jit(solution)/shard_map/ppermute | solution.py:549
  274.5 49.8 %collective-permute-start.1 = (bf16[2,64,3200]{2,1,0:T(8,128)(2,1)}, bf16[2,64,3200]{2,1,0:T(8,128)(2,1)S(1)}, u32[]{:S(2)}, u32[]{:S(2)}) collective-permute-start(bf16[2,64,3200]{2,1,0:T(8,128)(2,1)} %get-tuple-element.34.refs_3_), channel_id=1, source_target_pairs={{0,6},{1,7},{2,0},{3,1},{4,2},{5,3},{6,4},{7,5},{8,14},{9,15},{10,... | collective-permute-start | bytes 2457608 | tf_op jit(solution)/shard_map/ppermute | solution.py:549
  277.7 47.1 %collective-permute-start.12 = (bf16[1,2,200,1024]{3,2,1,0:T(8,128)(2,1)}, bf16[1,2,200,1024]{3,2,1,0:T(8,128)(2,1)}, u32[]{:S(2)}, u32[]{:S(2)}) collective-permute-start(bf16[1,2,200,1024]{3,2,1,0:T(8,128)(2,1)} %get-tuple-element.42.refs_1_), channel_id=1, source_target_pairs={{0,2},{1,7},{2,4},{3,1},{4,6},{5,3},{6,0},{7,5},{8,10},{9,15},{10,... | collective-permute-start | bytes 2457608 | tf_op jit(solution)/shard_map/ppermute | solution.py:549
  301.7 71.1 %collective-permute-start.5 = (bf16[2,2,64,3200]{3,2,1,0:T(8,128)(2,1)S(1)}, bf16[2,2,64,3200]{3,2,1,0:T(8,128)(2,1)S(1)}, u32[]{:S(2)}, u32[]{:S(2)}) collective-permute-start(bf16[2,2,64,3200]{3,2,1,0:T(8,128)(2,1)S(1)} %collective-permute-done.4.refs_0_), channel_id=1, source_target_pairs={{0,1},{1,0},{2,3},{3,2},{4,5},{5,4},{6,7},{7,6},{8,9},{9,8},{10,11... | collective-permute-start | bytes 4915208 | tf_op jit(solution)/shard_map/ppermute | solution.py:550
  302.6 18.9 %collective-permute-start.10 = (bf16[1,2,56,1024]{3,2,1,0:T(8,128)(2,1)S(1)}, bf16[1,2,56,1024]{3,2,1,0:T(8,128)(2,1)}, u32[]{:S(2)}, u32[]{:S(2)}) collective-permute-start(bf16[1,2,56,1024]{3,2,1,0:T(8,128)(2,1)S(1)} %maximum_bitcast_fusion.1), channel_id=1, source_target_pairs={{0,2},{1,7},{2,4},{3,1},{4,6},{5,3},{6,0},{7,5},{8,10},{9,15},{10,... | collective-permute-start | bytes 688136 | tf_op jit(solution)/shard_map/ppermute | solution.py:549
  321.5 9.6 %collective-permute-start.7 = (bf16[1,2,144,1024]{3,2,1,0:T(8,128)(2,1)S(1)}, bf16[1,2,144,1024]{3,2,1,0:T(8,128)(2,1)}, u32[]{:S(2)}, u32[]{:S(2)}) collective-permute-start(bf16[1,2,144,1024]{3,2,1,0:T(8,128)(2,1)S(1)} %maximum_bitcast_fusion), channel_id=1, source_target_pairs={{0,2},{1,7},{2,4},{3,1},{4,6},{5,3},{6,0},{7,5},{8,10},{9,15},{10,... | collective-permute-start | bytes 1769480 | tf_op jit(solution)/shard_map/ppermute | solution.py:549
  324.3 6.8 %collective-permute-start.2 = (bf16[2,64,3200]{2,1,0:T(8,128)(2,1)S(1)}, bf16[2,64,3200]{2,1,0:T(8,128)(2,1)S(1)}, u32[]{:S(2)}, u32[]{:S(2)}) collective-permute-start(bf16[2,64,3200]{2,1,0:T(8,128)(2,1)S(1)} %collective-permute-done.refs_0_), channel_id=1, source_target_pairs={{0,1},{1,0},{2,3},{3,2},{4,5},{5,4},{6,7},{7,6},{8,9},{9,8},{10,11... | collective-permute-start | bytes 2457608 | tf_op jit(solution)/shard_map/ppermute | solution.py:550
  324.3 39.6 %collective-permute-start.3 = (bf16[2,64,3200]{2,1,0:T(8,128)(2,1)S(1)}, bf16[2,64,3200]{2,1,0:T(8,128)(2,1)S(1)}, u32[]{:S(2)}, u32[]{:S(2)}) collective-permute-start(bf16[2,64,3200]{2,1,0:T(8,128)(2,1)S(1)} %collective-permute-done.1.refs_1_), channel_id=1, source_target_pairs={{0,1},{1,0},{2,3},{3,2},{4,5},{5,4},{6,7},{7,6},{8,9},{9,8},{10,11... | collective-permute-start | bytes 2457608 | tf_op jit(solution)/shard_map/ppermute | solution.py:550
  324.8 41.0 %collective-permute-start.13 = (bf16[1,2,200,1024]{3,2,1,0:T(8,128)(2,1)}, bf16[1,2,200,1024]{3,2,1,0:T(8,128)(2,1)}, u32[]{:S(2)}, u32[]{:S(2)}) collective-permute-start(bf16[1,2,200,1024]{3,2,1,0:T(8,128)(2,1)} %collective-permute-done.12.refs_0_), channel_id=1, source_target_pairs={{0,1},{1,0},{2,3},{3,2},{4,5},{5,4},{6,7},{7,6},{8,9},{9,8},{10,11... | collective-permute-start | bytes 2457608 | tf_op jit(solution)/shard_map/ppermute | solution.py:550
  331.1 39.1 %collective-permute-start.8 = (bf16[1,2,144,1024]{3,2,1,0:T(8,128)(2,1)}, bf16[1,2,144,1024]{3,2,1,0:T(8,128)(2,1)}, u32[]{:S(2)}, u32[]{:S(2)}) collective-permute-start(bf16[1,2,144,1024]{3,2,1,0:T(8,128)(2,1)} %collective-permute-done.7.refs_0_), channel_id=1, source_target_pairs={{0,1},{1,0},{2,3},{3,2},{4,5},{5,4},{6,7},{7,6},{8,9},{9,8},{10,11... | collective-permute-start | bytes 1769480 | tf_op jit(solution)/shard_map/ppermute | solution.py:550
  331.1 39.1 %collective-permute-start.11 = (bf16[1,2,56,1024]{3,2,1,0:T(8,128)(2,1)}, bf16[1,2,56,1024]{3,2,1,0:T(8,128)(2,1)}, u32[]{:S(2)}, u32[]{:S(2)}) collective-permute-start(bf16[1,2,56,1024]{3,2,1,0:T(8,128)(2,1)} %collective-permute-done.10.refs_2_), channel_id=1, source_target_pairs={{0,1},{1,0},{2,3},{3,2},{4,5},{5,4},{6,7},{7,6},{8,9},{9,8},{10,11... | collective-permute-start | bytes 688136 | tf_op jit(solution)/shard_map/ppermute | solution.py:550
  363.9 2.0 copy-start
  363.9 2.5 copy-start.1

commit v6 on v5

--- a/solution.py
+++ b/solution.py
@@ -440,6 +440,10 @@
     )(*sources, into)
 
 
+def fixed(*index):
+    return lambda chip, core: index
+
+
 def known_moves(chunks, which, source, onward, target):
     def blocks(c, steps, block):
         return lambda chip, core: (c.layer, pl.ds((lax.rem(chip + steps * (1 + 2 * core), CHIPS) * 2 + block(core)) * 2, 2))
@@ -449,9 +453,6 @@
 
     def beside(c, r, h):
         return lambda chip, core: (c.layer, (lax.rem(chip + OFFSET[r], CHIPS) * 2 + core) * 2 + h)
-
-    def at(*index):
-        return lambda chip, core: index
 
     def add(source, source_at, place, shape):
         moves.append(Move(source, source_at, target, place, shape))
@@ -469,7 +470,7 @@
                 place = blocks(c, steps, its)
                 add(source, place, place, block)
             for passed, r in enumerate((LEFT, RIGHT)):
-                add(onward[0][passed], at(index), beside(c, r, passed), piece)
+                add(onward[0][passed], fixed(index), beside(c, r, passed), piece)
                 place = beside(c, r, 1 - passed)
                 add(source, place, place, piece)
         else:
@@ -478,7 +479,7 @@
                 add(source, place, place, block)
                 place = behind(c, parity, its)
                 add(source, place, place, piece)
-                add(onward[stage], at(index, parity), behind(c, parity, mine), piece)
+                add(onward[stage], fixed(index, parity), behind(c, parity, mine), piece)
     return moves
 
 
@@ -491,7 +492,7 @@
                 owner = lax.rem(chip + (3 - 2 * there if i < 2 else 1 + 2 * there), CHIPS) * 2 + there
                 return c.layer, owner * 2 + (there if i in (0, 3) else 1 - there), pl.ds(start, size)
 
-            moves.append(Move(source, lambda chip, core, i=i: (i,), target, to, (size, c.cols)))
+            moves.append(Move(source, fixed(i), target, to, (size, c.cols)))
     return moves
 
 
@@ -503,7 +504,7 @@
                 owner = lax.rem(chip + 2, CHIPS) * 2 + (core if k < 2 else 1 - core)
                 return c.layer, owner * 2 + k % 2
 
-            moves.append(Move(source, lambda chip, core, index=index: (index,), target, to, (c.rows, c.cols)))
+            moves.append(Move(source, fixed(index), target, to, (c.rows, c.cols)))
     return moves
 
 
@@ -517,8 +518,7 @@
                     owner = lax.rem(chip + 2, CHIPS) * 2 + ((half if parity == 0 else 1 - half) if joined else parity)
                     return c.layer, owner * 2 + half, pl.ds(start, size)
 
-                at = lambda chip, core, index=index, parity=parity: (index, parity)
-                moves.append(Move(source, at, target, to, (size, c.cols)))
+                moves.append(Move(source, fixed(index, parity), target, to, (size, c.cols)))
     return moves
 
 
@@ -555,20 +555,25 @@
         for s in range(1, late.start):
             hop(s, onward[s], onward_to)
         after = {s: lax.ppermute(onward[s], "dp", across) for s in late}
+        whole = [None] * 3
+        whole[:1] = move(known_moves(chunks, 0, 0, [(1, 2)], 0), [gathered[0], *first_stage], gathered[:1])
+        sources, targets = [gathered[1], onward[1]], [gathered[1]]
+        moves = known_moves(chunks, 1, 0, [None, 1], 0)
         for s in late:
-            hop(s, jnp.stack([onward[s][0], after[s][2]])[None], onward_to)
-
-        whole = [None] * 3
-        sources = [*gathered[:2], *first_stage, onward[1]]
-        moves = [u for i in (0, 1) for u in known_moves(chunks, i, i, [(2, 3), 4], i)]
-        whole[:2] = move(moves, sources, gathered[:2])
+            c, _, size = stages[s][0]
+            for k, (piece, i) in enumerate(((onward[s], 0), (after[s], 2))):
+                moves.append(Move(len(sources), fixed(i), len(targets), fixed(0, k), (size, c.cols)))
+                sources.append(piece)
+            targets.append(jax.ShapeDtypeStruct((1, 2, size, c.cols), BF16))
+        whole[1], *joined = move(moves, sources, targets)
+        for s, piece in zip(late, joined):
+            hop(s, piece, onward_to)
         sources = [gathered[2], onward[2], *moments]
         moves = known_moves(chunks, 2, 0, [None, None, 1], 0)
         for a, array in enumerate(moments):
             for layer in range(array.shape[0]):
                 for h in (0, 1):
-                    at = lambda chip, core, layer=layer, h=h: (layer, h)
-                    moves.append(Move(2 + a, at, 1 + a, at, array.shape[2:]))
+                    moves.append(Move(2 + a, fixed(layer, h), 1 + a, fixed(layer, h), array.shape[2:]))
         whole[2], *moments = move(moves, sources, [gathered[2], *moments])
 
         whole[0] = put(first_moves(stages[0], range(4), 0), [*passed[0], *crossed[0]], whole[0])

time: 375 us -> 364 us (0.971)
  waiting for transfers between devices: 45.7 us -> 36.8 us
    ppermute x6, waiting for transfers between devices: 45.2 us -> 35 us  [hop(): passed.setdefault(s, []).append(lax.ppermute(piece, 'dp', to))]
    ppermute x6, starting transfers between devices: 9.91 us -> 6.03 us  [hop(): passed.setdefault(s, []).append(lax.ppermute(piece, 'dp', to))]
    pallas_call x2 -> x3, Pallas kernels: 32.3 us -> 33.9 us  [move(): pl.pallas_call(functools.partial(move_body, moves, kinds, depth, len(sour...]
  transfers between devices with their start and end apart: 14 -> 14, of which waited for: 4 -> 4; matrix products, arithmetic and copies ran while one was open for 1% -> 0% of each run, Pallas kernels for 11% -> 11%
where the time goes in v6:
time: 364 us
  Pallas kernels  314 us (86%)
  waiting for transfers between devices  36.8 us (10%)
  starting transfers between devices  9.99 us (3%)
    pallas_call x1, Pallas kernels, gather_step(): pl.pallas_call(functools.partial(exchange, chunks, kinds, used, stages),...  272 us
    ppermute x6, waiting for transfers between devices, hop(): passed.setdefault(s, []).append(lax.ppermute(piece, 'dp', to))  35 us
    pallas_call x3, Pallas kernels, move(): pl.pallas_call(functools.partial(move_body, moves, kinds, depth, len(sour...  33.9 us
    pallas_call x4, Pallas kernels, put(): pl.pallas_call(functools.partial(put_body, moves, len(sources) + 1), out_...  8.54 us
  transfers between devices with their start and end apart: 14, of which 4 were waited for; matrix products, arithmetic and copies ran while one was open for 0% of the time, Pallas kernels for 11%

profile of v6, /device:TPU:113, one launch (start us, length us, event | category | flops | bytes accessed | tf_op | source)
XLA Modules:
  0.0 363.9 jit_solution(1194106739406550579)
XLA Ops:
  0.6 271.7 %shard_map.187 = (bf16[2,16,64,3200]{3,2,1,0:T(8,128)(2,1)}, bf16[2,16,64,3200]{3,2,1,0:T(8,128)(2,1)}, bf16[2,16,200,1024]{3,2,1,0:T(8,128)(2,1)}, f32[2,2,64,3...) custom-call(bf16[2,16,64,3200]{3,2,1,0:T(8,128)(2,1)} %bitcast.23, ...), custom_call_target="tpu_custom_call" | custom-call | tf_op jit(solution)/shard_map/pallas_call | solution.py:322
  272.3 1.7 collective-permute-start.4
  274.0 0.0 collective-permute-start.6
  274.0 0.5 collective-permute-start.7
  274.5 0.2 collective-permute-start.12
  274.7 1.2 collective-permute-start
  276.0 1.7 collective-permute-done.7.refs_5_
  277.7 0.0 copy-start.4
  277.7 0.2 collective-permute-start.1
  277.9 23.7 %collective-permute-done.4.refs_0_ = bf16[2,2,64,3200]{3,2,1,0:T(8,128)(2,1)S(1)} collective-permute-done((bf16[2,2,64,3200]{3,2,1,0:T(8,128)(2,1)}, bf16[2,2,64,3200]{3,2,1,0:T(8,128)(2,1)S(1)}, u32[]{:S(2)}, u32[]{:S(2)}) %collective-permute-start.4) | collective-permute-done | bytes 1638432 | tf_op jit(solution)/shard_map/ppermute | solution.py:549
  301.7 0.0 collective-permute-start.5
  301.7 0.0 collective-permute-done.6.refs_3_
  301.7 0.0 copy-start.1
  301.7 0.0 copy-done.4
  301.7 1.0 copy-done.1
  302.7 8.3 %shard_map.190 = (bf16[2,16,64,3200]{3,2,1,0:T(8,128)(2,1)}, bf16[1,2,144,1024]{3,2,1,0:T(8,128)(2,1)}, bf16[1,2,56,1024]{3,2,1,0:T(8,128)(2,1)}) custom-call(bf16[2,16,64,3200]{3,2,1,0:T(8,128)(2,1)} %get-tuple-element.38.refs_0_, bf16[2,2,64,3200]{3,2,1,0:T(8,128)(2,1)} %get-tuple-element.37.refs_1_, bf16[4,144,1024]{2,1,0:T(8,128)(2,1)} %get-tuple-element.39.refs_2_, ...), custom_call_target="tpu_custom_call" | custom-call | flops 42598400 | bytes 21299200 | tf_op jit(solution)/shard_map/pallas_call | solution.py:401
  311.0 2.6 collective-permute-start.8
  313.5 0.0 collective-permute-done.12.refs_0_
  313.6 0.1 collective-permute-start.10
  313.7 0.0 collective-permute-done.refs_0_
  313.7 2.9 collective-permute-start.2
  316.5 2.8 collective-permute-done.1.refs_1_
  319.3 0.0 collective-permute-start.3
  319.3 8.5 %collective-permute-done.10.refs_2_ = bf16[1,2,56,1024]{3,2,1,0:T(8,128)(2,1)} collective-permute-done((bf16[1,2,56,1024]{3,2,1,0:T(8,128)(2,1)}, bf16[1,2,56,1024]{3,2,1,0:T(8,128)(2,1)}, u32[]{:S(2)}, u32[]{:S(2)}) %collective-permute-start.10) | collective-permute-done | bytes 229408 | tf_op jit(solution)/shard_map/ppermute | solution.py:549
  327.8 0.0 collective-permute-start.13
  327.8 0.0 collective-permute-done.8.refs_0_
  327.8 0.5 collective-permute-start.9
  328.3 0.0 collective-permute-done.2.refs_2_
  328.3 0.1 collective-permute-start.11
  328.4 7.4 %shard_map.188.refs_4_ = bf16[2,16,64,3200]{3,2,1,0:T(8,128)(2,1)} custom-call(bf16[2,16,64,3200]{3,2,1,0:T(8,128)(2,1)} %get-tuple-element.36.refs_0_, bf16[2,64,3200]{2,1,0:T(8,128)(2,1)} %get-tuple-element.34.refs_1_, bf16[2,64,3200]{2,1,0:T(8,128)(2,1)} %get-tuple-element.35.refs_2_), custom_call_target="tpu_custom_call" | custom-call | flops 39321600 | bytes 19660800 | tf_op jit(solution)/shard_map/pallas_call | solution.py:401
  335.8 18.3 %shard_map.192 = (bf16[2,16,200,1024]{3,2,1,0:T(8,128)(2,1)}, f32[2,2,64,3200]{3,2,1,0:T(8,128)}, f32[2,2,64,3200]{3,2,1,0:T(8,128)}, f32[2,2,200,1024]{3,2,1,0:...) custom-call(bf16[2,16,200,1024]{3,2,1,0:T(8,128)(2,1)} %get-tuple-element.45.refs_0_, ...), custom_call_target="tpu_custom_call" | custom-call | flops 104857600 | bytes 52428800 | tf_op jit(solution)/shard_map/pallas_call | solution.py:401
  354.1 0.0 copy-start
  354.1 0.0 copy-start.2
  354.1 0.0 copy-start.3
  354.1 0.0 copy-start.5
  354.1 0.0 collective-permute-done.3.refs_3_
  354.1 1.8 shard_map.189
  355.9 0.0 collective-permute-done.13.refs_1_
  355.9 0.1 copy-done
  356.0 0.9 copy-done.2
  356.9 0.1 copy-done.3
  357.0 0.1 copy-done.5
  357.1 2.4 shard_map.193.refs_4_
  359.5 0.0 collective-permute-done.11.refs_3_
  359.5 0.0 collective-permute-done.9.refs_1_
  359.5 2.6 shard_map.194
  362.1 0.0 collective-permute-done.5.refs_1_
  362.1 1.8 shard_map.191
Async XLA Ops:
  272.3 29.3 %collective-permute-start.4 = (bf16[2,2,64,3200]{3,2,1,0:T(8,128)(2,1)}, bf16[2,2,64,3200]{3,2,1,0:T(8,128)(2,1)S(1)}, u32[]{:S(2)}, u32[]{:S(2)}) collective-permute-start(bf16[2,2,64,3200]{3,2,1,0:T(8,128)(2,1)} %get-tuple-element.37.refs_1_), channel_id=1, source_target_pairs={{0,2},{1,7},{2,4},{3,1},{4,6},{5,3},{6,0},{7,5},{8,10},{9,15},{10,... | collective-permute-start | bytes 4915208 | tf_op jit(solution)/shard_map/ppermute | solution.py:549
  274.0 27.7 %collective-permute-start.6 = (bf16[4,144,1024]{2,1,0:T(8,128)(2,1)}, bf16[4,144,1024]{2,1,0:T(8,128)(2,1)S(1)}, u32[]{:S(2)}, u32[]{:S(2)}) collective-permute-start(bf16[4,144,1024]{2,1,0:T(8,128)(2,1)} %get-tuple-element.39.refs_2_), channel_id=1, source_target_pairs={{0,1},{1,0},{2,3},{3,2},{4,5},{5,4},{6,7},{7,6},{8,9},{9,8},{10,11... | collective-permute-start | bytes 3538952 | tf_op jit(solution)/shard_map/ppermute | solution.py:557
  274.0 3.7 %collective-permute-start.7 = (bf16[4,56,1024]{2,1,0:T(8,128)(2,1)}, bf16[4,56,1024]{2,1,0:T(8,128)(2,1)S(1)}, u32[]{:S(2)}, u32[]{:S(2)}) collective-permute-start(bf16[4,56,1024]{2,1,0:T(8,128)(2,1)} %get-tuple-element.40.refs_4_), channel_id=1, source_target_pairs={{0,1},{1,0},{2,3},{3,2},{4,5},{5,4},{6,7},{7,6},{8,9},{9,8},{10,11... | collective-permute-start | bytes 1376264 | tf_op jit(solution)/shard_map/ppermute | solution.py:557
  274.5 39.1 %collective-permute-start.12 = (bf16[1,2,200,1024]{3,2,1,0:T(8,128)(2,1)}, bf16[1,2,200,1024]{3,2,1,0:T(8,128)(2,1)S(1)}, u32[]{:S(2)}, u32[]{:S(2)}) collective-permute-start(bf16[1,2,200,1024]{3,2,1,0:T(8,128)(2,1)} %get-tuple-element.44.refs_1_), channel_id=1, source_target_pairs={{0,2},{1,7},{2,4},{3,1},{4,6},{5,3},{6,0},{7,5},{8,10},{9,15},{10,... | collective-permute-start | bytes 2457608 | tf_op jit(solution)/shard_map/ppermute | solution.py:549
  274.7 39.0 %collective-permute-start = (bf16[2,64,3200]{2,1,0:T(8,128)(2,1)}, bf16[2,64,3200]{2,1,0:T(8,128)(2,1)S(1)}, u32[]{:S(2)}, u32[]{:S(2)}) collective-permute-start(bf16[2,64,3200]{2,1,0:T(8,128)(2,1)} %get-tuple-element.34.refs_1_), channel_id=1, source_target_pairs={{0,2},{1,3},{2,4},{3,5},{4,6},{5,7},{6,0},{7,1},{8,10},{9,11},{10,... | collective-permute-start | bytes 2457608 | tf_op jit(solution)/shard_map/ppermute | solution.py:549
  277.7 24.0 %copy-start.4 = (bf16[4,56,1024]{2,1,0:T(8,128)(2,1)}, bf16[4,56,1024]{2,1,0:T(8,128)(2,1)S(1)}, u32[]{:S(2)}) copy-start(bf16[4,56,1024]{2,1,0:T(8,128)(2,1)S(1)} %collective-permute-done.7.refs_5_) | copy-start | bytes 1376260
  277.7 41.6 %collective-permute-start.1 = (bf16[2,64,3200]{2,1,0:T(8,128)(2,1)}, bf16[2,64,3200]{2,1,0:T(8,128)(2,1)S(1)}, u32[]{:S(2)}, u32[]{:S(2)}) collective-permute-start(bf16[2,64,3200]{2,1,0:T(8,128)(2,1)} %get-tuple-element.35.refs_2_), channel_id=1, source_target_pairs={{0,6},{1,7},{2,0},{3,1},{4,2},{5,3},{6,4},{7,5},{8,14},{9,15},{10,... | collective-permute-start | bytes 2457608 | tf_op jit(solution)/shard_map/ppermute | solution.py:549
  301.7 60.5 %collective-permute-start.5 = (bf16[2,2,64,3200]{3,2,1,0:T(8,128)(2,1)S(1)}, bf16[2,2,64,3200]{3,2,1,0:T(8,128)(2,1)S(1)}, u32[]{:S(2)}, u32[]{:S(2)}) collective-permute-start(bf16[2,2,64,3200]{3,2,1,0:T(8,128)(2,1)S(1)} %collective-permute-done.4.refs_0_), channel_id=1, source_target_pairs={{0,1},{1,0},{2,3},{3,2},{4,5},{5,4},{6,7},{7,6},{8,9},{9,8},{10,11... | collective-permute-start | bytes 4915208 | tf_op jit(solution)/shard_map/ppermute | solution.py:550
  301.7 1.0 copy-start.1
  311.0 16.8 %collective-permute-start.8 = (bf16[1,2,144,1024]{3,2,1,0:T(8,128)(2,1)}, bf16[1,2,144,1024]{3,2,1,0:T(8,128)(2,1)}, u32[]{:S(2)}, u32[]{:S(2)}) collective-permute-start(bf16[1,2,144,1024]{3,2,1,0:T(8,128)(2,1)} %get-tuple-element.42), channel_id=1, source_target_pairs={{0,2},{1,7},{2,4},{3,1},{4,6},{5,3},{6,0},{7,5},{8,10},{9,15},{10,... | collective-permute-start | bytes 1769480 | tf_op jit(solution)/shard_map/ppermute | solution.py:549
  313.6 14.2 %collective-permute-start.10 = (bf16[1,2,56,1024]{3,2,1,0:T(8,128)(2,1)}, bf16[1,2,56,1024]{3,2,1,0:T(8,128)(2,1)}, u32[]{:S(2)}, u32[]{:S(2)}) collective-permute-start(bf16[1,2,56,1024]{3,2,1,0:T(8,128)(2,1)} %get-tuple-element.43), channel_id=1, source_target_pairs={{0,2},{1,7},{2,4},{3,1},{4,6},{5,3},{6,0},{7,5},{8,10},{9,15},{10,... | collective-permute-start | bytes 688136 | tf_op jit(solution)/shard_map/ppermute | solution.py:549
  313.7 14.7 %collective-permute-start.2 = (bf16[2,64,3200]{2,1,0:T(8,128)(2,1)S(1)}, bf16[2,64,3200]{2,1,0:T(8,128)(2,1)S(1)}, u32[]{:S(2)}, u32[]{:S(2)}) collective-permute-start(bf16[2,64,3200]{2,1,0:T(8,128)(2,1)S(1)} %collective-permute-done.refs_0_), channel_id=1, source_target_pairs={{0,1},{1,0},{2,3},{3,2},{4,5},{5,4},{6,7},{7,6},{8,9},{9,8},{10,11... | collective-permute-start | bytes 2457608 | tf_op jit(solution)/shard_map/ppermute | solution.py:550
  319.3 34.8 %collective-permute-start.3 = (bf16[2,64,3200]{2,1,0:T(8,128)(2,1)S(1)}, bf16[2,64,3200]{2,1,0:T(8,128)(2,1)S(1)}, u32[]{:S(2)}, u32[]{:S(2)}) collective-permute-start(bf16[2,64,3200]{2,1,0:T(8,128)(2,1)S(1)} %collective-permute-done.1.refs_1_), channel_id=1, source_target_pairs={{0,1},{1,0},{2,3},{3,2},{4,5},{5,4},{6,7},{7,6},{8,9},{9,8},{10,11... | collective-permute-start | bytes 2457608 | tf_op jit(solution)/shard_map/ppermute | solution.py:550
  327.8 28.1 %collective-permute-start.13 = (bf16[1,2,200,1024]{3,2,1,0:T(8,128)(2,1)S(1)}, bf16[1,2,200,1024]{3,2,1,0:T(8,128)(2,1)S(1)}, u32[]{:S(2)}, u32[]{:S(2)}) collective-permute-start(bf16[1,2,200,1024]{3,2,1,0:T(8,128)(2,1)S(1)} %collective-permute-done.12.refs_0_), channel_id=1, source_target_pairs={{0,1},{1,0},{2,3},{3,2},{4,5},{5,4},{6,7},{7,6},{8,9},{9,8},{10,11... | collective-permute-start | bytes 2457608 | tf_op jit(solution)/shard_map/ppermute | solution.py:550
  327.8 31.7 %collective-permute-start.9 = (bf16[1,2,144,1024]{3,2,1,0:T(8,128)(2,1)}, bf16[1,2,144,1024]{3,2,1,0:T(8,128)(2,1)}, u32[]{:S(2)}, u32[]{:S(2)}) collective-permute-start(bf16[1,2,144,1024]{3,2,1,0:T(8,128)(2,1)} %collective-permute-done.8.refs_0_), channel_id=1, source_target_pairs={{0,1},{1,0},{2,3},{3,2},{4,5},{5,4},{6,7},{7,6},{8,9},{9,8},{10,11... | collective-permute-start | bytes 1769480 | tf_op jit(solution)/shard_map/ppermute | solution.py:550
  328.3 31.2 %collective-permute-start.11 = (bf16[1,2,56,1024]{3,2,1,0:T(8,128)(2,1)}, bf16[1,2,56,1024]{3,2,1,0:T(8,128)(2,1)}, u32[]{:S(2)}, u32[]{:S(2)}) collective-permute-start(bf16[1,2,56,1024]{3,2,1,0:T(8,128)(2,1)} %collective-permute-done.10.refs_2_), channel_id=1, source_target_pairs={{0,1},{1,0},{2,3},{3,2},{4,5},{5,4},{6,7},{7,6},{8,9},{9,8},{10,11... | collective-permute-start | bytes 688136 | tf_op jit(solution)/shard_map/ppermute | solution.py:550
  354.1 1.9 copy-start
  354.1 2.8 copy-start.2
  354.1 2.9 copy-start.3
  354.1 3.0 copy-start.5

commit v7 on v6

--- a/solution.py
+++ b/solution.py
@@ -15,7 +15,7 @@
 OPPOSITE, RIGHT, LEFT, OWN = range(4)
 OFFSET = (2, 1, 3, 0)
 FIRST_ROWS = 16
-LAST_ROWS = 56
+LAST_ROWS = 40
 
 
 def adamw(w, m, v, g):
@@ -80,7 +80,7 @@
     ahead, behind = ahead_chip * 2 + core, behind_chip * 2 + core
 
     barrier = pltpu.get_barrier_semaphore()
-    for d in (right, left, other):
+    for d in (chip_at[RIGHT] * 2, chip_at[LEFT] * 2, other):
         pl.semaphore_signal(barrier, inc=1, device_id={"dp": d}, device_id_type=MESH)
 
     def remote(src, dst, send, recv, to):
@@ -123,7 +123,14 @@
     own_load(0).start()
     own_load(1).start()
     await_bytes(first_in, first_sem.at[0])
-    pl.semaphore_wait(barrier, 3)
+
+    @pl.when(core == 0)
+    def _():
+        pl.semaphore_wait(barrier, 5)
+
+    @pl.when(core == 1)
+    def _():
+        pl.semaphore_wait(barrier, 1)
 
     def swap(r, c):
         remote(
@@ -199,6 +206,11 @@
             @pl.when(core == 0)
             def _():
                 await_bytes(pass_in[first.kind].at[first.place], lead_send.at[0])
+
+        if c.number == 2:
+
+            @pl.when(core == 0)
+            def _():
                 pl.semaphore_signal(lead_sem, inc=1, device_id={"dp": other}, device_id_type=MESH)
 
     for c in chunks:
@@ -405,7 +417,7 @@
         out_specs=[hbm] * len(targets),
         scratch_shapes=[pltpu.VMEM((d, *shape), dtype) for d, (shape, dtype) in zip(depth, kinds)]
         + [pltpu.SemaphoreType.DMA((sum(depth),)), pltpu.SemaphoreType.DMA((sum(depth),))],
-        compiler_params=pltpu.CompilerParams(vmem_limit_bytes=56 * 2**20),
+        compiler_params=pltpu.CompilerParams(vmem_limit_bytes=48 * 2**20),
         cost_estimate=pl.CostEstimate(flops=2 * nbytes, bytes_accessed=nbytes, transcendentals=0),
     )(*sources)
 

time: 364 us -> 365 us (level)
  local copies, waits for them, and re-layouts: 2.19 us -> 6.33 us
    unnamed x12 -> x16, local copies, waits for them, and re-layouts: 2.19 us -> 6.33 us
where the time goes in v7:
time: 365 us
  Pallas kernels  313 us (86%)
  waiting for transfers between devices  37 us (10%)
  starting transfers between devices  8.19 us (2%)
  local copies, waits for them, and re-layouts  6.33 us (2%)
    pallas_call x1, Pallas kernels, gather_step(): pl.pallas_call(functools.partial(exchange, chunks, kinds, used, stages),...  272 us
    ppermute x6, waiting for transfers between devices, hop(): passed.setdefault(s, []).append(lax.ppermute(piece, 'dp', to))  35.2 us
    pallas_call x3, Pallas kernels, move(): pl.pallas_call(functools.partial(move_body, moves, kinds, depth, len(sour...  31.6 us
    pallas_call x4, Pallas kernels, put(): pl.pallas_call(functools.partial(put_body, moves, len(sources) + 1), out_...  9.41 us
  transfers between devices with their start and end apart: 14, of which 4 were waited for; matrix products, arithmetic and copies ran while one was open for 0% of the time, Pallas kernels for 11%

profile of v7, /device:TPU:113, one launch (start us, length us, event | category | flops | bytes accessed | tf_op | source)
XLA Modules:
  0.0 365.0 jit_solution(2231988566881571735)
XLA Ops:
  0.6 271.7 %shard_map.187 = (bf16[2,16,64,3200]{3,2,1,0:T(8,128)(2,1)}, bf16[2,16,64,3200]{3,2,1,0:T(8,128)(2,1)}, bf16[2,16,200,1024]{3,2,1,0:T(8,128)(2,1)}, f32[2,2,64,3...) custom-call(bf16[2,16,64,3200]{3,2,1,0:T(8,128)(2,1)} %bitcast.23, ...), custom_call_target="tpu_custom_call" | custom-call | tf_op jit(solution)/shard_map/pallas_call | solution.py:334
  272.3 1.1 collective-permute-start.4
  273.5 0.0 collective-permute-start.6
  273.5 0.5 collective-permute-start.7
  274.0 0.7 collective-permute-start.12
  274.7 0.7 collective-permute-start
  275.4 1.7 collective-permute-done.7.refs_5_
  277.2 0.7 collective-permute-start.1
  277.9 23.7 %collective-permute-done.4.refs_0_ = bf16[2,2,64,3200]{3,2,1,0:T(8,128)(2,1)S(1)} collective-permute-done((bf16[2,2,64,3200]{3,2,1,0:T(8,128)(2,1)}, bf16[2,2,64,3200]{3,2,1,0:T(8,128)(2,1)S(1)}, u32[]{:S(2)}, u32[]{:S(2)}) %collective-permute-start.4) | collective-permute-done | bytes 1638432 | tf_op jit(solution)/shard_map/ppermute | solution.py:561
  301.7 0.0 collective-permute-start.5
  301.7 0.0 collective-permute-done.6.refs_3_
  301.7 0.0 copy-start
  301.7 1.3 copy-done
  303.0 0.0 copy-start.3
  303.0 1.4 copy-done.3
  304.4 0.0 copy-start.4
  304.4 1.0 copy-done.4
  305.4 7.1 %shard_map.190 = (bf16[2,16,64,3200]{3,2,1,0:T(8,128)(2,1)}, bf16[1,2,160,1024]{3,2,1,0:T(8,128)(2,1)S(1)}, bf16[1,2,40,1024]{3,2,1,0:T(8,128)(2,1)S(1)}) custom-call(bf16[2,16,64,3200]{3,2,1,0:T(8,128)(2,1)} %get-tuple-element.38.refs_0_, bf16[2,2,64,3200]{3,2,1,0:T(8,128)(2,1)S(1)} %copy-done.3, bf16[4,160,1024]{2,1,0:T(8,128)(2,1)S(1)} %copy-done, ...), custom_call_target="tpu_custom_call" | custom-call | flops 42598400 | bytes 21299200 | tf_op jit(solution)/shard_map/pallas_call | solution.py:413
  312.5 2.1 collective-permute-start.8
  314.5 0.0 collective-permute-done.12.refs_0_
  314.5 0.1 collective-permute-start.10
  314.6 0.0 collective-permute-done.refs_0_
  314.6 1.6 collective-permute-start.2
  316.2 3.0 collective-permute-done.1.refs_1_
  319.2 0.0 collective-permute-start.3
  319.2 8.5 %collective-permute-done.10.refs_2_ = bf16[1,2,40,1024]{3,2,1,0:T(8,128)(2,1)S(1)} collective-permute-done((bf16[1,2,40,1024]{3,2,1,0:T(8,128)(2,1)S(1)}, bf16[1,2,40,1024]{3,2,1,0:T(8,128)(2,1)S(1)}, u32[]{:S(2)}, u32[]{:S(2)}) %collective-permute-start.10) | collective-permute-done | bytes 163872 | tf_op jit(solution)/shard_map/ppermute | solution.py:561
  327.7 0.0 collective-permute-start.13
  327.7 0.0 collective-permute-done.8.refs_0_
  327.7 0.5 collective-permute-start.9
  328.2 0.0 collective-permute-done.2.refs_2_
  328.2 0.1 collective-permute-start.11
  328.3 1.1 copy-done.6
  329.4 1.1 copy-done.7
  330.6 7.6 %shard_map.188.refs_4_ = bf16[2,16,64,3200]{3,2,1,0:T(8,128)(2,1)} custom-call(bf16[2,16,64,3200]{3,2,1,0:T(8,128)(2,1)} %get-tuple-element.36.refs_0_, bf16[2,64,3200]{2,1,0:T(8,128)(2,1)S(1)} %copy-done.6, bf16[2,64,3200]{2,1,0:T(8,128)(2,1)S(1)} %copy-done.7), custom_call_target="tpu_custom_call" | custom-call | flops 39321600 | bytes 19660800 | tf_op jit(solution)/shard_map/pallas_call | solution.py:413
  338.1 0.0 copy-done.2
  338.2 0.0 copy-done.5
  338.2 17.0 %shard_map.192 = (bf16[2,16,200,1024]{3,2,1,0:T(8,128)(2,1)}, f32[2,2,64,3200]{3,2,1,0:T(8,128)}, f32[2,2,64,3200]{3,2,1,0:T(8,128)}, f32[2,2,200,1024]{3,2,1,0:...) custom-call(bf16[2,16,200,1024]{3,2,1,0:T(8,128)(2,1)} %get-tuple-element.45.refs_0_, ...), custom_call_target="tpu_custom_call" | custom-call | flops 104857600 | bytes 52428800 | tf_op jit(solution)/shard_map/pallas_call | solution.py:413
  355.2 0.0 copy-start.1
  355.2 0.0 collective-permute-done.3.refs_3_
  355.2 1.8 shard_map.189
  357.0 0.0 collective-permute-done.13.refs_1_
  357.0 0.3 copy-done.1
  357.3 3.5 shard_map.193.refs_4_
  360.9 0.0 collective-permute-done.11.refs_3_
  360.9 0.0 collective-permute-done.9.refs_1_
  360.9 2.3 shard_map.194
  363.2 0.0 collective-permute-done.5.refs_1_
  363.2 1.8 shard_map.191
  (4 shorter events, 0.0 us)
Async XLA Ops:
  272.3 29.3 %collective-permute-start.4 = (bf16[2,2,64,3200]{3,2,1,0:T(8,128)(2,1)}, bf16[2,2,64,3200]{3,2,1,0:T(8,128)(2,1)S(1)}, u32[]{:S(2)}, u32[]{:S(2)}) collective-permute-start(bf16[2,2,64,3200]{3,2,1,0:T(8,128)(2,1)} %get-tuple-element.37.refs_1_), channel_id=1, source_target_pairs={{0,2},{1,7},{2,4},{3,1},{4,6},{5,3},{6,0},{7,5},{8,10},{9,15},{10,... | collective-permute-start | bytes 4915208 | tf_op jit(solution)/shard_map/ppermute | solution.py:561
  273.5 28.2 %collective-permute-start.6 = (bf16[4,160,1024]{2,1,0:T(8,128)(2,1)}, bf16[4,160,1024]{2,1,0:T(8,128)(2,1)S(1)}, u32[]{:S(2)}, u32[]{:S(2)}) collective-permute-start(bf16[4,160,1024]{2,1,0:T(8,128)(2,1)} %get-tuple-element.39.refs_2_), channel_id=1, source_target_pairs={{0,1},{1,0},{2,3},{3,2},{4,5},{5,4},{6,7},{7,6},{8,9},{9,8},{10,11... | collective-permute-start | bytes 3932168 | tf_op jit(solution)/shard_map/ppermute | solution.py:569
  273.5 3.7 %collective-permute-start.7 = (bf16[4,40,1024]{2,1,0:T(8,128)(2,1)}, bf16[4,40,1024]{2,1,0:T(8,128)(2,1)S(1)}, u32[]{:S(2)}, u32[]{:S(2)}) collective-permute-start(bf16[4,40,1024]{2,1,0:T(8,128)(2,1)} %get-tuple-element.40.refs_4_), channel_id=1, source_target_pairs={{0,1},{1,0},{2,3},{3,2},{4,5},{5,4},{6,7},{7,6},{8,9},{9,8},{10,11... | collective-permute-start | bytes 983048 | tf_op jit(solution)/shard_map/ppermute | solution.py:569
  274.0 40.5 %collective-permute-start.12 = (bf16[1,2,200,1024]{3,2,1,0:T(8,128)(2,1)}, bf16[1,2,200,1024]{3,2,1,0:T(8,128)(2,1)S(1)}, u32[]{:S(2)}, u32[]{:S(2)}) collective-permute-start(bf16[1,2,200,1024]{3,2,1,0:T(8,128)(2,1)} %get-tuple-element.44.refs_1_), channel_id=1, source_target_pairs={{0,2},{1,7},{2,4},{3,1},{4,6},{5,3},{6,0},{7,5},{8,10},{9,15},{10,... | collective-permute-start | bytes 2457608 | tf_op jit(solution)/shard_map/ppermute | solution.py:561
  274.7 39.9 %collective-permute-start = (bf16[2,64,3200]{2,1,0:T(8,128)(2,1)}, bf16[2,64,3200]{2,1,0:T(8,128)(2,1)S(1)}, u32[]{:S(2)}, u32[]{:S(2)}) collective-permute-start(bf16[2,64,3200]{2,1,0:T(8,128)(2,1)} %get-tuple-element.34.refs_1_), channel_id=1, source_target_pairs={{0,2},{1,3},{2,4},{3,5},{4,6},{5,7},{6,0},{7,1},{8,10},{9,11},{10,... | collective-permute-start | bytes 2457608 | tf_op jit(solution)/shard_map/ppermute | solution.py:561
  277.2 42.0 %collective-permute-start.1 = (bf16[2,64,3200]{2,1,0:T(8,128)(2,1)}, bf16[2,64,3200]{2,1,0:T(8,128)(2,1)S(1)}, u32[]{:S(2)}, u32[]{:S(2)}) collective-permute-start(bf16[2,64,3200]{2,1,0:T(8,128)(2,1)} %get-tuple-element.35.refs_2_), channel_id=1, source_target_pairs={{0,6},{1,7},{2,0},{3,1},{4,2},{5,3},{6,4},{7,5},{8,14},{9,15},{10,... | collective-permute-start | bytes 2457608 | tf_op jit(solution)/shard_map/ppermute | solution.py:561
  301.7 61.5 %collective-permute-start.5 = (bf16[2,2,64,3200]{3,2,1,0:T(8,128)(2,1)S(1)}, bf16[2,2,64,3200]{3,2,1,0:T(8,128)(2,1)S(1)}, u32[]{:S(2)}, u32[]{:S(2)}) collective-permute-start(bf16[2,2,64,3200]{3,2,1,0:T(8,128)(2,1)S(1)} %collective-permute-done.4.refs_0_), channel_id=1, source_target_pairs={{0,1},{1,0},{2,3},{3,2},{4,5},{5,4},{6,7},{7,6},{8,9},{9,8},{10,11... | collective-permute-start | bytes 4915208 | tf_op jit(solution)/shard_map/ppermute | solution.py:562
  301.7 1.3 copy-start
  303.0 1.4 copy-start.3
  304.4 1.0 copy-start.4
  312.5 15.2 %collective-permute-start.8 = (bf16[1,2,160,1024]{3,2,1,0:T(8,128)(2,1)S(1)}, bf16[1,2,160,1024]{3,2,1,0:T(8,128)(2,1)S(1)}, u32[]{:S(2)}, u32[]{:S(2)}) collective-permute-start(bf16[1,2,160,1024]{3,2,1,0:T(8,128)(2,1)S(1)} %get-tuple-element.42), channel_id=1, source_target_pairs={{0,2},{1,7},{2,4},{3,1},{4,6},{5,3},{6,0},{7,5},{8,10},{9,15},{10,... | collective-permute-start | bytes 1966088 | tf_op jit(solution)/shard_map/ppermute | solution.py:561
  314.5 13.2 %collective-permute-start.10 = (bf16[1,2,40,1024]{3,2,1,0:T(8,128)(2,1)S(1)}, bf16[1,2,40,1024]{3,2,1,0:T(8,128)(2,1)S(1)}, u32[]{:S(2)}, u32[]{:S(2)}) collective-permute-start(bf16[1,2,40,1024]{3,2,1,0:T(8,128)(2,1)S(1)} %get-tuple-element.43), channel_id=1, source_target_pairs={{0,2},{1,7},{2,4},{3,1},{4,6},{5,3},{6,0},{7,5},{8,10},{9,15},{10,... | collective-permute-start | bytes 491528 | tf_op jit(solution)/shard_map/ppermute | solution.py:561
  314.6 13.6 %collective-permute-start.2 = (bf16[2,64,3200]{2,1,0:T(8,128)(2,1)S(1)}, bf16[2,64,3200]{2,1,0:T(8,128)(2,1)S(1)}, u32[]{:S(2)}, u32[]{:S(2)}) collective-permute-start(bf16[2,64,3200]{2,1,0:T(8,128)(2,1)S(1)} %collective-permute-done.refs_0_), channel_id=1, source_target_pairs={{0,1},{1,0},{2,3},{3,2},{4,5},{5,4},{6,7},{7,6},{8,9},{9,8},{10,11... | collective-permute-start | bytes 2457608 | tf_op jit(solution)/shard_map/ppermute | solution.py:562
  319.2 36.0 %collective-permute-start.3 = (bf16[2,64,3200]{2,1,0:T(8,128)(2,1)S(1)}, bf16[2,64,3200]{2,1,0:T(8,128)(2,1)S(1)}, u32[]{:S(2)}, u32[]{:S(2)}) collective-permute-start(bf16[2,64,3200]{2,1,0:T(8,128)(2,1)S(1)} %collective-permute-done.1.refs_1_), channel_id=1, source_target_pairs={{0,1},{1,0},{2,3},{3,2},{4,5},{5,4},{6,7},{7,6},{8,9},{9,8},{10,11... | collective-permute-start | bytes 2457608 | tf_op jit(solution)/shard_map/ppermute | solution.py:562
  327.7 29.3 %collective-permute-start.13 = (bf16[1,2,200,1024]{3,2,1,0:T(8,128)(2,1)S(1)}, bf16[1,2,200,1024]{3,2,1,0:T(8,128)(2,1)}, u32[]{:S(2)}, u32[]{:S(2)}) collective-permute-start(bf16[1,2,200,1024]{3,2,1,0:T(8,128)(2,1)S(1)} %collective-permute-done.12.refs_0_), channel_id=1, source_target_pairs={{0,1},{1,0},{2,3},{3,2},{4,5},{5,4},{6,7},{7,6},{8,9},{9,8},{10,11... | collective-permute-start | bytes 2457608 | tf_op jit(solution)/shard_map/ppermute | solution.py:562
  327.7 33.2 %collective-permute-start.9 = (bf16[1,2,160,1024]{3,2,1,0:T(8,128)(2,1)S(1)}, bf16[1,2,160,1024]{3,2,1,0:T(8,128)(2,1)}, u32[]{:S(2)}, u32[]{:S(2)}) collective-permute-start(bf16[1,2,160,1024]{3,2,1,0:T(8,128)(2,1)S(1)} %collective-permute-done.8.refs_0_), channel_id=1, source_target_pairs={{0,1},{1,0},{2,3},{3,2},{4,5},{5,4},{6,7},{7,6},{8,9},{9,8},{10,11... | collective-permute-start | bytes 1966088 | tf_op jit(solution)/shard_map/ppermute | solution.py:562
  328.2 32.6 %collective-permute-start.11 = (bf16[1,2,40,1024]{3,2,1,0:T(8,128)(2,1)S(1)}, bf16[1,2,40,1024]{3,2,1,0:T(8,128)(2,1)S(1)}, u32[]{:S(2)}, u32[]{:S(2)}) collective-permute-start(bf16[1,2,40,1024]{3,2,1,0:T(8,128)(2,1)S(1)} %collective-permute-done.10.refs_2_), channel_id=1, source_target_pairs={{0,1},{1,0},{2,3},{3,2},{4,5},{5,4},{6,7},{7,6},{8,9},{9,8},{10,11... | collective-permute-start | bytes 491528 | tf_op jit(solution)/shard_map/ppermute | solution.py:562
  328.3 1.1 copy-start.6
  329.4 1.1 copy-start.7
  330.6 7.6 %copy-start.2 = (f32[2,2,64,3200]{3,2,1,0:T(8,128)S(1)}, f32[2,2,64,3200]{3,2,1,0:T(8,128)}, u32[]{:S(2)}) copy-start(f32[2,2,64,3200]{3,2,1,0:T(8,128)} %get-tuple-element.46.refs_2_) | copy-start | bytes 9830404
  330.6 7.6 %copy-start.5 = (bf16[1,2,200,1024]{3,2,1,0:T(8,128)(2,1)S(1)}, bf16[1,2,200,1024]{3,2,1,0:T(8,128)(2,1)}, u32[]{:S(2)}) copy-start(bf16[1,2,200,1024]{3,2,1,0:T(8,128)(2,1)} %get-tuple-element.44.refs_1_) | copy-start | bytes 2457604
  355.2 2.1 copy-start.1
